TPU v7x, 32 devices: a whole 2x2x4 slice. The times are simulated.
32 devices in a mesh: narrow: 4 (over z), wide: 8 (over y, x, core).
Axes of the slice: x: 2, y: 2, z: 4, core: 2. Of those that a mesh axis runs over, the one named last changes fastest.
Arguments:
- hidden_in: bfloat16 [8, 2048, 2048], P('narrow', 'wide'), may hold values from -6 to 6
- out_grad: bfloat16 [8, 2048, 2048], P('narrow', 'wide'), may hold values from -6 to 6
- doc_lengths: int32 [8, 8], P('narrow'), may hold values from 1 to 1024, 2048 in all within a row
- attn_gain: bfloat16 [2048], P('narrow'), may hold values from 0.5 to 1.5
- w_query: bfloat16 [2048, 2048], P('narrow', 'wide'), may hold values from -0.125 to 0.125
- w_key: bfloat16 [2048, 2048], P('narrow', 'wide'), may hold values from -0.125 to 0.125
- w_value: bfloat16 [2048, 2048], P('narrow', 'wide'), may hold values from -0.125 to 0.125
- w_out: bfloat16 [2048, 2048], P('wide', 'narrow'), may hold values from -1 to 1
- mlp_gain: bfloat16 [2048], P('narrow'), may hold values from 0.5 to 1.5
- w_gate: bfloat16 [2048, 8192], P('narrow', 'wide'), may hold values from -0.125 to 0.125
- w_up: bfloat16 [2048, 8192], P('narrow', 'wide'), may hold values from -0.125 to 0.125
- w_down: bfloat16 [8192, 2048], P('wide', 'narrow'), may hold values from -0.0625 to 0.0625
Outputs:
- hidden_out: bfloat16 [8, 2048, 2048], P('narrow', 'wide')
- in_grad: bfloat16 [8, 2048, 2048], P('narrow', 'wide')
- grad_attn_gain: float32 [2048], P(('narrow', 'wide'))
- grad_w_query: float32 [2048, 2048], P('narrow', 'wide')
- grad_w_key: float32 [2048, 2048], P('narrow', 'wide')
- grad_w_value: float32 [2048, 2048], P('narrow', 'wide')
- grad_w_out: float32 [2048, 2048], P('wide', 'narrow')
- grad_mlp_gain: float32 [2048], P(('narrow', 'wide'))
- grad_w_gate: float32 [2048, 8192], P('narrow', 'wide')
- grad_w_up: float32 [2048, 8192], P('narrow', 'wide')
- grad_w_down: float32 [8192, 2048], P('wide', 'narrow')
Inputs may be any that keep to these rules, and one draw needn't show every extreme that they name: `doc_lengths`: in every row the 8 lengths sum to 2048, and the longest is exactly 1024.
All inputs are finite; a program needn't handle non-finite values.
Results may differ from a plain program's by a relative error of at most 0.029.
Values may be sent and summed in bfloat16 or wider, within the bound.
No kernel may reach another device: no remote copies, remote signals or barrier semaphores. Data moves between devices by JAX's collectives and lax.ppermute only.
A program may use at most 192 MiB of HBM per device.

v0:
```python
import jax
import jax.numpy as jnp
from jax import lax
from jax.sharding import PartitionSpec as P

HEAD_DIM = 64


EPS = 1e-05
NEG = -1e30
ROPE_BASE = 130000.0


def mat_plain(left_op, right_op):
    return jnp.dot(left_op, right_op, preferred_element_type=jnp.float32)


def mat_back(left_op, right_op):
    return lax.dot_general(
        left_op, right_op, (((1,), (1,)), ((), ())), preferred_element_type=jnp.float32
    )


def mat_outer(left_op, right_op):
    return lax.dot_general(
        left_op, right_op, (((0,), (0,)), ((), ())), preferred_element_type=jnp.float32
    )


def rounded(values_in):
    return values_in.astype(jnp.bfloat16).astype(jnp.float32)


def doc_starts(lengths, seq_len):
    tokens = jnp.arange(seq_len, dtype=jnp.int32)
    ends_at = jnp.cumsum(lengths)
    before = jnp.where(ends_at[None, :] <= tokens[:, None], ends_at[None, :], jnp.int32(0))
    return jnp.max(before, axis=1)


def rope_tables(starts, seq_len):
    half_dim = HEAD_DIM // 2
    position = (jnp.arange(seq_len, dtype=jnp.int32) - starts).astype(jnp.float32)
    inverse = ROPE_BASE ** (-(jnp.arange(half_dim, dtype=jnp.float32) * 2.0) / HEAD_DIM)
    angles = position[:, None] * inverse[None, :]
    return (jnp.cos(angles)[:, None, :], jnp.sin(angles)[:, None, :])


def rotate(tensor, cos_table, sin_table):
    half_dim = tensor.shape[-1] // 2
    front_half = tensor[..., :half_dim]
    back_half = tensor[..., half_dim:]
    return jnp.concatenate(
        [
            front_half * cos_table - back_half * sin_table,
            back_half * cos_table + front_half * sin_table,
        ],
        axis=-1,
    )


def allowed_keys(starts, first_row, block_len, seq_len):
    row_ids = first_row + jnp.arange(block_len, dtype=jnp.int32)
    columns = jnp.arange(seq_len, dtype=jnp.int32)
    begins = lax.dynamic_slice_in_dim(starts, first_row, block_len)
    return (columns[None, :] <= row_ids[:, None]) & (columns[None, :] >= begins[:, None])


def attend_forward(queries, keys_rot, values_in, starts, block_len):
    seq_len, heads_here, head_size = queries.shape
    n_blocks = seq_len // block_len
    score_scale = head_size ** (-0.5)
    blocks = queries.reshape(n_blocks, block_len, heads_here, head_size)
    firsts = jnp.arange(n_blocks, dtype=jnp.int32) * block_len

    def one_block(block_pair):
        q_block, first_row = block_pair
        allowed = allowed_keys(starts, first_row, block_len, seq_len)
        scores = (
            jnp.einsum("qhd,khd->hqk", q_block, keys_rot, preferred_element_type=jnp.float32)
            * score_scale
        )
        masked = jnp.where(allowed[None], scores, NEG)
        row_max = jnp.max(masked, axis=-1, keepdims=True)
        exp_terms = jnp.exp(masked - row_max)
        row_total = jnp.sum(exp_terms, axis=-1, keepdims=True)
        prob_rows = (exp_terms / row_total).astype(jnp.bfloat16)
        block_out = jnp.einsum(
            "hqk,khd->qhd", prob_rows, values_in, preferred_element_type=jnp.float32
        )
        return (block_out, (row_max + jnp.log(row_total))[..., 0])

    block_outs, log_totals = lax.map(one_block, (blocks, firsts))
    return (block_outs.reshape(seq_len, heads_here * head_size), log_totals)


def attend_backward(queries, keys_rot, values_in, grad_att, log_totals, starts, block_len):
    seq_len, heads_here, head_size = queries.shape
    n_blocks = seq_len // block_len
    score_scale = head_size ** (-0.5)
    q_blocks = queries.reshape(n_blocks, block_len, heads_here, head_size)
    g_blocks = grad_att.reshape(n_blocks, block_len, heads_here, head_size)
    firsts = jnp.arange(n_blocks, dtype=jnp.int32) * block_len

    def one_block(carried, block_pack):
        key_acc, value_acc = carried
        q_block, g_block, lse_block, first_row = block_pack
        allowed = allowed_keys(starts, first_row, block_len, seq_len)
        scores = (
            jnp.einsum("qhd,khd->hqk", q_block, keys_rot, preferred_element_type=jnp.float32)
            * score_scale
        )
        masked = jnp.where(allowed[None], scores, NEG)
        probs_full = jnp.exp(masked - lse_block[..., None])
        prob_rows = probs_full.astype(jnp.bfloat16)
        value_acc = value_acc + jnp.einsum(
            "hqk,qhd->khd", prob_rows, g_block, preferred_element_type=jnp.float32
        )
        grad_probs = jnp.einsum(
            "qhd,khd->hqk", g_block, values_in, preferred_element_type=jnp.float32
        )
        row_inner = jnp.sum(probs_full * grad_probs, axis=-1, keepdims=True)
        grad_scores = (probs_full * (grad_probs - row_inner)).astype(jnp.bfloat16)
        query_grad = (
            jnp.einsum("hqk,khd->qhd", grad_scores, keys_rot, preferred_element_type=jnp.float32)
            * score_scale
        )
        key_acc = (
            key_acc
            + jnp.einsum("hqk,qhd->khd", grad_scores, q_block, preferred_element_type=jnp.float32)
            * score_scale
        )
        return ((key_acc, value_acc), query_grad)

    zero_field = jnp.zeros((seq_len, heads_here, head_size), jnp.float32)
    (key_grad, value_grad), query_grads = lax.scan(
        one_block, (zero_field, zero_field), (q_blocks, g_blocks, log_totals, firsts)
    )
    return (query_grads.reshape(seq_len, heads_here, head_size), key_grad, value_grad)


def one_row(input_row, grad_row, lengths, weights):
    inner_set, outer_set = weights
    w_query, w_key, w_value, w_gate, w_up, gain_attn, gain_mlp = inner_set
    w_out, w_down = outer_set
    attn_scale = gain_attn.astype(jnp.float32)
    mlp_scale = gain_mlp.astype(jnp.float32)
    local_rows = input_row.shape[0]
    seq_len = local_rows * lax.axis_size("wide")
    heads_here = w_query.shape[1] // HEAD_DIM
    block_len = min(512, seq_len)
    field_shape = (seq_len, heads_here, HEAD_DIM)
    flat_shape = (seq_len, heads_here * HEAD_DIM)
    starts = doc_starts(lengths, seq_len)
    cos_table, sin_table = rope_tables(starts, seq_len)
    residual = input_row.astype(jnp.float32)
    inv_first = lax.rsqrt(jnp.mean(residual * residual, axis=-1, keepdims=True) + EPS)
    normed = residual * inv_first
    attn_in = lax.all_gather((normed * attn_scale).astype(jnp.bfloat16), "wide", axis=0, tiled=True)
    queries = rotate(mat_plain(attn_in, w_query).reshape(field_shape), cos_table, sin_table).astype(
        jnp.bfloat16
    )
    keys_rot = rotate(mat_plain(attn_in, w_key).reshape(field_shape), cos_table, sin_table).astype(
        jnp.bfloat16
    )
    values_in = mat_plain(attn_in, w_value).astype(jnp.bfloat16).reshape(field_shape)
    attended, log_totals = attend_forward(queries, keys_rot, values_in, starts, block_len)
    attended = attended.astype(jnp.bfloat16)
    middle = residual + lax.psum_scatter(
        rounded(mat_plain(attended, w_out)).astype(jnp.bfloat16),
        "wide",
        scatter_dimension=0,
        tiled=True,
    ).astype(jnp.float32)
    inv_second = lax.rsqrt(jnp.mean(middle * middle, axis=-1, keepdims=True) + EPS)
    normed_mid = middle * inv_second
    mlp_in = lax.all_gather(
        (normed_mid * mlp_scale).astype(jnp.bfloat16), "wide", axis=0, tiled=True
    )
    gate_pre = mat_plain(mlp_in, w_gate)
    up_pre = mat_plain(mlp_in, w_up)
    sigmoid_gate = jax.nn.sigmoid(gate_pre)
    silu_gate = gate_pre * sigmoid_gate
    hidden = (silu_gate * up_pre).astype(jnp.bfloat16)
    output = middle + lax.psum_scatter(
        rounded(mat_plain(hidden, w_down)).astype(jnp.bfloat16),
        "wide",
        scatter_dimension=0,
        tiled=True,
    ).astype(jnp.float32)
    grad_full = lax.all_gather(grad_row, "wide", axis=0, tiled=True)
    grad_down = mat_outer(hidden, grad_full)
    grad_hidden = mat_back(grad_full, w_down)
    grad_gate_pre = (
        grad_hidden * up_pre * sigmoid_gate * (1.0 + gate_pre * (1.0 - sigmoid_gate))
    ).astype(jnp.bfloat16)
    grad_up_pre = (grad_hidden * silu_gate).astype(jnp.bfloat16)
    grad_gate = mat_outer(mlp_in, grad_gate_pre)
    grad_up = mat_outer(mlp_in, grad_up_pre)
    grad_mlp_in = lax.psum_scatter(
        rounded(mat_back(grad_gate_pre, w_gate) + mat_back(grad_up_pre, w_up)).astype(jnp.bfloat16),
        "wide",
        scatter_dimension=0,
        tiled=True,
    ).astype(jnp.float32)
    scaled_mid = grad_mlp_in * mlp_scale
    gain_mlp_grad = jnp.sum(grad_mlp_in * normed_mid, axis=0)
    grad_middle = grad_row.astype(jnp.float32) + inv_second * (
        scaled_mid - normed_mid * jnp.mean(scaled_mid * normed_mid, axis=-1, keepdims=True)
    )
    grad_branch = lax.all_gather(grad_middle.astype(jnp.bfloat16), "wide", axis=0, tiled=True)
    grad_out = mat_outer(attended, grad_branch)
    grad_att = mat_back(grad_branch, w_out).astype(jnp.bfloat16).reshape(field_shape)
    query_grad, key_grad, value_grad = attend_backward(
        queries, keys_rot, values_in, grad_att, log_totals, starts, block_len
    )
    query_raw = rotate(query_grad, cos_table, -sin_table).reshape(flat_shape).astype(jnp.bfloat16)
    key_raw = rotate(key_grad, cos_table, -sin_table).reshape(flat_shape).astype(jnp.bfloat16)
    value_raw = value_grad.reshape(flat_shape).astype(jnp.bfloat16)
    grad_query = mat_outer(attn_in, query_raw)
    grad_key = mat_outer(attn_in, key_raw)
    grad_value = mat_outer(attn_in, value_raw)
    grad_attn_in = lax.psum_scatter(
        rounded(
            mat_back(query_raw, w_query) + mat_back(key_raw, w_key) + mat_back(value_raw, w_value)
        ).astype(jnp.bfloat16),
        "wide",
        scatter_dimension=0,
        tiled=True,
    ).astype(jnp.float32)
    scaled_in = grad_attn_in * attn_scale
    gain_attn_grad = jnp.sum(grad_attn_in * normed, axis=0)
    grad_input = grad_middle + inv_first * (
        scaled_in - normed * jnp.mean(scaled_in * normed, axis=-1, keepdims=True)
    )
    return (
        output.astype(jnp.bfloat16),
        grad_input.astype(jnp.bfloat16),
        (grad_query, grad_key, grad_value, grad_gate, grad_up),
        (grad_out, grad_down),
        (gain_attn_grad, gain_mlp_grad),
    )


def per_device(
    hidden_in,
    out_grad,
    doc_lengths,
    attn_gain,
    w_query,
    w_key,
    w_value,
    w_out,
    mlp_gain,
    w_gate,
    w_up,
    w_down,
):
    narrow_count = lax.axis_size("narrow")

    def fetch_weights():
        inner_set = (
            lax.all_gather(w_query, "narrow", axis=0, tiled=True),
            lax.all_gather(w_key, "narrow", axis=0, tiled=True),
            lax.all_gather(w_value, "narrow", axis=0, tiled=True),
            lax.all_gather(w_gate, "narrow", axis=0, tiled=True),
            lax.all_gather(w_up, "narrow", axis=0, tiled=True),
            lax.all_gather(attn_gain, "narrow", axis=0, tiled=True),
            lax.all_gather(mlp_gain, "narrow", axis=0, tiled=True),
        )
        outer_set = (
            lax.all_gather(w_out, "narrow", axis=1, tiled=True),
            lax.all_gather(w_down, "narrow", axis=1, tiled=True),
        )
        return (inner_set, outer_set)

    def share_grads(grads_in, grads_out):
        summed_in = (
            lax.psum_scatter(
                grads_in[0].astype(jnp.bfloat16), "narrow", scatter_dimension=0, tiled=True
            ).astype(jnp.float32),
            lax.psum_scatter(
                grads_in[1].astype(jnp.bfloat16), "narrow", scatter_dimension=0, tiled=True
            ).astype(jnp.float32),
            lax.psum_scatter(
                grads_in[2].astype(jnp.bfloat16), "narrow", scatter_dimension=0, tiled=True
            ).astype(jnp.float32),
            lax.psum_scatter(
                grads_in[3].astype(jnp.bfloat16), "narrow", scatter_dimension=0, tiled=True
            ).astype(jnp.float32),
            lax.psum_scatter(
                grads_in[4].astype(jnp.bfloat16), "narrow", scatter_dimension=0, tiled=True
            ).astype(jnp.float32),
        )
        summed_out = (
            lax.psum_scatter(
                grads_out[0].astype(jnp.bfloat16), "narrow", scatter_dimension=1, tiled=True
            ).astype(jnp.float32),
            lax.psum_scatter(
                grads_out[1].astype(jnp.bfloat16), "narrow", scatter_dimension=1, tiled=True
            ).astype(jnp.float32),
        )
        return (summed_in, summed_out)

    acc_in = tuple(
        (jnp.zeros(weight.shape, jnp.float32) for weight in (w_query, w_key, w_value, w_gate, w_up))
    )
    acc_out = tuple((jnp.zeros(weight.shape, jnp.float32) for weight in (w_out, w_down)))
    gain_acc = (
        jnp.zeros((attn_gain.shape[0] * narrow_count,), jnp.float32),
        jnp.zeros((mlp_gain.shape[0] * narrow_count,), jnp.float32),
    )

    def micro_step(carried, inputs):
        sum_in, sum_out, sum_gain = carried
        input_row, grad_row, lengths = inputs
        weights = fetch_weights()
        output, grad_input, grads_in, grads_out, grads_gain = one_row(
            input_row, grad_row, lengths, weights
        )
        grads_in, grads_out = share_grads(grads_in, grads_out)
        sum_in = tuple((acc_item + new_item for acc_item, new_item in zip(sum_in, grads_in)))
        sum_out = tuple((acc_item + new_item for acc_item, new_item in zip(sum_out, grads_out)))
        sum_gain = tuple((acc_item + new_item for acc_item, new_item in zip(sum_gain, grads_gain)))
        return ((sum_in, sum_out, sum_gain), (output, grad_input))

    carried, (outputs, in_grads) = lax.scan(
        micro_step, (acc_in, acc_out, gain_acc), (hidden_in, out_grad, doc_lengths)
    )
    sum_in, sum_out, sum_gain = carried
    gain_grads = (
        lax.psum_scatter(sum_gain[0], ("narrow", "wide"), scatter_dimension=0, tiled=True),
        lax.psum_scatter(sum_gain[1], ("narrow", "wide"), scatter_dimension=0, tiled=True),
    )
    return (
        outputs,
        in_grads,
        gain_grads[0],
        sum_in[0],
        sum_in[1],
        sum_in[2],
        sum_out[0],
        gain_grads[1],
        sum_in[3],
        sum_in[4],
        sum_out[1],
    )


def solution(mesh):
    in_specs = (
        P("narrow", "wide", None),
        P("narrow", "wide", None),
        P("narrow", None),
        P("narrow"),
        P("narrow", "wide"),
        P("narrow", "wide"),
        P("narrow", "wide"),
        P("wide", "narrow"),
        P("narrow"),
        P("narrow", "wide"),
        P("narrow", "wide"),
        P("wide", "narrow"),
    )
    out_specs = (
        P("narrow", "wide", None),
        P("narrow", "wide", None),
        P(("narrow", "wide")),
        P("narrow", "wide"),
        P("narrow", "wide"),
        P("narrow", "wide"),
        P("wide", "narrow"),
        P(("narrow", "wide")),
        P("narrow", "wide"),
        P("narrow", "wide"),
        P("wide", "narrow"),
    )
    return jax.shard_map(
        per_device, mesh=mesh, in_specs=in_specs, out_specs=out_specs, check_vma=False
    )
```

profile of v0, /device:TPU:0, one launch (start us, length us, event | category | flops | bytes accessed | tf_op | source)
XLA Modules:
  0.0 2786.1 jit_solution(1502561951740328314)
XLA Ops:
  7.3 2731.1 %while.62 = (s32[]{:T(128)}, f32[512,256]{1,0:T(8,128)}, f32[512,256]{1,0:T(8,128)}, f32[512,256]{1,0:T(8,128)}, f32[512,1024]{1,0:T(8,128)}, /*index=5*/f32[512...) while((s32[]{:T(128)}, f32[512,256]{1,0:T(8,128)}, ...), condition=%wide.region_27.28_spmd.clone, body=%wide.region_0.27_spmd.clone.sunk | while | flops 107088232448 | bytes 1211792128 | solution.py:327
  40.8 55.8 %all-gather.24.cloned.1.call-done = bf16[2048,2048]{1,0:T(8,128)(2,1)} async-done(((bf16[256,2048]{1,0:T(8,128)(2,1)}), bf16[2048,2048]{1,0:T(8,128)(2,1)}) %all-gather.24.cloned.1.call-update) | async-done | bytes 8388624 | tf_op jit(solution)/shard_map/while/body/eval_jaxpr/all_gather | solution.py:159
  161.1 74.7 %while.63 = (s32[]{:T(128)}, bf16[4,512,4,64]{1,3,2,0:T(8,128)(2,1)}, f32[4,4,512]{2,1,0:T(4,128)}, s32[4]{0:T(128)S(1)}, s32[2048]{0:T(1024)}, /*index=5*/bf16[...) while((s32[]{:T(128)}, ...), condition=%wide.region_7.7_spmd, body=%wide.region_4.6_spmd.sunk | while | flops 1127217664 | bytes 65874156 | solution.py:93
  263.1 54.9 %reduce-scatter.12.cloned.1.call-done = bf16[256,2048]{1,0:T(8,128)(2,1)} async-done(((bf16[2048,2048]{1,0:T(8,128)(2,1)}), bf16[256,2048]{1,0:T(8,128)(2,1)}) %reduce-scatter.12.cloned.1.call-update) | async-done | bytes 1048592 | tf_op jit(solution)/shard_map/while/body/eval_jaxpr/reduce_scatter | solution.py:169
  323.1 77.4 %all-gather.38.cloned.1.call-done = bf16[1024,2048]{1,0:T(8,128)(2,1)} async-done(((bf16[1024,512]{1,0:T(8,128)(2,1)}), bf16[1024,2048]{1,0:T(8,128)(2,1)}) %all-gather.38.cloned.1.call-update) | async-done | bytes 4194320 | tf_op jit(solution)/shard_map/while/body/eval_jaxpr/all_gather | solution.py:273
  400.4 55.0 %all-gather.40.cloned.1.call-done = bf16[1,2048,2048]{2,1,0:T(8,128)(2,1)} async-done(((bf16[1,256,2048]{2,1,0:T(8,128)(2,1)}), bf16[1,2048,2048]{2,1,0:T(8,128)(2,1)}) %all-gather.40.cloned.1.call-update) | async-done | bytes 8388624 | tf_op jit(solution)/shard_map/while/body/eval_jaxpr/all_gather | solution.py:191
  470.1 67.7 %all-gather.36.cloned.1.call-done = bf16[2048,1024]{1,0:T(8,128)(2,1)} async-done(((bf16[512,1024]{1,0:T(8,128)(2,1)}), bf16[2048,1024]{1,0:T(8,128)(2,1)}) %all-gather.36.cloned.1.call-update) | async-done | bytes 4194320 | tf_op jit(solution)/shard_map/while/body/eval_jaxpr/all_gather | solution.py:266
  537.9 54.8 %all-gather.34.cloned.1.call-done = bf16[2048,2048]{1,0:T(8,128)(2,1)} async-done(((bf16[256,2048]{1,0:T(8,128)(2,1)}), bf16[2048,2048]{1,0:T(8,128)(2,1)}) %all-gather.34.cloned.1.call-update) | async-done | bytes 8388624 | tf_op jit(solution)/shard_map/while/body/eval_jaxpr/all_gather | solution.py:177
  607.1 68.1 %all-gather.42.cloned.1.call-done = bf16[2048,1024]{1,0:T(8,128)(2,1)} async-done(((bf16[512,1024]{1,0:T(8,128)(2,1)}), bf16[2048,1024]{1,0:T(8,128)(2,1)}) %all-gather.42.cloned.1.call-update) | async-done | bytes 4194320 | tf_op jit(solution)/shard_map/while/body/eval_jaxpr/all_gather | solution.py:267
  727.9 69.9 %reduce-scatter.14.cloned.1.call-done = bf16[256,2048]{1,0:T(8,128)(2,1)} async-done(((bf16[2048,2048]{1,0:T(8,128)(2,1)}), bf16[256,2048]{1,0:T(8,128)(2,1)}) %reduce-scatter.14.cloned.1.call-update) | async-done | bytes 1048592 | tf_op jit(solution)/shard_map/while/body/eval_jaxpr/reduce_scatter | solution.py:200
  875.4 249.1 %while.64 = (s32[]{:T(128)}, f32[2048,4,64]{0,2,1:T(8,128)}, f32[2048,4,64]{0,2,1:T(8,128)}, f32[4,512,4,64]{1,0,3,2:T(4,128)}, bf16[4,512,4,64]{1,3,2,0:T(8,128...) while((s32[]{:T(128)}, f32[2048,4,64]{0,2,1:T(8,128)}, ...), condition=%wide.region_14.14_spmd.clone, body=%wide.region_12.13_spmd.clone.sunk | while | flops 2753165824 | bytes 183044368 | solution.py:136
  1221.5 72.0 %reduce-scatter.30.cloned.1.call-done = bf16[256,2048]{1,0:T(8,128)(2,1)} async-done(((bf16[2048,2048]{1,0:T(8,128)(2,1)}), bf16[256,2048]{1,0:T(8,128)(2,1)}) %reduce-scatter.30.cloned.1.call-update) | async-done | bytes 1048592 | tf_op jit(solution)/shard_map/while/body/eval_jaxpr/reduce_scatter | solution.py:223
  1295.6 72.7 %reduce-scatter.32.cloned.1.call-done = bf16[256,2048]{1,0:T(8,128)(2,1)} async-done(((bf16[2048,2048]{1,0:T(8,128)(2,1)}), bf16[256,2048]{1,0:T(8,128)(2,1)}) %reduce-scatter.32.cloned.1.call-update) | async-done | bytes 1048592 | tf_op jit(solution)/shard_map/while/body/eval_jaxpr/reduce_scatter | solution.py:185
  1404.3 55.7 %all-gather.24.cloned.1.call-done = bf16[2048,2048]{1,0:T(8,128)(2,1)} async-done(((bf16[256,2048]{1,0:T(8,128)(2,1)}), bf16[2048,2048]{1,0:T(8,128)(2,1)}) %all-gather.24.cloned.1.call-update) | async-done | bytes 8388624 | tf_op jit(solution)/shard_map/while/body/eval_jaxpr/all_gather | solution.py:159
  1524.4 74.7 %while.63 = (s32[]{:T(128)}, bf16[4,512,4,64]{1,3,2,0:T(8,128)(2,1)}, f32[4,4,512]{2,1,0:T(4,128)}, s32[4]{0:T(128)S(1)}, s32[2048]{0:T(1024)}, /*index=5*/bf16[...) while((s32[]{:T(128)}, ...), condition=%wide.region_7.7_spmd, body=%wide.region_4.6_spmd.sunk | while | flops 1127217664 | bytes 65874156 | solution.py:93
  1686.2 77.5 %all-gather.38.cloned.1.call-done = bf16[1024,2048]{1,0:T(8,128)(2,1)} async-done(((bf16[1024,512]{1,0:T(8,128)(2,1)}), bf16[1024,2048]{1,0:T(8,128)(2,1)}) %all-gather.38.cloned.1.call-update) | async-done | bytes 4194320 | tf_op jit(solution)/shard_map/while/body/eval_jaxpr/all_gather | solution.py:273
  1763.7 54.8 %all-gather.40.cloned.1.call-done = bf16[1,2048,2048]{2,1,0:T(8,128)(2,1)} async-done(((bf16[1,256,2048]{2,1,0:T(8,128)(2,1)}), bf16[1,2048,2048]{2,1,0:T(8,128)(2,1)}) %all-gather.40.cloned.1.call-update) | async-done | bytes 8388624 | tf_op jit(solution)/shard_map/while/body/eval_jaxpr/all_gather | solution.py:191
  1833.3 67.7 %all-gather.36.cloned.1.call-done = bf16[2048,1024]{1,0:T(8,128)(2,1)} async-done(((bf16[512,1024]{1,0:T(8,128)(2,1)}), bf16[2048,1024]{1,0:T(8,128)(2,1)}) %all-gather.36.cloned.1.call-update) | async-done | bytes 4194320 | tf_op jit(solution)/shard_map/while/body/eval_jaxpr/all_gather | solution.py:266
  1901.0 55.0 %all-gather.34.cloned.1.call-done = bf16[2048,2048]{1,0:T(8,128)(2,1)} async-done(((bf16[256,2048]{1,0:T(8,128)(2,1)}), bf16[2048,2048]{1,0:T(8,128)(2,1)}) %all-gather.34.cloned.1.call-update) | async-done | bytes 8388624 | tf_op jit(solution)/shard_map/while/body/eval_jaxpr/all_gather | solution.py:177
  1970.4 67.9 %all-gather.42.cloned.1.call-done = bf16[2048,1024]{1,0:T(8,128)(2,1)} async-done(((bf16[512,1024]{1,0:T(8,128)(2,1)}), bf16[2048,1024]{1,0:T(8,128)(2,1)}) %all-gather.42.cloned.1.call-update) | async-done | bytes 4194320 | tf_op jit(solution)/shard_map/while/body/eval_jaxpr/all_gather | solution.py:267
  2091.0 69.9 %reduce-scatter.14.cloned.1.call-done = bf16[256,2048]{1,0:T(8,128)(2,1)} async-done(((bf16[2048,2048]{1,0:T(8,128)(2,1)}), bf16[256,2048]{1,0:T(8,128)(2,1)}) %reduce-scatter.14.cloned.1.call-update) | async-done | bytes 1048592 | tf_op jit(solution)/shard_map/while/body/eval_jaxpr/reduce_scatter | solution.py:200
  2238.6 249.0 %while.64 = (s32[]{:T(128)}, f32[2048,4,64]{0,2,1:T(8,128)}, f32[2048,4,64]{0,2,1:T(8,128)}, f32[4,512,4,64]{1,0,3,2:T(4,128)}, bf16[4,512,4,64]{1,3,2,0:T(8,128...) while((s32[]{:T(128)}, f32[2048,4,64]{0,2,1:T(8,128)}, ...), condition=%wide.region_14.14_spmd.clone, body=%wide.region_12.13_spmd.clone.sunk | while | flops 2753165824 | bytes 183044368 | solution.py:136
  2585.0 71.8 %reduce-scatter.30.cloned.1.call-done = bf16[256,2048]{1,0:T(8,128)(2,1)} async-done(((bf16[2048,2048]{1,0:T(8,128)(2,1)}), bf16[256,2048]{1,0:T(8,128)(2,1)}) %reduce-scatter.30.cloned.1.call-update) | async-done | bytes 1048592 | tf_op jit(solution)/shard_map/while/body/eval_jaxpr/reduce_scatter | solution.py:223
  2658.8 72.7 %reduce-scatter.32.cloned.1.call-done = bf16[256,2048]{1,0:T(8,128)(2,1)} async-done(((bf16[2048,2048]{1,0:T(8,128)(2,1)}), bf16[256,2048]{1,0:T(8,128)(2,1)}) %reduce-scatter.32.cloned.1.call-update) | async-done | bytes 1048592 | tf_op jit(solution)/shard_map/while/body/eval_jaxpr/reduce_scatter | solution.py:185
  (657 shorter events, 1492.9 us)
Async XLA Ops:
  28.8 211.0 %all-gather.32.cloned.1.call-start = ((), (), s32[]{:S(2)}) async-start(), calls=%async_computation.15 | async-start | bytes 1310720 | tf_op jit(solution)/shard_map/while/body/eval_jaxpr/all_gather | solution.py:272
  29.3 288.7 %reduce-scatter.12.cloned.1.call-start = ((), (), s32[]{:S(2)}) async-start(), calls=%async_computation.16 | async-start | bytes 9437184 | tf_op jit(solution)/shard_map/while/body/eval_jaxpr/reduce_scatter | solution.py:169
  247.8 207.6 %all-gather.40.cloned.1.call-start = ((), (), s32[]{:S(2)}) async-start(), calls=%async_computation.20 | async-start | bytes 9437184 | tf_op jit(solution)/shard_map/while/body/eval_jaxpr/all_gather | solution.py:191
  250.2 287.6 %all-gather.36.cloned.1.call-start = ((), (), s32[]{:S(2)}) async-start(), calls=%async_computation.18 | async-start | bytes 5242880 | tf_op jit(solution)/shard_map/while/body/eval_jaxpr/all_gather | solution.py:266
  251.0 341.7 %all-gather.34.cloned.1.call-start = ((), (), s32[]{:S(2)}) async-start(), calls=%async_computation.17 | async-start | bytes 9437184 | tf_op jit(solution)/shard_map/while/body/eval_jaxpr/all_gather | solution.py:177
  322.3 352.9 %all-gather.42.cloned.1.call-start = ((), (), s32[]{:S(2)}) async-start(), calls=%async_computation.21 | async-start | bytes 5242880 | tf_op jit(solution)/shard_map/while/body/eval_jaxpr/all_gather | solution.py:267
  323.0 474.8 %reduce-scatter.14.cloned.1.call-start = ((), (), s32[]{:S(2)}) async-start(), calls=%async_computation.22 | async-start | bytes 9437184 | tf_op jit(solution)/shard_map/while/body/eval_jaxpr/reduce_scatter | solution.py:200
  804.7 395.0 %reduce-scatter.28.cloned.1.call-start = ((), (), s32[]{:S(2)}) async-start(), calls=%async_computation.30 | async-start | bytes 5242880 | tf_op jit(solution)/shard_map/while/body/eval_jaxpr/reduce_scatter | solution.py:299
  819.0 384.1 %reduce-scatter.22.cloned.1.call-start = ((), (), s32[]{:S(2)}) async-start(), calls=%async_computation.27 | async-start | bytes 5242880 | tf_op jit(solution)/shard_map/while/body/eval_jaxpr/reduce_scatter | solution.py:288
  833.1 373.9 %reduce-scatter.24.cloned.1.call-start = ((), (), s32[]{:S(2)}) async-start(), calls=%async_computation.28 | async-start | bytes 5242880 | tf_op jit(solution)/shard_map/while/body/eval_jaxpr/reduce_scatter | solution.py:291
  847.9 362.4 %reduce-scatter.26.cloned.1.call-start = ((), (), s32[]{:S(2)}) async-start(), calls=%async_computation.29 | async-start | bytes 1310720 | tf_op jit(solution)/shard_map/while/body/eval_jaxpr/reduce_scatter | solution.py:296
  875.4 336.8 %reduce-scatter.18.cloned.1.call-start = ((), (), s32[]{:S(2)}) async-start(), calls=%async_computation.25 | async-start | bytes 1310720 | tf_op jit(solution)/shard_map/while/body/eval_jaxpr/reduce_scatter | solution.py:282
  1393.3 209.8 %all-gather.32.cloned.1.call-start = ((), (), s32[]{:S(2)}) async-start(), calls=%async_computation.15 | async-start | bytes 1310720 | tf_op jit(solution)/shard_map/while/body/eval_jaxpr/all_gather | solution.py:272
  1393.9 287.4 %reduce-scatter.12.cloned.1.call-start = ((), (), s32[]{:S(2)}) async-start(), calls=%async_computation.16 | async-start | bytes 9437184 | tf_op jit(solution)/shard_map/while/body/eval_jaxpr/reduce_scatter | solution.py:169
  1611.1 207.4 %all-gather.40.cloned.1.call-start = ((), (), s32[]{:S(2)}) async-start(), calls=%async_computation.20 | async-start | bytes 9437184 | tf_op jit(solution)/shard_map/while/body/eval_jaxpr/all_gather | solution.py:191
  1613.5 287.5 %all-gather.36.cloned.1.call-start = ((), (), s32[]{:S(2)}) async-start(), calls=%async_computation.18 | async-start | bytes 5242880 | tf_op jit(solution)/shard_map/while/body/eval_jaxpr/all_gather | solution.py:266
  1614.3 341.7 %all-gather.34.cloned.1.call-start = ((), (), s32[]{:S(2)}) async-start(), calls=%async_computation.17 | async-start | bytes 9437184 | tf_op jit(solution)/shard_map/while/body/eval_jaxpr/all_gather | solution.py:177
  1685.6 352.8 %all-gather.42.cloned.1.call-start = ((), (), s32[]{:S(2)}) async-start(), calls=%async_computation.21 | async-start | bytes 5242880 | tf_op jit(solution)/shard_map/while/body/eval_jaxpr/all_gather | solution.py:267
  1686.2 474.8 %reduce-scatter.14.cloned.1.call-start = ((), (), s32[]{:S(2)}) async-start(), calls=%async_computation.22 | async-start | bytes 9437184 | tf_op jit(solution)/shard_map/while/body/eval_jaxpr/reduce_scatter | solution.py:200
  2167.9 395.0 %reduce-scatter.28.cloned.1.call-start = ((), (), s32[]{:S(2)}) async-start(), calls=%async_computation.30 | async-start | bytes 5242880 | tf_op jit(solution)/shard_map/while/body/eval_jaxpr/reduce_scatter | solution.py:299
  2182.2 384.1 %reduce-scatter.22.cloned.1.call-start = ((), (), s32[]{:S(2)}) async-start(), calls=%async_computation.27 | async-start | bytes 5242880 | tf_op jit(solution)/shard_map/while/body/eval_jaxpr/reduce_scatter | solution.py:288
  2196.3 374.5 %reduce-scatter.24.cloned.1.call-start = ((), (), s32[]{:S(2)}) async-start(), calls=%async_computation.28 | async-start | bytes 5242880 | tf_op jit(solution)/shard_map/while/body/eval_jaxpr/reduce_scatter | solution.py:291
  2211.0 363.7 %reduce-scatter.26.cloned.1.call-start = ((), (), s32[]{:S(2)}) async-start(), calls=%async_computation.29 | async-start | bytes 1310720 | tf_op jit(solution)/shard_map/while/body/eval_jaxpr/reduce_scatter | solution.py:296
  2238.5 338.2 %reduce-scatter.18.cloned.1.call-start = ((), (), s32[]{:S(2)}) async-start(), calls=%async_computation.25 | async-start | bytes 1310720 | tf_op jit(solution)/shard_map/while/body/eval_jaxpr/reduce_scatter | solution.py:282
  (128 other events, 7630.2 us)
Sparse Core Ops, SparseCore 0:
  42.7 53.8 all-gather.23
  247.2 70.7 reduce-scatter.11
  319.6 80.7 all-gather.37
  457.1 80.7 all-gather.35
  594.4 80.7 all-gather.41
  727.9 69.8 reduce-scatter.13
  804.8 54.3 all-gather.43
  861.4 76.7 reduce-scatter.27
  940.4 77.2 reduce-scatter.21
  1019.9 77.2 reduce-scatter.23
  1223.6 69.9 reduce-scatter.29
  1297.0 71.2 reduce-scatter.31
  1406.0 53.8 all-gather.23
  1610.5 70.7 reduce-scatter.11
  1683.0 80.7 all-gather.37
  1820.2 80.7 all-gather.35
  1957.5 80.7 all-gather.41
  2091.1 69.8 reduce-scatter.13
  2168.0 54.3 all-gather.43
  2224.5 76.7 reduce-scatter.27
  2303.6 77.2 reduce-scatter.21
  2383.2 77.2 reduce-scatter.23
  2586.7 69.9 reduce-scatter.29
  2660.2 71.2 reduce-scatter.31
  (20 shorter events, 647.7 us)
where the time goes:
time: 2790 us
  waiting for transfers between devices  1440 us (52%)
  matrix products  787 us (28%)
  other arithmetic  254 us (9%)
  local copies, waits for them, and re-layouts  161 us (6%)
  blocking collectives  89.3 us (3%)
  loops' own time  37.8 us (1%)
    dot_general x14, matrix products, mat_back(): lax.dot_general(left_op, right_op, (((1,), (1,)), ((), ())), preferred_el...  169 us
    all_gather x2, waiting for transfers between devices, fetch_weights(): lax.all_gather(w_down, 'narrow', axis=1, tiled=True)  155 us
    dot_general x14, matrix products, mat_plain(): return jnp.dot(left_op, right_op, preferred_element_type=jnp.float32)  151 us
    reduce_scatter x2, waiting for transfers between devices, one_row(): lax.psum_scatter(rounded(mat_plain(hidden, w_down)).astype(jnp.bfloat16),...  145 us
    reduce_scatter x2, waiting for transfers between devices, one_row(): lax.psum_scatter(rounded(mat_back(query_raw, w_query) + mat_back(key_raw,...  144 us
    reduce_scatter x2, waiting for transfers between devices, one_row(): lax.psum_scatter(rounded(mat_back(grad_gate_pre, w_gate) + mat_back(grad_...  140 us
    all_gather x2, waiting for transfers between devices, fetch_weights(): lax.all_gather(w_up, 'narrow', axis=0, tiled=True)  136 us
    all_gather x2, waiting for transfers between devices, fetch_weights(): lax.all_gather(w_gate, 'narrow', axis=0, tiled=True)  135 us
  transfers between devices with their start and end apart: 44, of which 30 were waited for; matrix products, arithmetic and copies ran while one was open for 38% of the time, Pallas kernels for 0%

commit v1 on v0

v1 whole, which is shorter than its diff:
```python
import functools

import jax
import jax.numpy as jnp
from jax import lax
from jax.experimental import pallas as pl
from jax.experimental.pallas import tpu as pltpu
from jax.sharding import PartitionSpec as P

HEAD_DIM = 64
EPS = 1e-05
NEG = -1e30
ROPE_BASE = 130000.0
F32 = jnp.float32
BF16 = jnp.bfloat16
NN = (((1,), (0,)), ((), ()))
NT = (((1,), (1,)), ((), ()))
TN = (((0,), (0,)), ((), ()))
VMEM_LIMIT = 60 * 1024 * 1024
COST = 0.02


def dot(left, right, dims=NN):
    return lax.dot_general(left, right, dims, preferred_element_type=F32)


def params_for(**extra):
    return pltpu.CompilerParams(vmem_limit_bytes=VMEM_LIMIT, **extra)


def cost(flops, bytes_accessed, transcendentals):
    return pl.CostEstimate(
        flops=int(flops * COST),
        bytes_accessed=int(bytes_accessed * COST),
        transcendentals=int(transcendentals * COST),
    )


def vmem():
    return pl.BlockSpec(memory_space=pltpu.VMEM)


def smem():
    return pl.BlockSpec(memory_space=pltpu.SMEM)


def bits_of(count):
    return count.bit_length() - 1


def offset_at(place, count):
    top = bits_of(count) - 1
    return ((place << 1) & (count - 1)) | (place >> top)


def place_of(offset, count):
    top = bits_of(count) - 1
    return (offset >> 1) | ((offset & 1) << top)


def swap(block, bit):
    count = lax.axis_size("wide")
    return lax.ppermute(block, "wide", [(i, i ^ (1 << bit)) for i in range(count)])


def after(value, *others):
    return lax.optimization_barrier((value,) + others)[0] if others else value


class Slots:
    def __init__(self):
        self.now = []
        self.then = []

    def gate(self, value):
        return after(value, *self.now)

    def ends(self, value):
        self.then.append(value)
        return value

    def turn(self):
        self.now = self.then or self.now
        self.then = []

    def swap(self, block, bit, axis="wide", hold=True):
        count = lax.axis_size(axis)
        pairs = [(i, i ^ (1 << bit)) for i in range(count)]
        got = lax.ppermute(self.gate(block), axis, pairs)
        return self.ends(got) if hold else got


class Gather:
    def __init__(self, slots, block):
        self.slots = slots
        self.block = block
        chip_bits = bits_of(lax.axis_size("wide")) - 1
        self.plain = not (chip_bits == 2 and block.shape[0] % 32 == 0)
        if not self.plain:
            self.from_x = slots.swap(block, 1)
            self.from_y = slots.swap(block, 2)

    def far(self):
        if not self.plain:
            half = self.block.shape[0] // 2
            self.far_low = self.slots.swap(self.from_y[:half], 1)
            self.far_high = self.slots.swap(self.from_x[half:], 2)

    def core(self):
        if self.plain:
            pieces = [self.block]
            for bit in range(1, bits_of(lax.axis_size("wide"))):
                pieces = pieces + [self.slots.swap(piece, bit) for piece in pieces]
        else:
            pieces = [self.block, self.from_x, self.from_y, self.far_low, self.far_high]
        own = jnp.concatenate(pieces, axis=0)
        self.halves = [own, self.slots.swap(own, 0)]


class Scatter:
    def __init__(self, slots, lefts, rights, dims):
        self.slots = slots
        self.factors = (lefts, rights, dims)
        self.sent = self.product(1)

    def product(self, side, got=None):
        lefts, rights, dims = self.factors
        lefts = [self.slots.gate(lefts[0])] + list(lefts[1:])
        made = partial_sums(lefts, rights, dims, side, got)
        self.slots.ends(made[0] if isinstance(made, (list, tuple)) else made)
        return made

    def core(self):
        self.got = self.slots.swap(self.sent, 0)

    def even(self):
        self.kept = self.product(0, self.got)

    def near(self):
        if isinstance(self.kept, (tuple, list)):
            self.got_x = self.slots.swap(self.kept[2], 1)
            self.got_y = self.slots.swap(self.kept[3], 2)
            return
        kept = self.kept
        for bit in reversed(range(bits_of(lax.axis_size("wide")) - 1)):
            rows = kept.shape[0] // 2
            got = self.slots.swap(kept[rows:], bit + 1)
            kept = (kept[:rows].astype(F32) + got.astype(F32)).astype(BF16)
        self.total = kept.astype(F32)

    def last(self):
        if not isinstance(self.kept, (tuple, list)):
            return
        keep_low, keep_high = self.kept[:2]
        half = keep_low.shape[0] // 2
        far_low = (keep_low[half:].astype(F32) + self.got_x[half:].astype(F32)).astype(BF16)
        far_high = (keep_high[half:].astype(F32) + self.got_y[half:].astype(F32)).astype(BF16)
        low = self.slots.swap(far_low, 2)
        high = self.slots.swap(far_high, 1)
        low = keep_low[:half].astype(F32) + self.got_x[:half].astype(F32) + low.astype(F32)
        high = keep_high[:half].astype(F32) + self.got_y[:half].astype(F32) + high.astype(F32)
        self.total = jnp.concatenate([low, high], axis=0)


def partner_lanes(values, width):
    lanes = lax.broadcasted_iota(jnp.int32, values.shape, 1)
    first = (lanes % HEAD_DIM) < HEAD_DIM // 2
    half = HEAD_DIM // 2
    return jnp.where(first, pltpu.roll(values, width - half, 1), pltpu.roll(values, half, 1))


def wide_table(table, width):
    copies = width // table.shape[1]
    return jnp.concatenate([table] * copies, axis=1) if copies > 1 else table


def streaming_call(streams, body, ins, in_specs, outs, out_specs, name, flops, moved):
    seq = sum(piece.shape[0] for piece in streams[0])
    rows = min(512, streams[0][0].shape[0])
    steps = seq // rows
    plan = []
    for number, pieces in enumerate(streams):
        first = 0
        for piece in pieces:
            plan.append((number, first, piece.shape[0]))
            first += piece.shape[0]
    count, groups = len(plan), len(streams)

    def kernel(*refs):
        piece_refs, rest = refs[:count], refs[count:]
        middle_refs, buffers, sems = rest[: -groups - 1], rest[-groups - 1 : -1], rest[-1]
        step = pl.program_id(0)

        def copies(block, slot):
            found = []
            for ref, (number, first, size) in zip(piece_refs, plan):
                place = block * rows - first
                if 0 <= place < size:
                    source = ref.at[pl.ds(place, rows)]
                    found.append(
                        pltpu.make_async_copy(
                            source, buffers[number].at[slot], sems.at[number, slot]
                        )
                    )
            return found

        for block in range(steps):

            @pl.when(step == (0 if block == 0 else block - 1))
            def _():
                for copy in copies(block, block % 2):
                    copy.start()

        for block in range(steps):

            @pl.when(step == block)
            def _():
                for copy in copies(block, block % 2):
                    copy.wait()

        slot = lax.rem(step, 2)
        body(*[buffer.at[slot] for buffer in buffers], *middle_refs)

    return pl.pallas_call(
        kernel,
        out_shape=outs,
        grid=(steps,),
        in_specs=[pl.BlockSpec(memory_space=pl.ANY)] * count + in_specs(rows),
        out_specs=out_specs(rows),
        scratch_shapes=[pltpu.VMEM((2, rows, pieces[0].shape[1]), BF16) for pieces in streams]
        + [pltpu.SemaphoreType.DMA((groups, 2))],
        compiler_params=params_for(),
        cost_estimate=cost(
            flops=flops,
            bytes_accessed=moved + sum(2 * seq * pieces[0].shape[1] for pieces in streams),
            transcendentals=0,
        ),
        name=name,
    )(*[piece for pieces in streams for piece in pieces], *ins)


def resident(array):
    shape = array.shape
    return pl.BlockSpec(shape, lambda i: (0,) * len(shape), pipeline_mode=pl.Buffered(1))


def by_rows(rows, cols):
    return pl.BlockSpec((rows, cols), lambda i: (i, 0))


def project_qkv(tokens, weights, cos, sin):
    seq = sum(piece.shape[0] for piece in tokens)
    dim, cols = weights.shape
    width = cols // 3

    def body(x_ref, w_ref, cos_ref, sin_ref, out_ref):
        raw = dot(x_ref[...], w_ref[...])
        cos = wide_table(cos_ref[...], width)
        sin = wide_table(sin_ref[...], width)
        query = raw[:, :width]
        key = raw[:, width : 2 * width]
        query = (query * cos + partner_lanes(query, width) * sin) * (HEAD_DIM**-0.5)
        key = key * cos + partner_lanes(key, width) * sin
        out_ref[:, :width] = query.astype(BF16)
        out_ref[:, width : 2 * width] = key.astype(BF16)
        out_ref[:, 2 * width :] = raw[:, 2 * width :].astype(BF16)

    return streaming_call(
        [tokens],
        body,
        [weights, cos, sin],
        lambda rows: [resident(weights), by_rows(rows, cos.shape[1]), by_rows(rows, sin.shape[1])],
        jax.ShapeDtypeStruct((seq, cols), BF16),
        lambda rows: by_rows(rows, cols),
        "project_qkv",
        2 * seq * dim * cols,
        2 * (dim * cols + seq * cols),
    )


def pull_back_out(tokens, w_out):
    seq = sum(piece.shape[0] for piece in tokens)
    width, dim = w_out.shape

    def body(x_ref, w_ref, out_ref):
        out_ref[...] = dot(x_ref[...], w_ref[...], NT).astype(BF16)

    return streaming_call(
        [tokens],
        body,
        [w_out],
        lambda rows: [resident(w_out)],
        jax.ShapeDtypeStruct((seq, width), BF16),
        lambda rows: by_rows(rows, width),
        "pull_back_out",
        2 * seq * dim * width,
        2 * (dim * width + seq * width),
    )


def mlp_body(x_ref, gy_ref, gu_ref, down_ref, hid_ref, dgu_ref):
    cols = hid_ref.shape[1]
    both = dot(x_ref[...], gu_ref[...])
    d_hid = dot(gy_ref[...], down_ref[...], NT)
    gp = both[:, :cols]
    up = both[:, cols:]
    sig = jax.nn.sigmoid(gp)
    silu = gp * sig
    hid_ref[...] = (silu * up).astype(BF16)
    dgu_ref[:, :cols] = (d_hid * up * sig * (1.0 + gp * (1.0 - sig))).astype(BF16)
    dgu_ref[:, cols:] = (d_hid * silu).astype(BF16)


def mlp_products(tokens, gy, w_gu, w_down):
    seq = sum(piece.shape[0] for piece in tokens)
    cols, dim = w_down.shape
    return streaming_call(
        [tokens, gy],
        mlp_body,
        [w_gu, w_down],
        lambda rows: [resident(w_gu), resident(w_down)],
        [jax.ShapeDtypeStruct((seq, cols), BF16), jax.ShapeDtypeStruct((seq, 2 * cols), BF16)],
        lambda rows: [by_rows(rows, cols), by_rows(rows, 2 * cols)],
        "mlp_products",
        6 * seq * dim * cols,
        2 * (3 * dim * cols + 3 * seq * cols),
    )


def partial_sums(lefts, rights, dims, side, got=None):
    seq = lefts[0].shape[0]
    dim = rights[0].shape[1] if dims == NN else rights[0].shape[0]
    rows = seq // 2
    count = len(lefts)
    wide = lax.axis_size("wide")
    chunk = seq // wide
    split = got is not None and bits_of(wide) == 3 and chunk % 32 == 0
    block = chunk if split else min(512, rows)
    steps = rows // block
    half = block // 2

    def kernel(*refs):
        total = None
        for left, right in zip(refs[:count], refs[count : 2 * count]):
            term = dot(left[...], right[...], dims)
            total = term if total is None else total + term
        if got is None:
            refs[-1][...] = total.astype(BF16)
            return
        total = total + refs[2 * count][...].astype(F32)
        if not split:
            refs[-1][...] = total.astype(BF16)
            return
        keep_low, keep_high, send_x, send_y = refs[-4:]
        step = pl.program_id(0)
        low = total[:half].astype(BF16)
        high = total[half:].astype(BF16)

        @pl.when(step % 2 == 0)
        def _():
            keep_low[...] = low

        @pl.when(step % 2 == 1)
        def _():
            send_x[...] = low

        @pl.when(step < 2)
        def _():
            keep_high[...] = high

        @pl.when(step >= 2)
        def _():
            send_y[...] = high

    in_specs = [
        pl.BlockSpec((block, left.shape[1]), lambda i: (side * steps + i, 0)) for left in lefts
    ] + [resident(right) for right in rights]
    ins = list(lefts) + list(rights)
    if got is not None:
        in_specs.append(by_rows(block, dim))
        ins.append(got)
    if split:
        out_shape = [jax.ShapeDtypeStruct((2 * half, dim), BF16)] * 4
        out_specs = [
            pl.BlockSpec((half, dim), lambda i: (i // 2, 0)),
            pl.BlockSpec((half, dim), lambda i: (jnp.minimum(i, 1), 0)),
            pl.BlockSpec((half, dim), lambda i: (i // 2, 0)),
            pl.BlockSpec((half, dim), lambda i: (jnp.maximum(i - 2, 0), 0)),
        ]
    else:
        out_shape = jax.ShapeDtypeStruct((rows, dim), BF16)
        out_specs = by_rows(block, dim)
    depth = sum(left.shape[1] for left in lefts)
    return pl.pallas_call(
        kernel,
        out_shape=out_shape,
        grid=(steps,),
        in_specs=in_specs,
        out_specs=out_specs,
        compiler_params=params_for(),
        cost_estimate=cost(
            flops=2 * rows * depth * dim,
            bytes_accessed=2 * (rows * depth + depth * dim + 2 * rows * dim),
            transcendentals=0,
        ),
        name="partial_sums",
    )(*ins)


def whole_sums(lefts, rights, dims, place):
    seq = lefts[0].shape[0]
    dim = rights[0].shape[1] if dims == NN else rights[0].shape[0]
    chunks = place.shape[0]
    block = seq // chunks
    count = len(lefts)

    def kernel(place_ref, *refs):
        total = None
        for left, right in zip(refs[:count], refs[count : 2 * count]):
            term = dot(left[...], right[...], dims)
            total = term if total is None else total + term
        refs[-1][...] = total.astype(BF16)

    def whole(array):
        return pl.BlockSpec(array.shape, lambda i, at: (0, 0), pipeline_mode=pl.Buffered(1))

    depth = sum(left.shape[1] for left in lefts)
    return pl.pallas_call(
        kernel,
        out_shape=jax.ShapeDtypeStruct((seq, dim), BF16),
        grid_spec=pltpu.PrefetchScalarGridSpec(
            num_scalar_prefetch=1,
            grid=(chunks,),
            in_specs=[
                pl.BlockSpec((block, left.shape[1]), lambda i, at: (at[i], 0)) for left in lefts
            ]
            + [whole(right) for right in rights],
            out_specs=pl.BlockSpec((block, dim), lambda i, at: (i, 0)),
        ),
        compiler_params=params_for(),
        cost_estimate=cost(
            flops=2 * seq * depth * dim,
            bytes_accessed=2 * (seq * depth + depth * dim + seq * dim),
            transcendentals=0,
        ),
        name="whole_sums",
    )(place, *lefts, *rights)


def halves(array):
    if isinstance(array, (list, tuple)):
        return [(half, 0) for half in array]
    return [(array, 0), (array, 1)]


def weight_grad(lefts, rights, seq):
    seq //= 2
    lefts = [pair for left in lefts for pair in halves(left)]
    rights = [pair for right in rights for pair in halves(right)]
    height = lefts[0][0].shape[1]
    cols = rights[0][0].shape[1]
    tall = min(512 if height < 1024 else 256, height)
    wide = min(1024, cols)
    count = len(lefts)

    def kernel(*refs):
        total = None
        for left, right in zip(refs[:count], refs[count : 2 * count]):
            term = dot(left[...], right[...], TN)
            total = term if total is None else total + term
        refs[-1][...] = total.astype(BF16)

    return pl.pallas_call(
        kernel,
        out_shape=jax.ShapeDtypeStruct((height, cols), BF16),
        grid=(cols // wide, height // tall),
        in_specs=[pl.BlockSpec((seq, tall), lambda n, m, p=p: (p, m)) for _, p in lefts]
        + [pl.BlockSpec((seq, wide), lambda n, m, p=p: (p, n)) for _, p in rights],
        out_specs=pl.BlockSpec((tall, wide), lambda n, m: (m, n)),
        compiler_params=params_for(),
        cost_estimate=cost(
            flops=2 * seq * height * cols * count,
            bytes_accessed=2 * count * (seq * height * (cols // wide) + seq * cols),
            transcendentals=0,
        ),
        name="weight_grad",
    )(*[a for a, _ in lefts], *[a for a, _ in rights])


def head_stack(block, heads):
    lanes = lax.broadcasted_iota(jnp.int32, block.shape, 1) // HEAD_DIM
    zero = jnp.zeros_like(block)
    return jnp.concatenate([jnp.where(lanes == h, block, zero) for h in range(heads)], axis=0)


def block_mask(first_key, first_query, begins, size):
    keys = first_key + lax.broadcasted_iota(jnp.int32, (size, size), 0)
    queries = first_query + lax.broadcasted_iota(jnp.int32, (size, size), 1)
    return (keys <= queries) & (keys >= begins)


def forward_kernel(heads, blocks, size, low_ref, place_ref, begins_ref, qkv_ref, att_ref, lse_ref, vt_ref):
    width = heads * HEAD_DIM

    def spin(b, carry):
        rows = pl.ds(pl.multiple_of(place_ref[b] * size, size), size)
        vt_ref[b] = qkv_ref[rows, 2 * width :].astype(F32).T.astype(BF16)
        return carry

    lax.fori_loop(0, blocks, spin, 0)

    def one_query_block(i, carry):
        rows = pl.ds(pl.multiple_of(place_ref[i] * size, size), size)
        stack = head_stack(qkv_ref[rows, :width], heads)
        begins = begins_ref[i]

        def one_key_block(j, state):
            maxes, totals, sums = state
            keys = pl.ds(pl.multiple_of(place_ref[j] * size, size), size)
            scores = dot(qkv_ref[keys, width : 2 * width], stack, NT)
            allowed = block_mask(j * size, i * size, begins, size)
            new_maxes, new_totals, new_sums = [], [], []
            for h in range(heads):
                part = jnp.where(allowed, scores[:, h * size : (h + 1) * size], NEG)
                peak = jnp.maximum(maxes[h], jnp.max(part, axis=0, keepdims=True))
                fade = jnp.exp(maxes[h] - peak)
                probs = jnp.exp(part - peak)
                new_maxes.append(peak)
                new_totals.append(totals[h] * fade + jnp.sum(probs, axis=0, keepdims=True))
                values_t = vt_ref[j, h * HEAD_DIM : (h + 1) * HEAD_DIM, :]
                new_sums.append(sums[h] * fade + dot(values_t, probs.astype(BF16)))
            return (tuple(new_maxes), tuple(new_totals), tuple(new_sums))

        start = (
            tuple(jnp.full((1, size), NEG, F32) for _ in range(heads)),
            tuple(jnp.zeros((1, size), F32) for _ in range(heads)),
            tuple(jnp.zeros((HEAD_DIM, size), F32) for _ in range(heads)),
        )
        maxes, totals, sums = lax.fori_loop(low_ref[i], i + 1, one_key_block, start)
        outs = jnp.concatenate([sums[h] / totals[h] for h in range(heads)], axis=0)
        att_ref[rows, :] = outs.T.astype(BF16)
        for h in range(heads):
            lse_ref[i, h : h + 1, :] = maxes[h] + jnp.log(totals[h])
        return carry

    lax.fori_loop(0, blocks, one_query_block, 0)


def attend_forward(qkv, low, place, begins, heads):
    seq = qkv.shape[0]
    blocks, _, size = begins.shape
    width = heads * HEAD_DIM
    pairs = seq * seq // 3
    return pl.pallas_call(
        functools.partial(forward_kernel, heads, blocks, size),
        out_shape=(
            jax.ShapeDtypeStruct((seq, width), BF16),
            jax.ShapeDtypeStruct((blocks, heads, size), F32),
        ),
        in_specs=[smem(), smem(), vmem(), vmem()],
        out_specs=(vmem(), vmem()),
        scratch_shapes=[pltpu.VMEM((blocks, width, size), BF16)],
        compiler_params=params_for(),
        cost_estimate=cost(
            flops=16 * pairs * width,
            bytes_accessed=2 * seq * width * 4,
            transcendentals=pairs * heads,
        ),
        name="attend_forward",
    )(low, place, begins, qkv)


def backward_kernel(
    heads,
    blocks,
    size,
    low_ref,
    place_ref,
    begins_ref,
    qkv_ref,
    att_ref,
    grad_ref,
    lse_ref,
    cos_ref,
    sin_ref,
    out_ref,
    kt_ref,
    dk_ref,
    dv_ref,
):
    width = heads * HEAD_DIM
    scale = HEAD_DIM**-0.5

    def spin(b, carry):
        rows = pl.ds(pl.multiple_of(place_ref[b] * size, size), size)
        kt_ref[b] = qkv_ref[rows, width : 2 * width].astype(F32).T.astype(BF16)
        dk_ref[b] = jnp.zeros((size, width), F32)
        dv_ref[b] = jnp.zeros((size, width), F32)
        return carry

    lax.fori_loop(0, blocks, spin, 0)

    def unrotate(values, rows):
        cos = wide_table(cos_ref[rows, :], width)
        sin = wide_table(sin_ref[rows, :], width)
        return values * cos - partner_lanes(values, width) * sin

    def one_query_block(i, carry):
        rows = pl.ds(pl.multiple_of(place_ref[i] * size, size), size)
        q_stack = head_stack(qkv_ref[rows, :width], heads)
        grad = grad_ref[rows, :]
        g_stack = head_stack(grad, heads)
        product = (grad.astype(F32) * att_ref[rows, :].astype(F32)).T
        deltas = [
            jnp.sum(product[h * HEAD_DIM : (h + 1) * HEAD_DIM], axis=0, keepdims=True)
            for h in range(heads)
        ]
        begins = begins_ref[i]

        def one_key_block(j, sums):
            keys = pl.ds(pl.multiple_of(place_ref[j] * size, size), size)
            scores = dot(qkv_ref[keys, width : 2 * width], q_stack, NT)
            grads = dot(qkv_ref[keys, 2 * width :], g_stack, NT)
            allowed = block_mask(j * size, i * size, begins, size)
            all_probs, all_ds, new_sums = [], [], []
            for h in range(heads):
                span = slice(h * size, (h + 1) * size)
                part = jnp.where(allowed, scores[:, span] - lse_ref[i, h : h + 1, :], NEG)
                probs = jnp.exp(part)
                d_scores = (probs * (grads[:, span] - deltas[h])).astype(BF16)
                all_probs.append(probs.astype(BF16))
                all_ds.append(d_scores)
                keys_t = kt_ref[j, h * HEAD_DIM : (h + 1) * HEAD_DIM, :]
                new_sums.append(sums[h] + dot(keys_t, d_scores))
            dv_ref[j] += dot(jnp.concatenate(all_probs, axis=1), g_stack)
            dk_ref[j] += dot(jnp.concatenate(all_ds, axis=1), q_stack)
            return tuple(new_sums)

        start = tuple(jnp.zeros((HEAD_DIM, size), F32) for _ in range(heads))
        sums = lax.fori_loop(low_ref[i], i + 1, one_key_block, start)
        query_grad = jnp.concatenate(sums, axis=0).T * scale
        out_ref[rows, :width] = unrotate(query_grad, rows).astype(BF16)
        return carry

    lax.fori_loop(0, blocks, one_query_block, 0)

    def finish(b, carry):
        rows = pl.ds(pl.multiple_of(place_ref[b] * size, size), size)
        out_ref[rows, width : 2 * width] = unrotate(dk_ref[b], rows).astype(BF16)
        out_ref[rows, 2 * width :] = dv_ref[b].astype(BF16)
        return carry

    lax.fori_loop(0, blocks, finish, 0)


def attend_backward(qkv, att, grad, lse, low, place, begins, cos, sin, heads):
    seq = qkv.shape[0]
    blocks, _, size = begins.shape
    width = heads * HEAD_DIM
    pairs = seq * seq // 3
    return pl.pallas_call(
        functools.partial(backward_kernel, heads, blocks, size),
        out_shape=jax.ShapeDtypeStruct((seq, 3 * width), BF16),
        in_specs=[smem(), smem()] + [vmem()] * 7,
        out_specs=vmem(),
        scratch_shapes=[
            pltpu.VMEM((blocks, width, size), BF16),
            pltpu.VMEM((blocks, size, width), F32),
            pltpu.VMEM((blocks, size, width), F32),
        ],
        compiler_params=params_for(),
        cost_estimate=cost(
            flops=40 * pairs * width,
            bytes_accessed=2 * seq * width * 10,
            transcendentals=pairs * heads,
        ),
        name="attend_backward",
    )(low, place, begins, qkv, att, grad, lse, cos, sin)


def row_facts(lengths, seq):
    wide = lax.axis_size("wide")
    me = lax.axis_index("wide")
    chunk = seq // wide
    docs = lengths.shape[0]
    upto = jnp.arange(docs)[:, None] <= jnp.arange(docs)[None, :]
    ends = jnp.sum(jnp.where(upto, lengths[:, None], 0), axis=0).astype(jnp.int32)

    def starts_of(tokens):
        before = jnp.where(ends[None, :] <= tokens[:, None], ends[None, :], jnp.int32(0))
        return jnp.max(before, axis=1)

    tokens = jnp.arange(seq, dtype=jnp.int32)
    begins = starts_of(tokens).reshape(wide, 1, chunk)
    low = begins[:, 0, 0] // chunk
    index = jnp.arange(wide, dtype=jnp.int32)
    place = place_of(index ^ me, wide)
    owner = me ^ offset_at(index, wide)
    here = (owner[:, None] * chunk + jnp.arange(chunk, dtype=jnp.int32)[None, :]).reshape(seq)
    position = (here - starts_of(here)).astype(F32)
    half_dim = HEAD_DIM // 2
    inverse = ROPE_BASE ** (-(jnp.arange(half_dim, dtype=F32) * 2.0) / HEAD_DIM)
    angles = position[:, None] * inverse[None, :]
    cos = jnp.cos(angles)
    sin = jnp.sin(angles)
    cos = jnp.concatenate([cos, cos, cos, cos], axis=1)
    sin = jnp.concatenate([-sin, sin, -sin, sin], axis=1)
    return low, place, begins, cos, sin


def norm_scale(values):
    return lax.rsqrt(jnp.mean(values * values, axis=-1, keepdims=True) + EPS)


def per_device(
    hidden_in,
    out_grad,
    doc_lengths,
    attn_gain,
    w_query,
    w_key,
    w_value,
    w_out,
    mlp_gain,
    w_gate,
    w_up,
    w_down,
):
    narrow = lax.axis_size("narrow")
    wide = lax.axis_size("wide")
    here = lax.axis_index("narrow")
    rows_here, chunk, dim = hidden_in.shape
    seq = chunk * wide
    width = w_query.shape[1]
    heads = width // HEAD_DIM

    def fetch(weight, axis):
        return lax.all_gather(weight, "narrow", axis=axis, tiled=True)

    gains = jnp.stack([attn_gain, mlp_gain])
    turned = [gains]
    for step in range(1, narrow):
        turned.append(
            lax.ppermute(gains, "narrow", [((i + step) % narrow, i) for i in range(narrow)])
        )
    order = (jnp.arange(narrow) - here) % narrow
    gains = jnp.take(jnp.stack(turned), order, axis=0)
    gains = jnp.swapaxes(gains, 0, 1).reshape(2, dim).astype(F32)
    attn_scale = gains[0]
    mlp_scale = gains[1]

    slots = Slots()
    gate, ends, turn = slots.gate, slots.ends, slots.turn
    hidden = w_gate.shape[1]
    cut = hidden // 2
    spans = [slice(0, cut), slice(cut, hidden)]
    w_qkv = fetch(jnp.concatenate([w_query, w_key, w_value], axis=1), 0)
    full_out = fetch(w_out, 1)
    full_gu, full_down = [], []
    for span in spans:
        full_gu.append(fetch(jnp.concatenate([w_gate[:, span], w_up[:, span]], axis=1), 0))
        full_down.append(fetch(w_down[span], 1))

    rows = range(rows_here)
    last = rows_here - 1
    facts = [row_facts(doc_lengths[r], seq) for r in rows]
    residual = [hidden_in[r].astype(F32) for r in rows]
    inv_first = [norm_scale(residual[r]) for r in rows]
    normed = [residual[r] * inv_first[r] for r in rows]
    scaled_in = [(normed[r] * attn_scale).astype(BF16) for r in rows]

    attn_in, gy, mlp_in, branch = {}, {}, {}, {}
    qkv, att, lse, middle, inv_second, normed_mid = ({} for _ in range(6))
    grad_middle, gain_mlp, gain_attn, outputs, in_grads, d_qkv = ({} for _ in range(6))
    hid = {r: [] for r in rows}
    d_gu = {r: [] for r in rows}

    def first_of(halves):
        return [gate(halves[0])] + list(halves[1:])

    def project(r):
        _, _, _, cos, sin = facts[r]
        qkv[r] = ends(project_qkv(first_of(attn_in[r].halves), w_qkv, cos, sin))

    def attend(r):
        low, place, begins, _, _ = facts[r]
        att[r], lse[r] = attend_forward(gate(qkv[r]), low, place, begins, heads)
        ends(att[r])

    def spread(lefts, rights, dims):
        return Scatter(slots, lefts, rights, dims)

    def after_attention(r, total):
        total = gate(total)
        middle[r] = residual[r] + total
        inv_second[r] = norm_scale(middle[r])
        normed_mid[r] = middle[r] * inv_second[r]
        mlp_in[r] = Gather(slots, (normed_mid[r] * mlp_scale).astype(BF16))

    def mlp(r, part):
        one, two = mlp_products(
            first_of(mlp_in[r].halves), gy[r].halves, full_gu[part], full_down[part]
        )
        ends(one)
        hid[r].append(one)
        d_gu[r].append(two)

    def after_mlp(r, total):
        total = gate(total)
        gain_mlp[r] = jnp.sum(total * normed_mid[r], axis=0)
        scaled = total * mlp_scale
        grad_middle[r] = out_grad[r].astype(F32) + inv_second[r] * (
            scaled - normed_mid[r] * jnp.mean(scaled * normed_mid[r], axis=-1, keepdims=True)
        )
        branch[r] = Gather(slots, grad_middle[r].astype(BF16))

    def back_attention(r):
        low, place, begins, cos, sin = facts[r]
        grad_att = pull_back_out(first_of(branch[r].halves), full_out)
        d_qkv[r] = ends(
            attend_backward(
                qkv[r], att[r], grad_att, lse[r], low, place, begins, cos, sin, heads
            )
        )

    def after_back(r, total):
        total = gate(total)
        gain_attn[r] = jnp.sum(total * normed[r], axis=0)
        scaled = total * attn_scale
        in_grads[r] = (
            grad_middle[r]
            + inv_first[r]
            * (scaled - normed[r] * jnp.mean(scaled * normed[r], axis=-1, keepdims=True))
        ).astype(BF16)

    def grad_of(lefts, rights, axis):
        lefts = [lefts[r] for r in rows]
        lefts[0] = first_of(lefts[0]) if isinstance(lefts[0], list) else gate(lefts[0])
        grad = ends(weight_grad(lefts, [rights[r] for r in rows], seq))
        return lax.psum_scatter(grad, "narrow", scatter_dimension=axis, tiled=True).astype(F32)

    def both(table):
        return [table[r] for r in rows]

    def halves_of(table):
        return {r: table[r].halves for r in rows}

    def part_of(table, part):
        return {r: table[r][part] for r in rows}

    sums, down, grad_gu, grad_down = {}, {}, [None, None], [None, None]

    def out_sum(r):
        sums[r] = spread([att[r]], [full_out], NN)

    def mlp_sum(r):
        whole = ends(whole_sums(first_of(d_gu[r]), full_gu, NT, facts[r][1]))
        sums[r] = lax.psum_scatter(whole, "wide", scatter_dimension=0, tiled=True).astype(F32)

    def back_sum(r):
        sums[r] = spread([d_qkv[r]], [w_qkv], NT)

    def down_sum(r):
        down[r] = spread(hid[r], full_down, NN)

    def gu_grad(part):
        grad_gu[part] = grad_of(halves_of(mlp_in), part_of(d_gu, part), 0)

    def down_grad(part):
        grad_down[part] = grad_of(part_of(hid, part), halves_of(gy), 1)

    one, two = 0, last
    attn_in[one] = Gather(slots, scaled_in[one])
    turn()
    attn_in[one].far()
    turn()
    attn_in[one].core()
    ends(w_qkv)
    turn()
    project(one)
    attn_in[two] = Gather(slots, scaled_in[two])
    ends(full_out)
    turn()
    attend(one)
    attn_in[two].far()
    turn()
    out_sum(one)
    attn_in[two].core()
    turn()
    project(two)
    sums[one].core()
    gy[one] = Gather(slots, out_grad[one])
    ends(full_down[0])
    turn()
    sums[one].even()
    gy[one].far()
    turn()
    attend(two)
    sums[one].near()
    gy[one].core()
    turn()
    out_sum(two)
    sums[one].last()
    ends(full_gu[0])
    turn()
    after_attention(one, sums[one].total)
    sums[two].core()
    turn()
    sums[two].even()
    mlp_in[one].far()
    turn()
    mlp_in[one].core()
    sums[two].near()
    ends(full_down[1])
    turn()
    mlp(one, 0)
    sums[two].last()
    gy[two] = Gather(slots, out_grad[two])
    turn()
    after_attention(two, sums[two].total)
    gy[two].far()
    turn()
    mlp_in[two].far()
    gy[two].core()
    ends(full_gu[1])
    turn()
    mlp(one, 1)
    mlp_in[two].core()
    turn()
    mlp_sum(one)
    turn()
    mlp(two, 0)
    turn()
    mlp(two, 1)
    turn()
    mlp_sum(two)
    turn()
    gu_grad(0)
    after_mlp(one, sums[one])
    turn()
    gu_grad(1)
    branch[one].far()
    turn()
    down_sum(one)
    down_sum(two)
    branch[one].core()
    turn()
    back_attention(one)
    after_mlp(two, sums[two])
    down[one].core()
    down[two].core()
    turn()
    back_sum(one)
    down[one].even()
    branch[two].far()
    turn()
    down_grad(0)
    branch[two].core()
    sums[one].core()
    down[one].near()
    turn()
    sums[one].even()
    down[two].even()
    down[one].last()
    turn()
    back_attention(two)
    sums[one].near()
    turn()
    back_sum(two)
    sums[one].last()
    turn()
    grad_qkv = grad_of(halves_of(attn_in), d_qkv, 0)
    sums[two].core()
    down[two].near()
    turn()
    sums[two].even()
    down[two].last()
    turn()
    grad_out = grad_of(att, halves_of(branch), 1)
    down_grad(1)
    sums[two].near()
    turn()
    sums[two].last()
    turn()
    for r in rows:
        outputs[r] = (middle[r] + down[r].total).astype(BF16)
        after_back(r, sums[r].total)

    def spread_gain(parts):
        total = sum(parts[1:], parts[0])
        for axis in ("narrow", "wide"):
            count = lax.axis_size(axis)
            me = lax.axis_index(axis)
            for bit in reversed(range(bits_of(count))):
                size = total.shape[0] // 2
                mine = (me >> bit) & 1
                sent = lax.dynamic_slice_in_dim(total, (1 - mine) * size, size)
                kept = lax.dynamic_slice_in_dim(total, mine * size, size)
                pairs = [(i, i ^ (1 << bit)) for i in range(count)]
                total = kept + lax.ppermute(sent, axis, pairs)
        return total

    grad_gate = [piece[:, :cut] for piece in grad_gu]
    grad_up = [piece[:, cut:] for piece in grad_gu]
    return (
        jnp.stack(both(outputs)),
        jnp.stack(both(in_grads)),
        spread_gain(both(gain_attn)),
        grad_qkv[:, :width],
        grad_qkv[:, width : 2 * width],
        grad_qkv[:, 2 * width :],
        grad_out,
        spread_gain(both(gain_mlp)),
        jnp.concatenate(grad_gate, axis=1),
        jnp.concatenate(grad_up, axis=1),
        jnp.concatenate(grad_down, axis=0),
    )


def solution(mesh):
    in_specs = (
        P("narrow", "wide", None),
        P("narrow", "wide", None),
        P("narrow", None),
        P("narrow"),
        P("narrow", "wide"),
        P("narrow", "wide"),
        P("narrow", "wide"),
        P("wide", "narrow"),
        P("narrow"),
        P("narrow", "wide"),
        P("narrow", "wide"),
        P("wide", "narrow"),
    )
    out_specs = (
        P("narrow", "wide", None),
        P("narrow", "wide", None),
        P(("narrow", "wide")),
        P("narrow", "wide"),
        P("narrow", "wide"),
        P("narrow", "wide"),
        P("wide", "narrow"),
        P(("narrow", "wide")),
        P("narrow", "wide"),
        P("narrow", "wide"),
        P("wide", "narrow"),
    )
    return jax.shard_map(
        per_device, mesh=mesh, in_specs=in_specs, out_specs=out_specs, check_vma=False
    )
```

time: 2790 us -> 1090 us (0.39)
  waiting for transfers between devices: 1440 us -> 310 us
  matrix products: 787 us -> 0 us
  Pallas kernels: 0 us -> 479 us
  other arithmetic: 254 us -> 96.5 us
  blocking collectives: 89.3 us -> 0 us
  starting transfers between devices: 2.21 us -> 85.6 us
  local copies, waits for them, and re-layouts: 161 us -> 90.2 us
  loops' own time: 37.8 us -> 0 us
    all_gather x22 -> x6, waiting for transfers between devices: 886 us -> 81.4 us  [fetch(): return lax.all_gather(weight, 'narrow', axis=axis, tiled=True)]
    dot_general x98 -> x0, matrix products: 787 us -> none  [the longest x14 169 us: mat_back(): lax.dot_general(left_op, right_op, (((1,), (1,)), ((), ())), preferred_el...]
    reduce_scatter x22 -> x8, waiting for transfers between devices: 545 us -> 29.3 us  [the longest x6 26.7 us: grad_of(): lax.psum_scatter(grad, 'narrow', scatter_dimension=axis, tiled=True)]
    pallas_call x0 -> x32, Pallas kernels: none -> 479 us  [the longest x8 125 us: streaming_call(): pl.pallas_call(kernel, out_shape=outs, grid=(steps,), in_specs=[pl.BlockS...]
    ppermute x0 -> x83, waiting for transfers between devices: none -> 199 us  [the longest x70 181 us: swap(): got = lax.ppermute(self.gate(block), axis, pairs)]
    dynamic_update_slice x16 -> x0, local copies, waits for them, and re-layouts: 93.2 us -> none  [attend_forward(): block_outs, log_totals = lax.map(one_block, (blocks, firsts))]
    convert_element_type x22 -> x17, other arithmetic: 110 us -> 23.8 us  [the longest x6 10.2 us: last(): (keep_low[half:].astype(F32) + self.got_x[half:].astype(F32)).astype(BF16)]
    ppermute x0 -> x83, starting transfers between devices: none -> 83.6 us  [the longest x70 64.2 us: swap(): got = lax.ppermute(self.gate(block), axis, pairs)]
  transfers between devices with their start and end apart: 44 -> 97, of which waited for: 30 -> 42; matrix products, arithmetic and copies ran while one was open for 38% -> 16% of each run, Pallas kernels for 0% -> 42%
where the time goes in v1:
time: 1090 us; the launch traced here: 1080 us
  Pallas kernels  479 us (44%)
  waiting for transfers between devices  310 us (28%)
  other arithmetic  96.5 us (9%)
  local copies, waits for them, and re-layouts  90.2 us (8%)
  starting transfers between devices  85.6 us (8%)
  between operations  15.5 us (1%)
    ppermute x70, waiting for transfers between devices, swap(): got = lax.ppermute(self.gate(block), axis, pairs)  181 us
    pallas_call x8, Pallas kernels, streaming_call(): pl.pallas_call(kernel, out_shape=outs, grid=(steps,), in_specs=[pl.BlockS...  125 us
    pallas_call x6, Pallas kernels, weight_grad(): pl.pallas_call(kernel, out_shape=jax.ShapeDtypeStruct((height, cols), BF1...  111 us
    pallas_call x12, Pallas kernels, partial_sums(): pl.pallas_call(kernel, out_shape=out_shape, grid=(steps,), in_specs=in_sp...  91.5 us
    all_gather x6, waiting for transfers between devices, fetch(): return lax.all_gather(weight, 'narrow', axis=axis, tiled=True)  81.4 us
    ppermute x70, starting transfers between devices, swap(): got = lax.ppermute(self.gate(block), axis, pairs)  64.2 us
    pallas_call x2, Pallas kernels, attend_backward(): pl.pallas_call(functools.partial(backward_kernel, heads, blocks, size), o...  64.1 us
    unnamed x134, local copies, waits for them, and re-layouts  49.6 us
  transfers between devices with their start and end apart: 97, of which 42 were waited for; matrix products, arithmetic and copies ran while one was open for 16% of the time, Pallas kernels for 42%

profile of v1, /device:TPU:0, one launch (start us, length us, event | category | flops | bytes accessed | tf_op | source)
XLA Modules:
  0.0 1077.2 jit_solution(1574690010714847454)
XLA Ops:
  26.9 19.4 %collective-permute-done.4 = bf16[256,2048]{1,0:T(8,128)(2,1)S(1)} collective-permute-done((bf16[256,2048]{1,0:T(8,128)(2,1)}, bf16[256,2048]{1,0:T(8,128)(2,1)S(1)}, u32[]{:S(2)}, u32[]{:S(2)}) %collective-permute-start.4) | collective-permute-done | bytes 1048608 | tf_op jit(solution)/shard_map/ppermute | solution.py:89
  62.9 24.0 %all-gather.7.cloned.1.call-done.refs_2_.refs_1_ = bf16[2048,768]{1,0:T(8,128)(2,1)} async-done(((bf16[512,768]{1,0:T(8,128)(2,1)}), bf16[2048,768]{1,0:T(8,128)(2,1)}) %all-gather.7.cloned.1.call-update) | async-done | bytes 3145744 | tf_op jit(solution)/shard_map/all_gather | solution.py:738
  122.8 17.4 %attend_forward.2 = (bf16[2048,256]{1,0:T(8,128)(2,1)}, f32[8,4,256]{2,1,0:T(4,128)}) custom-call(s32[8]{0:T(128)} %and_select_fusion.3.low_ref, s32[8]{0:T(128)} %shift-left_or_fusion.place_ref, s32[8,1,256]{2,1,0:T(1,128)} %bitcast.86, bf16[2048,768]{1,0:T(8,128)(2,1)} %project_qkv.2.qkv_ref), custom_call_target="tpu_custom_call" | custom-call | flops 114532432 | bytes 83886 | tf_op jit(solution)/shard_map/attend_forward/pallas_call | solution.py:554
  185.4 18.2 %all-gather.11.cloned.1.call-done.refs_5_.refs_2_ = bf16[512,2048]{1,0:T(8,128)(2,1)} async-done(((bf16[512,512]{1,0:T(8,128)(2,1)}), bf16[512,2048]{1,0:T(8,128)(2,1)}) %all-gather.11.cloned.1.call-update) | async-done | bytes 2097168 | tf_op jit(solution)/shard_map/all_gather | solution.py:738
  227.3 21.1 %attend_forward.3 = (bf16[2048,256]{1,0:T(8,128)(2,1)}, f32[8,4,256]{2,1,0:T(4,128)}) custom-call(s32[8]{0:T(128)} %and_select_fusion.low_ref, s32[8]{0:T(128)} %shift-left_or_fusion.place_ref, s32[8,1,256]{2,1,0:T(1,128)} %bitcast.83, bf16[2048,768]{1,0:T(8,128)(2,1)} %project_qkv.3.qkv_ref), custom_call_target="tpu_custom_call" | custom-call | flops 114532432 | bytes 83886 | tf_op jit(solution)/shard_map/attend_forward/pallas_call | solution.py:554
  260.6 24.5 %all-gather.13.cloned.1.call-done.refs_4_.refs_2_ = bf16[2048,1024]{1,0:T(8,128)(2,1)} async-done(((bf16[512,1024]{1,0:T(8,128)(2,1)}), bf16[2048,1024]{1,0:T(8,128)(2,1)}) %all-gather.13.cloned.1.call-update) | async-done | bytes 4194320 | tf_op jit(solution)/shard_map/all_gather | solution.py:738
  293.4 22.6 %collective-permute-done.24 = bf16[256,2048]{1,0:T(8,128)(2,1)S(1)} collective-permute-done((bf16[256,2048]{1,0:T(8,128)(2,1)S(1)}, bf16[256,2048]{1,0:T(8,128)(2,1)S(1)}, u32[]{:S(2)}, u32[]{:S(2)}) %collective-permute-start.24) | collective-permute-done | bytes 1048608 | tf_op jit(solution)/shard_map/ppermute | solution.py:89
  336.7 23.9 %collective-permute-done.29 = bf16[256,2048]{1,0:T(8,128)(2,1)S(1)} collective-permute-done((bf16[256,2048]{1,0:T(8,128)(2,1)}, bf16[256,2048]{1,0:T(8,128)(2,1)S(1)}, u32[]{:S(2)}, u32[]{:S(2)}) %collective-permute-start.29) | collective-permute-done | bytes 1048608 | tf_op jit(solution)/shard_map/ppermute | solution.py:89
  385.2 21.3 %mlp_products.4 = (bf16[2048,512]{1,0:T(8,128)(2,1)}, bf16[2048,1024]{1,0:T(8,128)(2,1)}) custom-call(bf16[1024,2048]{1,0:T(8,128)(2,1)} %constant_dynamic-update-slice_fusion.15.refs_0_, bf16[1024,2048]{1,0:T(8,128)(2,1)} %collective-permute-done.28.refs_1_, bf16[1024,2048]{1,0:T(8,128)(2,1)} %constant_dynamic-update-slice_fusion.10.refs_2_.refs_4_, ...), custom_call_target="tpu_custom_call" | custom-call | flops 257698032 | bytes 587202 | tf_op jit(solution)/shard_map/mlp_products/pallas_call | solution.py:224
  431.4 25.9 %collective-permute-done.37 = bf16[128,2048]{1,0:T(8,128)(2,1)S(1)} collective-permute-done((bf16[128,2048]{1,0:T(8,128)(2,1)S(1)}, bf16[128,2048]{1,0:T(8,128)(2,1)S(1)}, u32[]{:S(2)}, u32[]{:S(2)}) %collective-permute-start.37) | collective-permute-done | bytes 524320 | tf_op jit(solution)/shard_map/ppermute | solution.py:89
  475.6 20.7 %mlp_products.5 = (bf16[2048,512]{1,0:T(8,128)(2,1)}, bf16[2048,1024]{1,0:T(8,128)(2,1)}) custom-call(bf16[1024,2048]{1,0:T(8,128)(2,1)} %constant_dynamic-update-slice_fusion.15.refs_0_, bf16[1024,2048]{1,0:T(8,128)(2,1)} %collective-permute-done.28.refs_1_, bf16[1024,2048]{1,0:T(8,128)(2,1)} %constant_dynamic-update-slice_fusion.10.refs_2_.refs_4_, ...), custom_call_target="tpu_custom_call" | custom-call | flops 257698032 | bytes 587202 | tf_op jit(solution)/shard_map/mlp_products/pallas_call | solution.py:224
  496.3 24.7 %whole_sums.2 = bf16[2048,2048]{1,0:T(8,128)(2,1)} custom-call(s32[8]{0:T(128)} %shift-left_or_fusion.place_ref, bf16[2048,1024]{1,0:T(8,128)(2,1)} %get-tuple-element.202.refs_0_.refs_4_.refs_5_, bf16[2048,1024]{1,0:T(8,128)(2,1)} %get-tuple-element.203.refs_1_.refs_4_.refs_5_, bf16[2048,1024]{1,0:T(8,128)(2,1)} %all-gather.13.cloned.1.call-done.refs_4_.refs_2_, ...), custom_call_target="tpu_custom_call" | custom-call | flops 343597376 | bytes 503316 | tf_op jit(solution)/shard_map/whole_sums/pallas_call | solution.py:428
  521.2 21.4 %mlp_products.6 = (bf16[2048,512]{1,0:T(8,128)(2,1)}, bf16[2048,1024]{1,0:T(8,128)(2,1)}) custom-call(bf16[1024,2048]{1,0:T(8,128)(2,1)} %constant_dynamic-update-slice_fusion.25.refs_0_.refs_2_, bf16[1024,2048]{1,0:T(8,128)(2,1)} %collective-permute-done.42.refs_1_.refs_3_, bf16[1024,2048]{1,0:T(8,128)(2,1)} %constant_dynamic-update-slice_fusion.20.refs_2_.refs_6_, ...), custom_call_target="tpu_custom_call" | custom-call | flops 257698032 | bytes 587202 | tf_op jit(solution)/shard_map/mlp_products/pallas_call | solution.py:224
  542.6 21.1 %mlp_products.7 = (bf16[2048,512]{1,0:T(8,128)(2,1)}, bf16[2048,1024]{1,0:T(8,128)(2,1)}) custom-call(bf16[1024,2048]{1,0:T(8,128)(2,1)} %constant_dynamic-update-slice_fusion.25.refs_0_.refs_2_, bf16[1024,2048]{1,0:T(8,128)(2,1)} %collective-permute-done.42.refs_1_.refs_3_, bf16[1024,2048]{1,0:T(8,128)(2,1)} %constant_dynamic-update-slice_fusion.20.refs_2_.refs_6_, ...), custom_call_target="tpu_custom_call" | custom-call | flops 257698032 | bytes 587202 | tf_op jit(solution)/shard_map/mlp_products/pallas_call | solution.py:224
  563.7 24.8 %whole_sums.3 = bf16[2048,2048]{1,0:T(8,128)(2,1)} custom-call(s32[8]{0:T(128)} %shift-left_or_fusion.place_ref, bf16[2048,1024]{1,0:T(8,128)(2,1)} %get-tuple-element.209.refs_0_.refs_6_.refs_7_, bf16[2048,1024]{1,0:T(8,128)(2,1)} %get-tuple-element.210.refs_1_.refs_6_.refs_7_, bf16[2048,1024]{1,0:T(8,128)(2,1)} %all-gather.13.cloned.1.call-done.refs_4_.refs_2_, ...), custom_call_target="tpu_custom_call" | custom-call | flops 343597376 | bytes 503316 | tf_op jit(solution)/shard_map/whole_sums/pallas_call | solution.py:428
  599.0 25.7 %weight_grad.6 = bf16[2048,1024]{1,0:T(8,128)(2,1)} custom-call(bf16[1024,2048]{1,0:T(8,128)(2,1)} %constant_dynamic-update-slice_fusion.15.refs_0_, bf16[1024,2048]{1,0:T(8,128)(2,1)} %collective-permute-done.28.refs_1_, bf16[1024,2048]{1,0:T(8,128)(2,1)} %constant_dynamic-update-slice_fusion.25.refs_0_.refs_2_, ...), custom_call_target="tpu_custom_call" | custom-call | flops 343597376 | bytes 503316 | tf_op jit(solution)/shard_map/weight_grad/pallas_call | solution.py:473
  631.6 24.5 %weight_grad.7 = bf16[2048,1024]{1,0:T(8,128)(2,1)} custom-call(bf16[1024,2048]{1,0:T(8,128)(2,1)} %constant_dynamic-update-slice_fusion.15.refs_0_, bf16[1024,2048]{1,0:T(8,128)(2,1)} %collective-permute-done.28.refs_1_, bf16[1024,2048]{1,0:T(8,128)(2,1)} %constant_dynamic-update-slice_fusion.25.refs_0_.refs_2_, ...), custom_call_target="tpu_custom_call" | custom-call | flops 343597376 | bytes 503316 | tf_op jit(solution)/shard_map/weight_grad/pallas_call | solution.py:473
  695.8 29.4 %attend_backward.2.refs_0_.refs_4_.refs_5_ = bf16[2048,768]{1,0:T(8,128)(2,1)} custom-call(s32[8]{0:T(128)} %and_select_fusion.3.low_ref, s32[8]{0:T(128)} %shift-left_or_fusion.place_ref, s32[8,1,256]{2,1,0:T(1,128)} %bitcast.87, bf16[2048,768]{1,0:T(8,128)(2,1)} %project_qkv.2.qkv_ref, bf16[2048,256]{1,0:T(8,128)(2,1)} %get-tuple-element.268.refs_0_.att_ref.refs_1_, ...), custom_call_target="tpu_custom_call" | custom-call | flops 286331072 | bytes 209715 | tf_op jit(solution)/shard_map/attend_backward/pallas_call | solution.py:661
  756.3 15.3 %weight_grad.8 = bf16[512,2048]{1,0:T(8,128)(2,1)} custom-call(bf16[2048,512]{1,0:T(8,128)(2,1)} %get-tuple-element.233.refs_0_.refs_1_, bf16[2048,512]{1,0:T(8,128)(2,1)} %get-tuple-element.233.refs_0_.refs_1_, bf16[2048,512]{1,0:T(8,128)(2,1)} %get-tuple-element.241.refs_0_.refs_2_.refs_3_, bf16[2048,512]{1,0:T(8,128)(2,1)} %get-tuple-element.241.refs_0_.refs_2_.refs_3_, ...), custom_call_target="tpu_custom_call" | custom-call | flops 171798688 | bytes 503316 | tf_op jit(solution)/shard_map/weight_grad/pallas_call | solution.py:473
  814.4 34.7 %attend_backward.3.refs_0_.refs_6_.refs_7_ = bf16[2048,768]{1,0:T(8,128)(2,1)} custom-call(s32[8]{0:T(128)} %and_select_fusion.low_ref, s32[8]{0:T(128)} %shift-left_or_fusion.place_ref, s32[8,1,256]{2,1,0:T(1,128)} %bitcast.84, bf16[2048,768]{1,0:T(8,128)(2,1)} %project_qkv.3.qkv_ref, bf16[2048,256]{1,0:T(8,128)(2,1)} %get-tuple-element.178.refs_0_.att_ref.refs_2_.refs_3_, ...), custom_call_target="tpu_custom_call" | custom-call | flops 286331072 | bytes 209715 | tf_op jit(solution)/shard_map/attend_backward/pallas_call | solution.py:661
  865.1 19.3 %weight_grad.9 = bf16[2048,768]{1,0:T(8,128)(2,1)} custom-call(bf16[1024,2048]{1,0:T(8,128)(2,1)} %constant_dynamic-update-slice_fusion.refs_0_, bf16[1024,2048]{1,0:T(8,128)(2,1)} %collective-permute-done.7.refs_1_, bf16[1024,2048]{1,0:T(8,128)(2,1)} %constant_dynamic-update-slice_fusion.5.refs_0_.refs_2_, ...), custom_call_target="tpu_custom_call" | custom-call | flops 257698032 | bytes 461373 | tf_op jit(solution)/shard_map/weight_grad/pallas_call | solution.py:473
  886.6 23.7 %collective-permute-done.64 = bf16[256,2048]{1,0:T(8,128)(2,1)S(1)} collective-permute-done((bf16[256,2048]{1,0:T(8,128)(2,1)}, bf16[256,2048]{1,0:T(8,128)(2,1)S(1)}, u32[]{:S(2)}, u32[]{:S(2)}) %collective-permute-start.64) | collective-permute-done | bytes 1048608 | tf_op jit(solution)/shard_map/ppermute | solution.py:89
  977.3 15.5 %weight_grad.11 = bf16[512,2048]{1,0:T(8,128)(2,1)} custom-call(bf16[2048,512]{1,0:T(8,128)(2,1)} %get-tuple-element.269.refs_1_.refs_0_, bf16[2048,512]{1,0:T(8,128)(2,1)} %get-tuple-element.269.refs_1_.refs_0_, bf16[2048,512]{1,0:T(8,128)(2,1)} %get-tuple-element.208.refs_1_.refs_2_.refs_3_, bf16[2048,512]{1,0:T(8,128)(2,1)} %get-tuple-element.208.refs_1_.refs_2_.refs_3_, ...), custom_call_target="tpu_custom_call" | custom-call | flops 171798688 | bytes 503316 | tf_op jit(solution)/shard_map/weight_grad/pallas_call | solution.py:473
  1040.8 26.6 %reduce-scatter.23.cloned.1.call-done = bf16[512,512]{1,0:T(8,128)(2,1)} async-done(((bf16[512,2048]{1,0:T(8,128)(2,1)}), bf16[512,512]{1,0:T(8,128)(2,1)}) %reduce-scatter.23.cloned.1.call-update) | async-done | bytes 524304 | tf_op jit(solution)/shard_map/reduce_scatter | solution.py:840
  (489 shorter events, 516.3 us)
Async XLA Ops:
  7.2 79.7 %all-gather.7.cloned.1.call-start = ((), (), s32[]{:S(2)}) async-start(), calls=%async_computation.8 | async-start | bytes 3932160 | tf_op jit(solution)/shard_map/all_gather | solution.py:738
  26.9 90.1 %all-gather.9.cloned.1.call-start = ((), (), s32[]{:S(2)}) async-start(), calls=%async_computation.9 | async-start | bytes 1310720 | tf_op jit(solution)/shard_map/all_gather | solution.py:738
  61.6 142.0 %all-gather.11.cloned.1.call-start = ((), (), s32[]{:S(2)}) async-start(), calls=%async_computation.10 | async-start | bytes 2621440 | tf_op jit(solution)/shard_map/all_gather | solution.py:738
  152.8 50.7 %collective-permute-start.13 = (bf16[1024,2048]{1,0:T(8,128)(2,1)}, bf16[1024,2048]{1,0:T(8,128)(2,1)}, u32[]{:S(2)}, u32[]{:S(2)}) collective-permute-start(bf16[1024,2048]{1,0:T(8,128)(2,1)} %partial_sums.12), channel_id=1, source_target_pairs={{0,1},{1,0},{2,3},{3,2},{4,5},{5,4},{6,7},{7,6},{8,9},{9,8},{10,11... | collective-permute-start | bytes 12582920 | tf_op jit(solution)/shard_map/ppermute | solution.py:89
  155.2 129.8 %all-gather.13.cloned.1.call-start = ((), (), s32[]{:S(2)}) async-start(), calls=%async_computation.11 | async-start | bytes 5242880 | tf_op jit(solution)/shard_map/all_gather | solution.py:738
  160.1 43.5 %collective-permute-start.14 = (bf16[256,2048]{1,0:T(8,128)(2,1)}, bf16[256,2048]{1,0:T(8,128)(2,1)}, u32[]{:S(2)}, u32[]{:S(2)}) collective-permute-start(bf16[256,2048]{1,0:T(8,128)(2,1)} %get-tuple-element.157), channel_id=1, source_target_pairs={{0,2},{1,3},{2,0},{3,1},{4,6},{5,7},{6,4},{7,5},{8,10},{9,11},{10,... | collective-permute-start | bytes 3145736 | tf_op jit(solution)/shard_map/ppermute | solution.py:89
  163.8 214.6 %all-gather.15.cloned.1.call-start = ((), (), s32[]{:S(2)}) async-start(), calls=%async_computation.12 | async-start | bytes 2621440 | tf_op jit(solution)/shard_map/all_gather | solution.py:738
  334.7 43.7 %collective-permute-start.28 = (bf16[1024,2048]{1,0:T(8,128)(2,1)}, bf16[1024,2048]{1,0:T(8,128)(2,1)}, u32[]{:S(2)}, u32[]{:S(2)}) collective-permute-start(bf16[1024,2048]{1,0:T(8,128)(2,1)} %constant_dynamic-update-slice_fusion.15.refs_0_), channel_id=1, source_target_pairs={{0,1},{1,0},{2,3},{3,2},{4,5},{5,4},{6,7},{7,6},{8,9},{9,8},{10,11... | collective-permute-start | bytes 12582920 | tf_op jit(solution)/shard_map/ppermute | solution.py:89
  334.7 140.9 %all-gather.17.cloned.1.call-start = ((), (), s32[]{:S(2)}) async-start(), calls=%async_computation.13 | async-start | bytes 5242880 | tf_op jit(solution)/shard_map/all_gather | solution.py:738
  336.0 42.4 %collective-permute-start.30 = (bf16[256,2048]{1,0:T(8,128)(2,1)}, bf16[256,2048]{1,0:T(8,128)(2,1)}, u32[]{:S(2)}, u32[]{:S(2)}) collective-permute-start(bf16[256,2048]{1,0:T(8,128)(2,1)} %get-tuple-element.184), channel_id=1, source_target_pairs={{0,4},{1,5},{2,6},{3,7},{4,0},{5,1},{6,2},{7,3},{8,12},{9,13},{10,... | collective-permute-start | bytes 3145736 | tf_op jit(solution)/shard_map/ppermute | solution.py:89
  381.0 210.3 %reduce-scatter.9.cloned.1.call-start = ((), (), s32[]{:S(2)}) async-start(), calls=%async_computation.14 | async-start | bytes 9437184 | tf_op jit(solution)/shard_map/reduce_scatter | solution.py:858
  521.0 157.8 %reduce-scatter.11.cloned.1.call-start = ((), (), s32[]{:S(2)}) async-start(), calls=%async_computation.15 | async-start | bytes 9437184 | tf_op jit(solution)/shard_map/reduce_scatter | solution.py:858
  588.6 369.3 %reduce-scatter.17.cloned.1.call-start = ((), (), s32[]{:S(2)}) async-start(), calls=%async_computation.18 | async-start | bytes 5242880 | tf_op jit(solution)/shard_map/reduce_scatter | solution.py:840
  624.8 336.1 %reduce-scatter.19.cloned.1.call-start = ((), (), s32[]{:S(2)}) async-start(), calls=%async_computation.19 | async-start | bytes 5242880 | tf_op jit(solution)/shard_map/reduce_scatter | solution.py:840
  678.3 48.9 %collective-permute-start.50 = (bf16[1024,2048]{1,0:T(8,128)(2,1)}, bf16[1024,2048]{1,0:T(8,128)(2,1)}, u32[]{:S(2)}, u32[]{:S(2)}) collective-permute-start(bf16[1024,2048]{1,0:T(8,128)(2,1)} %partial_sums.16), channel_id=1, source_target_pairs={{0,1},{1,0},{2,3},{3,2},{4,5},{5,4},{6,7},{7,6},{8,9},{9,8},{10,11... | collective-permute-start | bytes 12582920 | tf_op jit(solution)/shard_map/ppermute | solution.py:89
  678.7 48.5 %collective-permute-start.51 = (bf16[1024,2048]{1,0:T(8,128)(2,1)}, bf16[1024,2048]{1,0:T(8,128)(2,1)}, u32[]{:S(2)}, u32[]{:S(2)}) collective-permute-start(bf16[1024,2048]{1,0:T(8,128)(2,1)} %partial_sums.17), channel_id=1, source_target_pairs={{0,1},{1,0},{2,3},{3,2},{4,5},{5,4},{6,7},{7,6},{8,9},{9,8},{10,11... | collective-permute-start | bytes 12582920 | tf_op jit(solution)/shard_map/ppermute | solution.py:89
  684.9 40.3 %collective-permute-start.49 = (bf16[256,2048]{1,0:T(8,128)(2,1)}, bf16[256,2048]{1,0:T(8,128)(2,1)S(1)}, u32[]{:S(2)}, u32[]{:S(2)}) collective-permute-start(bf16[256,2048]{1,0:T(8,128)(2,1)} %get-tuple-element.223), channel_id=1, source_target_pairs={{0,4},{1,5},{2,6},{3,7},{4,0},{5,1},{6,2},{7,3},{8,12},{9,13},{10,... | collective-permute-start | bytes 3145736 | tf_op jit(solution)/shard_map/ppermute | solution.py:89
  687.0 38.3 %collective-permute-start.48 = (bf16[256,2048]{1,0:T(8,128)(2,1)}, bf16[256,2048]{1,0:T(8,128)(2,1)}, u32[]{:S(2)}, u32[]{:S(2)}) collective-permute-start(bf16[256,2048]{1,0:T(8,128)(2,1)} %get-tuple-element.223), channel_id=1, source_target_pairs={{0,2},{1,3},{2,0},{3,1},{4,6},{5,7},{6,4},{7,5},{8,10},{9,11},{10,... | collective-permute-start | bytes 3145736 | tf_op jit(solution)/shard_map/ppermute | solution.py:89
  687.9 348.2 %reduce-scatter.13.cloned.1.call-start = ((), (), s32[]{:S(2)}) async-start(), calls=%async_computation.16 | async-start | bytes 3932160 | tf_op jit(solution)/shard_map/reduce_scatter | solution.py:840
  805.1 43.9 %collective-permute-start.61 = (bf16[256,2048]{1,0:T(8,128)(2,1)}, bf16[256,2048]{1,0:T(8,128)(2,1)}, u32[]{:S(2)}, u32[]{:S(2)}) collective-permute-start(bf16[256,2048]{1,0:T(8,128)(2,1)} %get-tuple-element.251), channel_id=1, source_target_pairs={{0,4},{1,5},{2,6},{3,7},{4,0},{5,1},{6,2},{7,3},{8,12},{9,13},{10,... | collective-permute-start | bytes 3145736 | tf_op jit(solution)/shard_map/ppermute | solution.py:89
  806.5 43.7 %collective-permute-start.60 = (bf16[256,2048]{1,0:T(8,128)(2,1)}, bf16[256,2048]{1,0:T(8,128)(2,1)}, u32[]{:S(2)}, u32[]{:S(2)}) collective-permute-start(bf16[256,2048]{1,0:T(8,128)(2,1)} %get-tuple-element.249), channel_id=1, source_target_pairs={{0,2},{1,3},{2,0},{3,1},{4,6},{5,7},{6,4},{7,5},{8,10},{9,11},{10,... | collective-permute-start | bytes 3145736 | tf_op jit(solution)/shard_map/ppermute | solution.py:89
  884.4 154.6 %reduce-scatter.15.cloned.1.call-start = ((), (), s32[]{:S(2)}) async-start(), calls=%async_computation.17 | async-start | bytes 1310720 | tf_op jit(solution)/shard_map/reduce_scatter | solution.py:840
  937.5 103.3 %reduce-scatter.21.cloned.1.call-start = ((), (), s32[]{:S(2)}) async-start(), calls=%async_computation.20 | async-start | bytes 2621440 | tf_op jit(solution)/shard_map/reduce_scatter | solution.py:840
  943.8 123.6 %reduce-scatter.23.cloned.1.call-start = ((), (), s32[]{:S(2)}) async-start(), calls=%async_computation.21 | async-start | bytes 2621440 | tf_op jit(solution)/shard_map/reduce_scatter | solution.py:840
  (127 other events, 2126.9 us)
Sparse Core Ops, SparseCore 0:
  27.0 59.8 all-gather.6
  88.4 26.5 all-gather.8
  155.4 48.1 all-gather.10
  205.6 79.4 all-gather.12
  334.8 43.5 all-gather.14
  381.1 78.5 all-gather.16
  521.1 70.1 reduce-scatter.8
  595.1 83.3 reduce-scatter.10
  680.8 76.7 reduce-scatter.16
  759.8 77.2 reduce-scatter.18
  884.5 63.1 reduce-scatter.12
  949.9 27.1 reduce-scatter.14
  979.5 42.5 reduce-scatter.20
  1024.2 43.2 reduce-scatter.22

commit v2 on v1

--- a/solution.py
+++ b/solution.py
@@ -71,6 +71,10 @@
     def __init__(self):
         self.now = []
         self.then = []
+        self.waiting = []
+
+    def later(self, action):
+        self.waiting.append(action)
 
     def gate(self, value):
         return after(value, *self.now)
@@ -82,6 +86,9 @@
     def turn(self):
         self.now = self.then or self.now
         self.then = []
+        waiting, self.waiting = self.waiting, []
+        for action in waiting:
+            action()
 
     def swap(self, block, bit, axis="wide", hold=True):
         count = lax.axis_size(axis)
@@ -117,16 +124,39 @@
         self.halves = [own, self.slots.swap(own, 0)]
 
 
+class Offloaded:
+    def __init__(self, slots, block):
+        self.slots = slots
+        count = lax.axis_size("wide")
+        groups = [list(range(core, count, 2)) for core in range(2)]
+        self.chips = lax.all_gather(
+            slots.gate(block), "wide", axis_index_groups=groups, axis=0, tiled=True
+        )
+
+    def core(self):
+        chips = lax.axis_size("wide") // 2
+        rows = self.chips.shape[0] // chips
+        here = lax.axis_index("wide") // 2
+        own = jnp.concatenate(
+            [
+                lax.dynamic_slice_in_dim(self.chips, (here ^ chip) * rows, rows)
+                for chip in range(chips)
+            ],
+            axis=0,
+        )
+        self.halves = [own, self.slots.swap(own, 0)]
+
+
 class Scatter:
-    def __init__(self, slots, lefts, rights, dims):
+    def __init__(self, slots, lefts, rights):
         self.slots = slots
-        self.factors = (lefts, rights, dims)
+        self.factors = (lefts, rights)
         self.sent = self.product(1)
 
     def product(self, side, got=None):
-        lefts, rights, dims = self.factors
+        lefts, rights = self.factors
         lefts = [self.slots.gate(lefts[0])] + list(lefts[1:])
-        made = partial_sums(lefts, rights, dims, side, got)
+        made = partial_sums(lefts, rights, side, got)
         self.slots.ends(made[0] if isinstance(made, (list, tuple)) else made)
         return made
 
@@ -148,15 +178,15 @@
             kept = (kept[:rows].astype(F32) + got.astype(F32)).astype(BF16)
         self.total = kept.astype(F32)
 
-    def last(self):
+    def last(self, hold=True):
         if not isinstance(self.kept, (tuple, list)):
             return
         keep_low, keep_high = self.kept[:2]
         half = keep_low.shape[0] // 2
         far_low = (keep_low[half:].astype(F32) + self.got_x[half:].astype(F32)).astype(BF16)
         far_high = (keep_high[half:].astype(F32) + self.got_y[half:].astype(F32)).astype(BF16)
-        low = self.slots.swap(far_low, 2)
-        high = self.slots.swap(far_high, 1)
+        low = self.slots.swap(far_low, 2, hold=hold)
+        high = self.slots.swap(far_high, 1, hold=hold)
         low = keep_low[:half].astype(F32) + self.got_x[:half].astype(F32) + low.astype(F32)
         high = keep_high[:half].astype(F32) + self.got_y[:half].astype(F32) + high.astype(F32)
         self.total = jnp.concatenate([low, high], axis=0)
@@ -236,12 +266,23 @@
             transcendentals=0,
         ),
         name=name,
-    )(*[piece for pieces in streams for piece in pieces], *ins)
-
-
-def resident(array):
-    shape = array.shape
-    return pl.BlockSpec(shape, lambda i: (0,) * len(shape), pipeline_mode=pl.Buffered(1))
+    )(
+        *[piece for pieces in streams for piece in pieces],
+        *[part.array if isinstance(part, Columns) else part for part in ins],
+    )
+
+
+class Columns:
+    def __init__(self, array, width, index):
+        self.array = array
+        self.index = index
+        self.shape = (array.shape[0], width)
+
+
+def resident(part):
+    return pl.BlockSpec(
+        part.shape, lambda i, *_: (0, part.index), pipeline_mode=pl.Buffered(1)
+    )
 
 
 def by_rows(rows, cols):
@@ -280,10 +321,10 @@
 
 def pull_back_out(tokens, w_out):
     seq = sum(piece.shape[0] for piece in tokens)
-    width, dim = w_out.shape
+    dim, width = w_out.shape
 
     def body(x_ref, w_ref, out_ref):
-        out_ref[...] = dot(x_ref[...], w_ref[...], NT).astype(BF16)
+        out_ref[...] = dot(x_ref[...], w_ref[...]).astype(BF16)
 
     return streaming_call(
         [tokens],
@@ -301,7 +342,7 @@
 def mlp_body(x_ref, gy_ref, gu_ref, down_ref, hid_ref, dgu_ref):
     cols = hid_ref.shape[1]
     both = dot(x_ref[...], gu_ref[...])
-    d_hid = dot(gy_ref[...], down_ref[...], NT)
+    d_hid = dot(gy_ref[...], down_ref[...])
     gp = both[:, :cols]
     up = both[:, cols:]
     sig = jax.nn.sigmoid(gp)
@@ -313,7 +354,7 @@
 
 def mlp_products(tokens, gy, w_gu, w_down):
     seq = sum(piece.shape[0] for piece in tokens)
-    cols, dim = w_down.shape
+    dim, cols = w_down.shape
     return streaming_call(
         [tokens, gy],
         mlp_body,
@@ -327,9 +368,9 @@
     )
 
 
-def partial_sums(lefts, rights, dims, side, got=None):
+def partial_sums(lefts, rights, side, got=None):
     seq = lefts[0].shape[0]
-    dim = rights[0].shape[1] if dims == NN else rights[0].shape[0]
+    dim = rights[0].shape[0]
     rows = seq // 2
     count = len(lefts)
     wide = lax.axis_size("wide")
@@ -342,7 +383,7 @@
     def kernel(*refs):
         total = None
         for left, right in zip(refs[:count], refs[count : 2 * count]):
-            term = dot(left[...], right[...], dims)
+            term = dot(left[...], right[...], NT)
             total = term if total is None else total + term
         if got is None:
             refs[-1][...] = total.astype(BF16)
@@ -375,7 +416,7 @@
     in_specs = [
         pl.BlockSpec((block, left.shape[1]), lambda i: (side * steps + i, 0)) for left in lefts
     ] + [resident(right) for right in rights]
-    ins = list(lefts) + list(rights)
+    ins = list(lefts) + [right.array for right in rights]
     if got is not None:
         in_specs.append(by_rows(block, dim))
         ins.append(got)
@@ -407,9 +448,9 @@
     )(*ins)
 
 
-def whole_sums(lefts, rights, dims, place):
+def whole_sums(lefts, rights, place):
     seq = lefts[0].shape[0]
-    dim = rights[0].shape[1] if dims == NN else rights[0].shape[0]
+    dim = rights[0].shape[0]
     chunks = place.shape[0]
     block = seq // chunks
     count = len(lefts)
@@ -417,12 +458,9 @@
     def kernel(place_ref, *refs):
         total = None
         for left, right in zip(refs[:count], refs[count : 2 * count]):
-            term = dot(left[...], right[...], dims)
+            term = dot(left[...], right[...], NT)
             total = term if total is None else total + term
         refs[-1][...] = total.astype(BF16)
-
-    def whole(array):
-        return pl.BlockSpec(array.shape, lambda i, at: (0, 0), pipeline_mode=pl.Buffered(1))
 
     depth = sum(left.shape[1] for left in lefts)
     return pl.pallas_call(
@@ -434,7 +472,7 @@
             in_specs=[
                 pl.BlockSpec((block, left.shape[1]), lambda i, at: (at[i], 0)) for left in lefts
             ]
-            + [whole(right) for right in rights],
+            + [resident(right) for right in rights],
             out_specs=pl.BlockSpec((block, dim), lambda i, at: (i, 0)),
         ),
         compiler_params=params_for(),
@@ -444,7 +482,7 @@
             transcendentals=0,
         ),
         name="whole_sums",
-    )(place, *lefts, *rights)
+    )(place, *lefts, *[right.array for right in rights])
 
 
 def halves(array):
@@ -453,7 +491,7 @@
     return [(array, 0), (array, 1)]
 
 
-def weight_grad(lefts, rights, seq):
+def weight_grad(lefts, rights, seq, before=None, parts=1):
     seq //= 2
     lefts = [pair for left in lefts for pair in halves(left)]
     rights = [pair for right in rights for pair in halves(right)]
@@ -462,6 +500,7 @@
     tall = min(512 if height < 1024 else 256, height)
     wide = min(1024, cols)
     count = len(lefts)
+    first = 0 if before is None else (parts - 1) * height // tall
 
     def kernel(*refs):
         total = None
@@ -472,11 +511,13 @@
 
     return pl.pallas_call(
         kernel,
-        out_shape=jax.ShapeDtypeStruct((height, cols), BF16),
+        out_shape=jax.ShapeDtypeStruct((parts * height, cols), BF16),
         grid=(cols // wide, height // tall),
         in_specs=[pl.BlockSpec((seq, tall), lambda n, m, p=p: (p, m)) for _, p in lefts]
-        + [pl.BlockSpec((seq, wide), lambda n, m, p=p: (p, n)) for _, p in rights],
-        out_specs=pl.BlockSpec((tall, wide), lambda n, m: (m, n)),
+        + [pl.BlockSpec((seq, wide), lambda n, m, p=p: (p, n)) for _, p in rights]
+        + [pl.BlockSpec(memory_space=pl.ANY)] * (before is not None),
+        out_specs=pl.BlockSpec((tall, wide), lambda n, m: (m + first, n)),
+        input_output_aliases={} if before is None else {2 * count: 0},
         compiler_params=params_for(),
         cost_estimate=cost(
             flops=2 * seq * height * cols * count,
@@ -484,7 +525,11 @@
             transcendentals=0,
         ),
         name="weight_grad",
-    )(*[a for a, _ in lefts], *[a for a, _ in rights])
+    )(
+        *[a for a, _ in lefts],
+        *[a for a, _ in rights],
+        *([] if before is None else [before]),
+    )
 
 
 def head_stack(block, heads):
@@ -754,26 +799,39 @@
     hidden = w_gate.shape[1]
     cut = hidden // 2
     spans = [slice(0, cut), slice(cut, hidden)]
-    w_qkv = fetch(jnp.concatenate([w_query, w_key, w_value], axis=1), 0)
-    full_out = fetch(w_out, 1)
-    full_gu, full_down = [], []
-    for span in spans:
-        full_gu.append(fetch(jnp.concatenate([w_gate[:, span], w_up[:, span]], axis=1), 0))
-        full_down.append(fetch(w_down[span], 1))
+    first_own = jnp.concatenate([w_query, w_key, w_value, w_out.T], axis=1)
+    first_set = fetch(first_own, 0)
+    w_qkv = Columns(first_set, 3 * width, 0)
+    full_out = Columns(first_set, width, 3)
+    ffn_sets, full_gu, full_down = [], [], []
+
+    def lay_out():
+        for span in spans:
+            own = [gate(w_gate)[:, span], gate(w_up)[:, span], gate(w_down)[span].T]
+            own = ends(jnp.concatenate(own, axis=1))
+            ffn_sets.append(fetch(own, 0))
+            full_gu.append(Columns(ffn_sets[-1], 2 * cut, 0))
+            full_down.append(Columns(ffn_sets[-1], cut, 2))
+
 
     rows = range(rows_here)
     last = rows_here - 1
-    facts = [row_facts(doc_lengths[r], seq) for r in rows]
+    facts = {}
     residual = [hidden_in[r].astype(F32) for r in rows]
     inv_first = [norm_scale(residual[r]) for r in rows]
     normed = [residual[r] * inv_first[r] for r in rows]
     scaled_in = [(normed[r] * attn_scale).astype(BF16) for r in rows]
 
     attn_in, gy, mlp_in, branch = {}, {}, {}, {}
-    qkv, att, lse, middle, inv_second, normed_mid = ({} for _ in range(6))
+    qkv, att, lse, middle, inv_second = ({} for _ in range(5))
     grad_middle, gain_mlp, gain_attn, outputs, in_grads, d_qkv = ({} for _ in range(6))
     hid = {r: [] for r in rows}
     d_gu = {r: [] for r in rows}
+
+    def know(r):
+        facts[r] = row_facts(gate(doc_lengths[r]), seq)
+        ends(facts[r][3])
+        ends(facts[r][4])
 
     def first_of(halves):
         return [gate(halves[0])] + list(halves[1:])
@@ -787,15 +845,13 @@
         att[r], lse[r] = attend_forward(gate(qkv[r]), low, place, begins, heads)
         ends(att[r])
 
-    def spread(lefts, rights, dims):
-        return Scatter(slots, lefts, rights, dims)
+    def spread(lefts, rights):
+        return Scatter(slots, lefts, rights)
 
     def after_attention(r, total):
-        total = gate(total)
-        middle[r] = residual[r] + total
+        middle[r] = gate(hidden_in[r]).astype(F32) + total
         inv_second[r] = norm_scale(middle[r])
-        normed_mid[r] = middle[r] * inv_second[r]
-        mlp_in[r] = Gather(slots, (normed_mid[r] * mlp_scale).astype(BF16))
+        mlp_in[r] = Gather(slots, (middle[r] * inv_second[r] * mlp_scale).astype(BF16))
 
     def mlp(r, part):
         one, two = mlp_products(
@@ -806,11 +862,12 @@
         d_gu[r].append(two)
 
     def after_mlp(r, total):
-        total = gate(total)
-        gain_mlp[r] = jnp.sum(total * normed_mid[r], axis=0)
+        total = gate(total).astype(F32)
+        normed_mid = gate(middle[r]) * inv_second[r]
+        gain_mlp[r] = jnp.sum(total * normed_mid, axis=0)
         scaled = total * mlp_scale
         grad_middle[r] = out_grad[r].astype(F32) + inv_second[r] * (
-            scaled - normed_mid[r] * jnp.mean(scaled * normed_mid[r], axis=-1, keepdims=True)
+            scaled - normed_mid * jnp.mean(scaled * normed_mid, axis=-1, keepdims=True)
         )
         branch[r] = Gather(slots, grad_middle[r].astype(BF16))
 
@@ -824,20 +881,32 @@
         )
 
     def after_back(r, total):
-        total = gate(total)
-        gain_attn[r] = jnp.sum(total * normed[r], axis=0)
+        normed_in = gate(hidden_in[r]).astype(F32) * inv_first[r]
+        gain_attn[r] = jnp.sum(total * normed_in, axis=0)
         scaled = total * attn_scale
         in_grads[r] = (
             grad_middle[r]
             + inv_first[r]
-            * (scaled - normed[r] * jnp.mean(scaled * normed[r], axis=-1, keepdims=True))
+            * (scaled - normed_in * jnp.mean(scaled * normed_in, axis=-1, keepdims=True))
         ).astype(BF16)
 
-    def grad_of(lefts, rights, axis):
+    def grad_factors(lefts, rights):
         lefts = [lefts[r] for r in rows]
         lefts[0] = first_of(lefts[0]) if isinstance(lefts[0], list) else gate(lefts[0])
-        grad = ends(weight_grad(lefts, [rights[r] for r in rows], seq))
-        return lax.psum_scatter(grad, "narrow", scatter_dimension=axis, tiled=True).astype(F32)
+        return lefts, [rights[r] for r in rows]
+
+    def grad_of(lefts, rights, table, key, wait=True, axis=0):
+        grad = ends(weight_grad(*grad_factors(lefts, rights), seq))
+
+        def start():
+            table[key] = lax.psum_scatter(
+                gate(grad) if wait else grad, "narrow", scatter_dimension=axis, tiled=True
+            )
+
+        if wait:
+            slots.later(start)
+        else:
+            start()
 
     def both(table):
         return [table[r] for r in rows]
@@ -848,92 +917,109 @@
     def part_of(table, part):
         return {r: table[r][part] for r in rows}
 
-    sums, down, grad_gu, grad_down = {}, {}, [None, None], [None, None]
+    sums, down, grad_gu, grad_down, grad_attn = {}, {}, [None, None], [None, None], {}
 
     def out_sum(r):
-        sums[r] = spread([att[r]], [full_out], NN)
+        sums[r] = spread([att[r]], [full_out])
 
     def mlp_sum(r):
-        whole = ends(whole_sums(first_of(d_gu[r]), full_gu, NT, facts[r][1]))
-        sums[r] = lax.psum_scatter(whole, "wide", scatter_dimension=0, tiled=True).astype(F32)
+        whole = ends(whole_sums(first_of(d_gu[r]), full_gu, facts[r][1]))
+
+        def start():
+            sums[r] = lax.psum_scatter(gate(whole), "wide", scatter_dimension=0, tiled=True)
+
+        slots.later(start)
 
     def back_sum(r):
-        sums[r] = spread([d_qkv[r]], [w_qkv], NT)
+        sums[r] = spread([d_qkv[r]], [w_qkv])
 
     def down_sum(r):
-        down[r] = spread(hid[r], full_down, NN)
+        down[r] = spread(hid[r], full_down)
 
     def gu_grad(part):
-        grad_gu[part] = grad_of(halves_of(mlp_in), part_of(d_gu, part), 0)
+        grad_of(halves_of(mlp_in), part_of(d_gu, part), grad_gu, part)
 
     def down_grad(part):
-        grad_down[part] = grad_of(part_of(hid, part), halves_of(gy), 1)
+        factors = grad_factors(part_of(hid, part), halves_of(gy))
+        if part == 0:
+            grad_down[0] = ends(weight_grad(*factors, seq, None, 2))
+            return
+        grad = ends(weight_grad(*factors, seq, grad_down[0], 2))
+
+        def start():
+            grad_down[0] = lax.psum_scatter(
+                gate(grad), "narrow", scatter_dimension=1, tiled=True
+            )
+
+        slots.later(start)
 
     one, two = 0, last
     attn_in[one] = Gather(slots, scaled_in[one])
+    ends(first_own)
     turn()
     attn_in[one].far()
+    know(one)
+    lay_out()
     turn()
     attn_in[one].core()
-    ends(w_qkv)
+    attn_in[two] = Gather(slots, scaled_in[two])
+    know(two)
+    ends(first_set)
     turn()
     project(one)
-    attn_in[two] = Gather(slots, scaled_in[two])
-    ends(full_out)
+    attn_in[two].far()
     turn()
     attend(one)
-    attn_in[two].far()
+    attn_in[two].core()
+    gy[one] = Gather(slots, out_grad[one])
     turn()
     out_sum(one)
-    attn_in[two].core()
-    turn()
+    sums[one].core()
     project(two)
-    sums[one].core()
-    gy[one] = Gather(slots, out_grad[one])
-    ends(full_down[0])
+    gy[one].far()
     turn()
     sums[one].even()
-    gy[one].far()
+    gy[one].core()
+    gy[two] = Gather(slots, out_grad[two])
     turn()
     attend(two)
     sums[one].near()
-    gy[one].core()
+    ends(ffn_sets[0])
     turn()
     out_sum(two)
     sums[one].last()
-    ends(full_gu[0])
+    gy[two].far()
     turn()
     after_attention(one, sums[one].total)
     sums[two].core()
+    gy[two].core()
     turn()
     sums[two].even()
     mlp_in[one].far()
     turn()
     mlp_in[one].core()
     sums[two].near()
-    ends(full_down[1])
+    ends(ffn_sets[1])
     turn()
     mlp(one, 0)
     sums[two].last()
-    gy[two] = Gather(slots, out_grad[two])
-    turn()
+    turn()
+    mlp(one, 1)
     after_attention(two, sums[two].total)
-    gy[two].far()
-    turn()
+    turn()
+    mlp_sum(one)
     mlp_in[two].far()
-    gy[two].core()
-    ends(full_gu[1])
-    turn()
-    mlp(one, 1)
+    turn()
+    down_sum(one)
     mlp_in[two].core()
     turn()
-    mlp_sum(one)
-    turn()
     mlp(two, 0)
+    down[one].core()
     turn()
     mlp(two, 1)
     turn()
     mlp_sum(two)
+    ends(sums[one])
     turn()
     gu_grad(0)
     after_mlp(one, sums[one])
@@ -941,43 +1027,45 @@
     gu_grad(1)
     branch[one].far()
     turn()
-    down_sum(one)
     down_sum(two)
+    down[one].even()
     branch[one].core()
     turn()
     back_attention(one)
+    down[one].near()
+    down[two].core()
+    ends(sums[two])
+    turn()
+    back_sum(one)
+    down[two].even()
     after_mlp(two, sums[two])
-    down[one].core()
-    down[two].core()
-    turn()
-    back_sum(one)
-    down[one].even()
+    turn()
+    down_grad(0)
+    sums[one].core()
     branch[two].far()
-    turn()
-    down_grad(0)
+    down[one].last()
+    turn()
+    sums[one].even()
+    down_grad(1)
     branch[two].core()
-    sums[one].core()
-    down[one].near()
-    turn()
-    sums[one].even()
-    down[two].even()
-    down[one].last()
-    turn()
+    down[two].near()
+    ends(grad_gu[0])
+    turn()
+    grad_of(att, halves_of(branch), grad_attn, "out", axis=1)
     back_attention(two)
     sums[one].near()
+    down[two].last()
     turn()
     back_sum(two)
     sums[one].last()
-    turn()
-    grad_qkv = grad_of(halves_of(attn_in), d_qkv, 0)
+    ends(grad_gu[1])
+    turn()
     sums[two].core()
-    down[two].near()
     turn()
     sums[two].even()
-    down[two].last()
-    turn()
-    grad_out = grad_of(att, halves_of(branch), 1)
-    down_grad(1)
+    ends(grad_down[0])
+    turn()
+    grad_of(halves_of(attn_in), d_qkv, grad_attn, "qkv", False)
     sums[two].near()
     turn()
     sums[two].last()
@@ -986,34 +1074,33 @@
         outputs[r] = (middle[r] + down[r].total).astype(BF16)
         after_back(r, sums[r].total)
 
-    def spread_gain(parts):
-        total = sum(parts[1:], parts[0])
-        for axis in ("narrow", "wide"):
-            count = lax.axis_size(axis)
-            me = lax.axis_index(axis)
-            for bit in reversed(range(bits_of(count))):
-                size = total.shape[0] // 2
-                mine = (me >> bit) & 1
-                sent = lax.dynamic_slice_in_dim(total, (1 - mine) * size, size)
-                kept = lax.dynamic_slice_in_dim(total, mine * size, size)
-                pairs = [(i, i ^ (1 << bit)) for i in range(count)]
-                total = kept + lax.ppermute(sent, axis, pairs)
-        return total
-
+    gains = jnp.stack([sum(both(part)[1:], part[one]) for part in (gain_attn, gain_mlp)])
+    for axis in ("narrow", "wide"):
+        count = lax.axis_size(axis)
+        me = lax.axis_index(axis)
+        for bit in reversed(range(bits_of(count))):
+            size = gains.shape[1] // 2
+            mine = (me >> bit) & 1
+            sent = lax.dynamic_slice_in_dim(gains, (1 - mine) * size, size, 1)
+            kept = lax.dynamic_slice_in_dim(gains, mine * size, size, 1)
+            gains = kept + lax.ppermute(sent, axis, [(i, i ^ (1 << bit)) for i in range(count)])
+
+    grad_gu = [grad.astype(F32) for grad in grad_gu]
+    grad_attn = {key: grad.astype(F32) for key, grad in grad_attn.items()}
     grad_gate = [piece[:, :cut] for piece in grad_gu]
     grad_up = [piece[:, cut:] for piece in grad_gu]
     return (
         jnp.stack(both(outputs)),
         jnp.stack(both(in_grads)),
-        spread_gain(both(gain_attn)),
-        grad_qkv[:, :width],
-        grad_qkv[:, width : 2 * width],
-        grad_qkv[:, 2 * width :],
-        grad_out,
-        spread_gain(both(gain_mlp)),
+        gains[0],
+        grad_attn["qkv"][:, :width],
+        grad_attn["qkv"][:, width : 2 * width],
+        grad_attn["qkv"][:, 2 * width :],
+        grad_attn["out"],
+        gains[1],
         jnp.concatenate(grad_gate, axis=1),
         jnp.concatenate(grad_up, axis=1),
-        jnp.concatenate(grad_down, axis=0),
+        grad_down[0].astype(F32),
     )
 
 

time: 1090 us -> 968 us (0.89)
  waiting for transfers between devices: 310 us -> 201 us
  starting transfers between devices: 85.6 us -> 71.4 us
    all_gather x6 -> x3, waiting for transfers between devices: 81.4 us -> 24.6 us  [fetch(): return lax.all_gather(weight, 'narrow', axis=axis, tiled=True)]
    ppermute x70, waiting for transfers between devices: 181 us -> 147 us  [swap(): got = lax.ppermute(self.gate(block), axis, pairs)]
    reduce_scatter x8 -> x7, waiting for transfers between devices: 29.3 us -> 19.3 us  [the longest x4 19.3 us: start(): lax.psum_scatter(gate(grad) if wait else grad, 'narrow', scatter_dimensio...]
    unnamed x134 -> x163, local copies, waits for them, and re-layouts: 49.6 us -> 50.4 us
  transfers between devices with their start and end apart: 97 -> 88, of which waited for: 42 -> 32; matrix products, arithmetic and copies ran while one was open for 16% -> 17% of each run, Pallas kernels for 42% -> 50%
where the time goes in v2:
time: 968 us; the launch traced here: 959 us
  Pallas kernels  480 us (50%)
  waiting for transfers between devices  201 us (21%)
  other arithmetic  102 us (11%)
  local copies, waits for them, and re-layouts  89.2 us (9%)
  starting transfers between devices  71.4 us (7%)
  between operations  15.6 us (2%)
    ppermute x70, waiting for transfers between devices, swap(): got = lax.ppermute(self.gate(block), axis, pairs)  147 us
    pallas_call x8, Pallas kernels, streaming_call(): pl.pallas_call(kernel, out_shape=outs, grid=(steps,), in_specs=[pl.BlockS...  124 us
    pallas_call x6, Pallas kernels, weight_grad(): pl.pallas_call(kernel, out_shape=jax.ShapeDtypeStruct((parts * height, co...  111 us
    pallas_call x12, Pallas kernels, partial_sums(): pl.pallas_call(kernel, out_shape=out_shape, grid=(steps,), in_specs=in_sp...  93.2 us
    pallas_call x2, Pallas kernels, attend_backward(): pl.pallas_call(functools.partial(backward_kernel, heads, blocks, size), o...  63.8 us
    ppermute x70, starting transfers between devices, swap(): got = lax.ppermute(self.gate(block), axis, pairs)  59.6 us
    unnamed x163, local copies, waits for them, and re-layouts  50.4 us
    pallas_call x2, Pallas kernels, whole_sums(): pl.pallas_call(kernel, out_shape=jax.ShapeDtypeStruct((seq, dim), BF16),...  49.5 us
  transfers between devices with their start and end apart: 88, of which 32 were waited for; matrix products, arithmetic and copies ran while one was open for 17% of the time, Pallas kernels for 50%

profile of v2, /device:TPU:0, one launch (start us, length us, event | category | flops | bytes accessed | tf_op | source)
XLA Modules:
  0.0 959.4 jit_solution(6919614640298394470)
XLA Ops:
  28.4 17.8 %collective-permute-done.3 = bf16[256,2048]{1,0:T(8,128)(2,1)S(1)} collective-permute-done((bf16[256,2048]{1,0:T(8,128)(2,1)}, bf16[256,2048]{1,0:T(8,128)(2,1)S(1)}, u32[]{:S(2)}, u32[]{:S(2)}) %collective-permute-start.3) | collective-permute-done | bytes 1048608 | tf_op jit(solution)/shard_map/ppermute | solution.py:96
  80.0 16.0 %collective-permute-done.8 = bf16[256,2048]{1,0:T(8,128)(2,1)S(1)} collective-permute-done((bf16[256,2048]{1,0:T(8,128)(2,1)}, bf16[256,2048]{1,0:T(8,128)(2,1)S(1)}, u32[]{:S(2)}, u32[]{:S(2)}) %collective-permute-start.8) | collective-permute-done | bytes 1048608 | tf_op jit(solution)/shard_map/ppermute | solution.py:96
  113.9 12.8 %project_qkv.2.qkv_ref = bf16[2048,768]{1,0:T(8,128)(2,1)} custom-call(bf16[1024,2048]{1,0:T(8,128)(2,1)} %constant_dynamic-update-slice_fusion.refs_0_, bf16[1024,2048]{1,0:T(8,128)(2,1)} %collective-permute-done.9.refs_1_, bf16[2048,1024]{1,0:T(8,128)(2,1)} %all-gather.4.cloned.1.call-done.refs_2_.refs_1_, f32[2048,128]{1,0:T(8,128)} %pad_maximum_fusion.9.refs_3_.cos_ref, ...), custom_call_target="tpu_custom_call" | custom-call | flops 128849016 | bytes 293601 | tf_op jit(solution)/shard_map/project_qkv/pallas_call | solution.py:254
  133.4 17.4 %attend_forward.2 = (bf16[2048,256]{1,0:T(8,128)(2,1)}, f32[8,4,256]{2,1,0:T(4,128)}) custom-call(s32[8]{0:T(128)} %and_select_fusion.low_ref, s32[8]{0:T(128)} %shift-left_or_fusion.place_ref, s32[8,1,256]{2,1,0:T(1,128)} %bitcast.96, bf16[2048,768]{1,0:T(8,128)(2,1)} %project_qkv.2.qkv_ref), custom_call_target="tpu_custom_call" | custom-call | flops 114532432 | bytes 83886 | tf_op jit(solution)/shard_map/attend_forward/pallas_call | solution.py:599
  170.3 12.7 %project_qkv.3.qkv_ref = bf16[2048,768]{1,0:T(8,128)(2,1)} custom-call(bf16[1024,2048]{1,0:T(8,128)(2,1)} %constant_dynamic-update-slice_fusion.5.refs_0_.refs_2_, bf16[1024,2048]{1,0:T(8,128)(2,1)} %collective-permute-done.12.refs_1_.refs_3_, bf16[2048,1024]{1,0:T(8,128)(2,1)} %all-gather.4.cloned.1.call-done.refs_2_.refs_1_, ...), custom_call_target="tpu_custom_call" | custom-call | flops 128849016 | bytes 293601 | tf_op jit(solution)/shard_map/project_qkv/pallas_call | solution.py:254
  194.5 17.0 %collective-permute-done.20 = bf16[256,2048]{1,0:T(8,128)(2,1)S(1)} collective-permute-done((bf16[256,2048]{1,0:T(8,128)(2,1)S(1)}, bf16[256,2048]{1,0:T(8,128)(2,1)S(1)}, u32[]{:S(2)}, u32[]{:S(2)}) %collective-permute-start.20) | collective-permute-done | bytes 1048608 | tf_op jit(solution)/shard_map/ppermute | solution.py:96
  218.3 21.5 %attend_forward.3 = (bf16[2048,256]{1,0:T(8,128)(2,1)}, f32[8,4,256]{2,1,0:T(4,128)}) custom-call(s32[8]{0:T(128)} %and_select_fusion.1.low_ref, s32[8]{0:T(128)} %shift-left_or_fusion.place_ref, s32[8,1,256]{2,1,0:T(1,128)} %bitcast.93, bf16[2048,768]{1,0:T(8,128)(2,1)} %project_qkv.3.qkv_ref), custom_call_target="tpu_custom_call" | custom-call | flops 114532432 | bytes 83886 | tf_op jit(solution)/shard_map/attend_forward/pallas_call | solution.py:599
  280.8 23.5 %collective-permute-done.28 = bf16[256,2048]{1,0:T(8,128)(2,1)S(1)} collective-permute-done((bf16[256,2048]{1,0:T(8,128)(2,1)S(1)}, bf16[256,2048]{1,0:T(8,128)(2,1)S(1)}, u32[]{:S(2)}, u32[]{:S(2)}) %collective-permute-start.28) | collective-permute-done | bytes 1048608 | tf_op jit(solution)/shard_map/ppermute | solution.py:96
  324.4 24.2 %collective-permute-done.34 = bf16[256,2048]{1,0:T(8,128)(2,1)S(1)} collective-permute-done((bf16[256,2048]{1,0:T(8,128)(2,1)}, bf16[256,2048]{1,0:T(8,128)(2,1)S(1)}, u32[]{:S(2)}, u32[]{:S(2)}) %collective-permute-start.34) | collective-permute-done | bytes 1048608 | tf_op jit(solution)/shard_map/ppermute | solution.py:96
  364.8 20.7 %mlp_products.4 = (bf16[2048,512]{1,0:T(8,128)(2,1)}, bf16[2048,1024]{1,0:T(8,128)(2,1)}) custom-call(bf16[1024,2048]{1,0:T(8,128)(2,1)} %constant_dynamic-update-slice_fusion.20.refs_0_, bf16[1024,2048]{1,0:T(8,128)(2,1)} %collective-permute-done.33.refs_1_, bf16[1024,2048]{1,0:T(8,128)(2,1)} %constant_dynamic-update-slice_fusion.10.refs_2_.refs_4_, ...), custom_call_target="tpu_custom_call" | custom-call | flops 257698032 | bytes 587202 | tf_op jit(solution)/shard_map/mlp_products/pallas_call | solution.py:254
  392.1 20.7 %mlp_products.5 = (bf16[2048,512]{1,0:T(8,128)(2,1)}, bf16[2048,1024]{1,0:T(8,128)(2,1)}) custom-call(bf16[1024,2048]{1,0:T(8,128)(2,1)} %constant_dynamic-update-slice_fusion.20.refs_0_, bf16[1024,2048]{1,0:T(8,128)(2,1)} %collective-permute-done.33.refs_1_, bf16[1024,2048]{1,0:T(8,128)(2,1)} %constant_dynamic-update-slice_fusion.10.refs_2_.refs_4_, ...), custom_call_target="tpu_custom_call" | custom-call | flops 257698032 | bytes 587202 | tf_op jit(solution)/shard_map/mlp_products/pallas_call | solution.py:254
  420.1 24.9 %whole_sums.2 = bf16[2048,2048]{1,0:T(8,128)(2,1)} custom-call(s32[8]{0:T(128)} %shift-left_or_fusion.place_ref, bf16[2048,1024]{1,0:T(8,128)(2,1)} %get-tuple-element.219.refs_0_.refs_4_.refs_5_, bf16[2048,1024]{1,0:T(8,128)(2,1)} %get-tuple-element.220.refs_1_.refs_4_.refs_5_, bf16[2048,1536]{1,0:T(8,128)(2,1)} %all-gather.6.cloned.1.call-done.refs_4_.refs_5_.refs_2_, ...), custom_call_target="tpu_custom_call" | custom-call | flops 343597376 | bytes 503316 | tf_op jit(solution)/shard_map/whole_sums/pallas_call | solution.py:466
  462.7 20.9 %mlp_products.6 = (bf16[2048,512]{1,0:T(8,128)(2,1)}, bf16[2048,1024]{1,0:T(8,128)(2,1)}) custom-call(bf16[1024,2048]{1,0:T(8,128)(2,1)} %constant_dynamic-update-slice_fusion.25.refs_0_.refs_2_, bf16[1024,2048]{1,0:T(8,128)(2,1)} %collective-permute-done.42.refs_1_.refs_3_, bf16[1024,2048]{1,0:T(8,128)(2,1)} %constant_dynamic-update-slice_fusion.15.refs_2_.refs_6_, ...), custom_call_target="tpu_custom_call" | custom-call | flops 257698032 | bytes 587202 | tf_op jit(solution)/shard_map/mlp_products/pallas_call | solution.py:254
  483.6 20.9 %mlp_products.7 = (bf16[2048,512]{1,0:T(8,128)(2,1)}, bf16[2048,1024]{1,0:T(8,128)(2,1)}) custom-call(bf16[1024,2048]{1,0:T(8,128)(2,1)} %constant_dynamic-update-slice_fusion.25.refs_0_.refs_2_, bf16[1024,2048]{1,0:T(8,128)(2,1)} %collective-permute-done.42.refs_1_.refs_3_, bf16[1024,2048]{1,0:T(8,128)(2,1)} %constant_dynamic-update-slice_fusion.15.refs_2_.refs_6_, ...), custom_call_target="tpu_custom_call" | custom-call | flops 257698032 | bytes 587202 | tf_op jit(solution)/shard_map/mlp_products/pallas_call | solution.py:254
  504.6 24.6 %whole_sums.3 = bf16[2048,2048]{1,0:T(8,128)(2,1)} custom-call(s32[8]{0:T(128)} %shift-left_or_fusion.place_ref, bf16[2048,1024]{1,0:T(8,128)(2,1)} %get-tuple-element.229.refs_0_.refs_6_.refs_7_, bf16[2048,1024]{1,0:T(8,128)(2,1)} %get-tuple-element.230.refs_1_.refs_6_.refs_7_, bf16[2048,1536]{1,0:T(8,128)(2,1)} %all-gather.6.cloned.1.call-done.refs_4_.refs_5_.refs_2_, ...), custom_call_target="tpu_custom_call" | custom-call | flops 343597376 | bytes 503316 | tf_op jit(solution)/shard_map/whole_sums/pallas_call | solution.py:466
  536.4 26.2 %weight_grad.6 = bf16[2048,1024]{1,0:T(8,128)(2,1)} custom-call(bf16[1024,2048]{1,0:T(8,128)(2,1)} %constant_dynamic-update-slice_fusion.20.refs_0_, bf16[1024,2048]{1,0:T(8,128)(2,1)} %collective-permute-done.33.refs_1_, bf16[1024,2048]{1,0:T(8,128)(2,1)} %constant_dynamic-update-slice_fusion.25.refs_0_.refs_2_, ...), custom_call_target="tpu_custom_call" | custom-call | flops 343597376 | bytes 503316 | tf_op jit(solution)/shard_map/weight_grad/pallas_call | solution.py:512
  573.2 24.4 %weight_grad.7 = bf16[2048,1024]{1,0:T(8,128)(2,1)} custom-call(bf16[1024,2048]{1,0:T(8,128)(2,1)} %constant_dynamic-update-slice_fusion.20.refs_0_, bf16[1024,2048]{1,0:T(8,128)(2,1)} %collective-permute-done.33.refs_1_, bf16[1024,2048]{1,0:T(8,128)(2,1)} %constant_dynamic-update-slice_fusion.25.refs_0_.refs_2_, ...), custom_call_target="tpu_custom_call" | custom-call | flops 343597376 | bytes 503316 | tf_op jit(solution)/shard_map/weight_grad/pallas_call | solution.py:512
  631.9 29.4 %attend_backward.2.refs_0_.refs_4_.refs_5_ = bf16[2048,768]{1,0:T(8,128)(2,1)} custom-call(s32[8]{0:T(128)} %and_select_fusion.low_ref, s32[8]{0:T(128)} %shift-left_or_fusion.place_ref, s32[8,1,256]{2,1,0:T(1,128)} %bitcast.97, bf16[2048,768]{1,0:T(8,128)(2,1)} %project_qkv.2.qkv_ref, bf16[2048,256]{1,0:T(8,128)(2,1)} %get-tuple-element.278.refs_0_.att_ref.refs_1_, ...), custom_call_target="tpu_custom_call" | custom-call | flops 286331072 | bytes 209715 | tf_op jit(solution)/shard_map/attend_backward/pallas_call | solution.py:706
  707.7 15.5 %weight_grad.8.refs_8_ = bf16[1024,2048]{1,0:T(8,128)(2,1)} custom-call(bf16[2048,512]{1,0:T(8,128)(2,1)} %get-tuple-element.261.refs_0_.refs_1_, bf16[2048,512]{1,0:T(8,128)(2,1)} %get-tuple-element.261.refs_0_.refs_1_, bf16[2048,512]{1,0:T(8,128)(2,1)} %get-tuple-element.252.refs_0_.refs_2_.refs_3_, ...), custom_call_target="tpu_custom_call" | custom-call | flops 171798688 | bytes 503316 | tf_op jit(solution)/shard_map/weight_grad/pallas_call | solution.py:512
  739.1 15.4 %weight_grad.9 = bf16[1024,2048]{1,0:T(8,128)(2,1)} custom-call(bf16[2048,512]{1,0:T(8,128)(2,1)} %get-tuple-element.268.refs_1_.refs_0_, bf16[2048,512]{1,0:T(8,128)(2,1)} %get-tuple-element.268.refs_1_.refs_0_, bf16[2048,512]{1,0:T(8,128)(2,1)} %get-tuple-element.228.refs_1_.refs_2_.refs_3_, ...), custom_call_target="tpu_custom_call", output_to_operand_aliasing={{}: (8, {})} | custom-call | flops 171798688 | bytes 503316 | tf_op jit(solution)/shard_map/weight_grad/pallas_call | solution.py:512
  771.5 10.4 %weight_grad.10 = bf16[256,2048]{1,0:T(8,128)(2,1)} custom-call(bf16[2048,256]{1,0:T(8,128)(2,1)} %get-tuple-element.278.refs_0_.att_ref.refs_1_, bf16[2048,256]{1,0:T(8,128)(2,1)} %get-tuple-element.278.refs_0_.att_ref.refs_1_, bf16[2048,256]{1,0:T(8,128)(2,1)} %get-tuple-element.200.refs_0_.refs_2_.refs_3_.att_ref, ...), custom_call_target="tpu_custom_call" | custom-call | flops 85899344 | bytes 419430 | tf_op jit(solution)/shard_map/weight_grad/pallas_call | solution.py:512
  781.8 34.5 %attend_backward.3.refs_0_.refs_6_.refs_7_ = bf16[2048,768]{1,0:T(8,128)(2,1)} custom-call(s32[8]{0:T(128)} %and_select_fusion.1.low_ref, s32[8]{0:T(128)} %shift-left_or_fusion.place_ref, s32[8,1,256]{2,1,0:T(1,128)} %bitcast.94, bf16[2048,768]{1,0:T(8,128)(2,1)} %project_qkv.3.qkv_ref, ...), custom_call_target="tpu_custom_call" | custom-call | flops 286331072 | bytes 209715 | tf_op jit(solution)/shard_map/attend_backward/pallas_call | solution.py:706
  860.5 19.3 %weight_grad.11 = bf16[2048,768]{1,0:T(8,128)(2,1)} custom-call(bf16[1024,2048]{1,0:T(8,128)(2,1)} %constant_dynamic-update-slice_fusion.refs_0_, bf16[1024,2048]{1,0:T(8,128)(2,1)} %collective-permute-done.9.refs_1_, bf16[1024,2048]{1,0:T(8,128)(2,1)} %constant_dynamic-update-slice_fusion.5.refs_0_.refs_2_, ...), custom_call_target="tpu_custom_call" | custom-call | flops 257698032 | bytes 461373 | tf_op jit(solution)/shard_map/weight_grad/pallas_call | solution.py:512
  930.8 19.3 %reduce-scatter.18.cloned.1.call-done = bf16[512,768]{1,0:T(8,128)(2,1)} async-done(((bf16[2048,768]{1,0:T(8,128)(2,1)}), bf16[512,768]{1,0:T(8,128)(2,1)}) %reduce-scatter.18.cloned.1.call-update) | async-done | bytes 786448 | tf_op jit(solution)/shard_map/reduce_scatter | solution.py:902
  (490 shorter events, 453.9 us)
Async XLA Ops:
  7.2 98.4 %all-gather.4.cloned.1.call-start = ((), (), s32[]{:S(2)}) async-start(), calls=%async_computation.7 | async-start | bytes 5242880 | tf_op jit(solution)/shard_map/all_gather | solution.py:783
  28.3 217.9 %all-gather.6.cloned.1.call-start = ((), (), s32[]{:S(2)}) async-start(), calls=%async_computation.8 | async-start | bytes 7864320 | tf_op jit(solution)/shard_map/all_gather | solution.py:783
  132.1 229.8 %all-gather.8.cloned.1.call-start = ((), (), s32[]{:S(2)}) async-start(), calls=%async_computation.9 | async-start | bytes 7864320 | tf_op jit(solution)/shard_map/all_gather | solution.py:783
  211.7 34.4 %collective-permute-start.21 = (bf16[256,2048]{1,0:T(8,128)(2,1)}, bf16[256,2048]{1,0:T(8,128)(2,1)}, u32[]{:S(2)}, u32[]{:S(2)}) collective-permute-start(bf16[256,2048]{1,0:T(8,128)(2,1)} %get-tuple-element.185), channel_id=1, source_target_pairs={{0,2},{1,3},{2,0},{3,1},{4,6},{5,7},{6,4},{7,5},{8,10},{9,11},{10,... | collective-permute-start | bytes 3145736 | tf_op jit(solution)/shard_map/ppermute | solution.py:96
  213.2 32.9 %collective-permute-start.22 = (bf16[256,2048]{1,0:T(8,128)(2,1)}, bf16[256,2048]{1,0:T(8,128)(2,1)}, u32[]{:S(2)}, u32[]{:S(2)}) collective-permute-start(bf16[256,2048]{1,0:T(8,128)(2,1)} %get-tuple-element.187), channel_id=1, source_target_pairs={{0,4},{1,5},{2,6},{3,7},{4,0},{5,1},{6,2},{7,3},{8,12},{9,13},{10,... | collective-permute-start | bytes 3145736 | tf_op jit(solution)/shard_map/ppermute | solution.py:96
  214.7 314.5 %reduce-scatter.8.cloned.1.call-start = ((), (), s32[]{:S(2)}) async-start(), calls=%async_computation.10 | async-start | bytes 9437184 | tf_op jit(solution)/shard_map/reduce_scatter | solution.py:929
  272.6 32.9 %collective-permute-start.29 = (bf16[1024,2048]{1,0:T(8,128)(2,1)}, bf16[1024,2048]{1,0:T(8,128)(2,1)}, u32[]{:S(2)}, u32[]{:S(2)}) collective-permute-start(bf16[1024,2048]{1,0:T(8,128)(2,1)} %partial_sums.14), channel_id=1, source_target_pairs={{0,1},{1,0},{2,3},{3,2},{4,5},{5,4},{6,7},{7,6},{8,9},{9,8},{10,11... | collective-permute-start | bytes 12582920 | tf_op jit(solution)/shard_map/ppermute | solution.py:96
  273.4 32.1 %collective-permute-start.30 = (bf16[1024,2048]{1,0:T(8,128)(2,1)}, bf16[1024,2048]{1,0:T(8,128)(2,1)}, u32[]{:S(2)}, u32[]{:S(2)}) collective-permute-start(bf16[1024,2048]{1,0:T(8,128)(2,1)} %constant_dynamic-update-slice_fusion.15.refs_2_.refs_6_), channel_id=1, source_target_pairs={{0,1},{1,0},{2,3},{3,2},{4,5},{5,4},{6,7},{7,6},{8,9},{9,8},{10,11... | collective-permute-start | bytes 12582920 | tf_op jit(solution)/shard_map/ppermute | solution.py:96
  322.8 39.1 %collective-permute-start.33 = (bf16[1024,2048]{1,0:T(8,128)(2,1)}, bf16[1024,2048]{1,0:T(8,128)(2,1)}, u32[]{:S(2)}, u32[]{:S(2)}) collective-permute-start(bf16[1024,2048]{1,0:T(8,128)(2,1)} %constant_dynamic-update-slice_fusion.20.refs_0_), channel_id=1, source_target_pairs={{0,1},{1,0},{2,3},{3,2},{4,5},{5,4},{6,7},{7,6},{8,9},{9,8},{10,11... | collective-permute-start | bytes 12582920 | tf_op jit(solution)/shard_map/ppermute | solution.py:96
  445.0 216.3 %reduce-scatter.10.cloned.1.call-start = ((), (), s32[]{:S(2)}) async-start(), calls=%async_computation.11 | async-start | bytes 9437184 | tf_op jit(solution)/shard_map/reduce_scatter | solution.py:929
  529.2 225.2 %reduce-scatter.12.cloned.1.call-start = ((), (), s32[]{:S(2)}) async-start(), calls=%async_computation.12 | async-start | bytes 5242880 | tf_op jit(solution)/shard_map/reduce_scatter | solution.py:902
  568.9 31.8 %collective-permute-start.47 = (bf16[128,2048]{1,0:T(8,128)(2,1)}, bf16[128,2048]{1,0:T(8,128)(2,1)}, u32[]{:S(2)}, u32[]{:S(2)}) collective-permute-start(bf16[128,2048]{1,0:T(8,128)(2,1)} %slice.393), channel_id=1, source_target_pairs={{0,4},{1,5},{2,6},{3,7},{4,0},{5,1},{6,2},{7,3},{8,12},{9,13},{10,... | collective-permute-start | bytes 1572872 | tf_op jit(solution)/shard_map/ppermute | solution.py:96
  602.5 228.0 %reduce-scatter.14.cloned.1.call-start = ((), (), s32[]{:S(2)}) async-start(), calls=%async_computation.13 | async-start | bytes 5242880 | tf_op jit(solution)/shard_map/reduce_scatter | solution.py:902
  621.8 39.5 %collective-permute-start.51 = (bf16[1024,2048]{1,0:T(8,128)(2,1)}, bf16[1024,2048]{1,0:T(8,128)(2,1)}, u32[]{:S(2)}, u32[]{:S(2)}) collective-permute-start(bf16[1024,2048]{1,0:T(8,128)(2,1)} %partial_sums.18), channel_id=1, source_target_pairs={{0,1},{1,0},{2,3},{3,2},{4,5},{5,4},{6,7},{7,6},{8,9},{9,8},{10,11... | collective-permute-start | bytes 12582920 | tf_op jit(solution)/shard_map/ppermute | solution.py:96
  622.3 38.9 %collective-permute-start.49 = (bf16[256,2048]{1,0:T(8,128)(2,1)}, bf16[256,2048]{1,0:T(8,128)(2,1)}, u32[]{:S(2)}, u32[]{:S(2)}) collective-permute-start(bf16[256,2048]{1,0:T(8,128)(2,1)} %get-tuple-element.244), channel_id=1, source_target_pairs={{0,2},{1,3},{2,0},{3,1},{4,6},{5,7},{6,4},{7,5},{8,10},{9,11},{10,... | collective-permute-start | bytes 3145736 | tf_op jit(solution)/shard_map/ppermute | solution.py:96
  623.2 38.1 %collective-permute-start.50 = (bf16[256,2048]{1,0:T(8,128)(2,1)S(1)}, bf16[256,2048]{1,0:T(8,128)(2,1)}, u32[]{:S(2)}, u32[]{:S(2)}) collective-permute-start(bf16[256,2048]{1,0:T(8,128)(2,1)S(1)} %copy-done.67), channel_id=1, source_target_pairs={{0,4},{1,5},{2,6},{3,7},{4,0},{5,1},{6,2},{7,3},{8,12},{9,13},{10,... | collective-permute-start | bytes 3145736 | tf_op jit(solution)/shard_map/ppermute | solution.py:96
  692.9 34.1 %collective-permute-start.56 = (bf16[1024,2048]{1,0:T(8,128)(2,1)}, bf16[1024,2048]{1,0:T(8,128)(2,1)}, u32[]{:S(2)}, u32[]{:S(2)}) collective-permute-start(bf16[1024,2048]{1,0:T(8,128)(2,1)} %partial_sums.19), channel_id=1, source_target_pairs={{0,1},{1,0},{2,3},{3,2},{4,5},{5,4},{6,7},{7,6},{8,9},{9,8},{10,11... | collective-permute-start | bytes 12582920 | tf_op jit(solution)/shard_map/ppermute | solution.py:96
  692.9 161.1 %reduce-scatter.16.cloned.1.call-start = ((), (), s32[]{:S(2)}) async-start(), calls=%async_computation.14 | async-start | bytes 5242880 | tf_op jit(solution)/shard_map/reduce_scatter | solution.py:950
  755.5 161.0 %reduce-scatter.20.cloned.1.call-start = ((), (), s32[]{:S(2)}) async-start(), calls=%async_computation.16 | async-start | bytes 1310720 | tf_op jit(solution)/shard_map/reduce_scatter | solution.py:902
  755.7 60.6 %collective-permute-start.64 = (bf16[256,2048]{1,0:T(8,128)(2,1)}, bf16[256,2048]{1,0:T(8,128)(2,1)}, u32[]{:S(2)}, u32[]{:S(2)}) collective-permute-start(bf16[256,2048]{1,0:T(8,128)(2,1)} %get-tuple-element.277), channel_id=1, source_target_pairs={{0,2},{1,3},{2,0},{3,1},{4,6},{5,7},{6,4},{7,5},{8,10},{9,11},{10,... | collective-permute-start | bytes 3145736 | tf_op jit(solution)/shard_map/ppermute | solution.py:96
  756.6 61.7 %collective-permute-start.65 = (bf16[256,2048]{1,0:T(8,128)(2,1)}, bf16[256,2048]{1,0:T(8,128)(2,1)}, u32[]{:S(2)}, u32[]{:S(2)}) collective-permute-start(bf16[256,2048]{1,0:T(8,128)(2,1)} %get-tuple-element.282), channel_id=1, source_target_pairs={{0,4},{1,5},{2,6},{3,7},{4,0},{5,1},{6,2},{7,3},{8,12},{9,13},{10,... | collective-permute-start | bytes 3145736 | tf_op jit(solution)/shard_map/ppermute | solution.py:96
  761.2 57.1 %collective-permute-start.62 = (bf16[128,2048]{1,0:T(8,128)(2,1)}, bf16[128,2048]{1,0:T(8,128)(2,1)S(1)}, u32[]{:S(2)}, u32[]{:S(2)}) collective-permute-start(bf16[128,2048]{1,0:T(8,128)(2,1)} %add_convert_fusion.7), channel_id=1, source_target_pairs={{0,4},{1,5},{2,6},{3,7},{4,0},{5,1},{6,2},{7,3},{8,12},{9,13},{10,... | collective-permute-start | bytes 1572872 | tf_op jit(solution)/shard_map/ppermute | solution.py:96
  762.7 55.6 %collective-permute-start.63 = (bf16[128,2048]{1,0:T(8,128)(2,1)}, bf16[128,2048]{1,0:T(8,128)(2,1)}, u32[]{:S(2)}, u32[]{:S(2)}) collective-permute-start(bf16[128,2048]{1,0:T(8,128)(2,1)} %add_convert_fusion.6), channel_id=1, source_target_pairs={{0,2},{1,3},{2,0},{3,1},{4,6},{5,7},{6,4},{7,5},{8,10},{9,11},{10,... | collective-permute-start | bytes 1572872 | tf_op jit(solution)/shard_map/ppermute | solution.py:96
  844.6 105.4 %reduce-scatter.18.cloned.1.call-start = ((), (), s32[]{:S(2)}) async-start(), calls=%async_computation.15 | async-start | bytes 3932160 | tf_op jit(solution)/shard_map/reduce_scatter | solution.py:902
  (132 other events, 2113.3 us)
Sparse Core Ops, SparseCore 0:
  28.4 77.1 all-gather.3
  132.2 113.8 all-gather.5
  248.3 113.5 all-gather.7
  445.1 78.7 reduce-scatter.7
  529.4 83.8 reduce-scatter.9
  615.4 76.7 reduce-scatter.11
  694.5 77.5 reduce-scatter.13
  774.4 77.2 reduce-scatter.15
  854.1 27.6 reduce-scatter.19
  889.5 60.5 reduce-scatter.17

commit v3 on v2

--- a/solution.py
+++ b/solution.py
@@ -77,6 +77,8 @@
         self.waiting.append(action)
 
     def gate(self, value):
+        if isinstance(value, Columns):
+            return Columns(after(value.array, *self.now), value.shape[1], value.index)
         return after(value, *self.now)
 
     def ends(self, value):
@@ -279,6 +281,10 @@
         self.shape = (array.shape[0], width)
 
 
+def columns_of(array):
+    return array if isinstance(array, Columns) else Columns(array, array.shape[1], 0)
+
+
 def resident(part):
     return pl.BlockSpec(
         part.shape, lambda i, *_: (0, part.index), pipeline_mode=pl.Buffered(1)
@@ -339,36 +345,102 @@
     )
 
 
-def mlp_body(x_ref, gy_ref, gu_ref, down_ref, hid_ref, dgu_ref):
-    cols = hid_ref.shape[1]
-    both = dot(x_ref[...], gu_ref[...])
-    d_hid = dot(gy_ref[...], down_ref[...])
-    gp = both[:, :cols]
-    up = both[:, cols:]
-    sig = jax.nn.sigmoid(gp)
-    silu = gp * sig
-    hid_ref[...] = (silu * up).astype(BF16)
-    dgu_ref[:, :cols] = (d_hid * up * sig * (1.0 + gp * (1.0 - sig))).astype(BF16)
-    dgu_ref[:, cols:] = (d_hid * silu).astype(BF16)
-
-
-def mlp_products(tokens, gy, w_gu, w_down):
+def mlp_products(tokens, gy, sets):
     seq = sum(piece.shape[0] for piece in tokens)
-    dim, cols = w_down.shape
-    return streaming_call(
-        [tokens, gy],
-        mlp_body,
-        [w_gu, w_down],
-        lambda rows: [resident(w_gu), resident(w_down)],
-        [jax.ShapeDtypeStruct((seq, cols), BF16), jax.ShapeDtypeStruct((seq, 2 * cols), BF16)],
-        lambda rows: [by_rows(rows, cols), by_rows(rows, 2 * cols)],
-        "mlp_products",
-        6 * seq * dim * cols,
-        2 * (3 * dim * cols + 3 * seq * cols),
-    )
+    dim = tokens[0].shape[1]
+    cut = sets[0].shape[1] // 3
+    parts = len(sets)
+    rows = min(512, tokens[0].shape[0])
+    steps = seq // rows
+    streams = [tokens, gy]
+    count = sum(len(pieces) for pieces in streams)
+
+    def kernel(*refs):
+        piece_refs, set_refs, rest = refs[:count], refs[count : count + parts], refs[count + parts :]
+        hid_ref, dgu_ref, x_buffer, gy_buffer, set_buffer, sems, set_sems = rest
+        step = pl.program_id(0)
+
+        def copies(number):
+            found, at = [], 0
+            slot = number % 2
+            for stream, (pieces, buffer) in enumerate(zip(streams, (x_buffer, gy_buffer))):
+                first = 0
+                for piece in pieces:
+                    place = (number % steps) * rows - first
+                    if 0 <= place < piece.shape[0]:
+                        source = piece_refs[at].at[pl.ds(place, rows)]
+                        found.append(
+                            pltpu.make_async_copy(source, buffer.at[slot], sems.at[stream, slot])
+                        )
+                    first += piece.shape[0]
+                    at += 1
+            return found
+
+        loads = [
+            pltpu.make_async_copy(set_refs[p], set_buffer.at[p], set_sems.at[p])
+            for p in range(parts)
+        ]
+
+        @pl.when(step == 0)
+        def _():
+            for copy in copies(0) + loads:
+                copy.start()
+
+        for number in range(parts * steps):
+
+            @pl.when(step == number)
+            def _():
+                if number + 1 < parts * steps:
+                    for copy in copies(number + 1):
+                        copy.start()
+                for copy in copies(number):
+                    copy.wait()
+                if number % steps == 0:
+                    loads[number // steps].wait()
+
+        slot = lax.rem(step, 2)
+        weights = set_buffer.at[step // steps]
+        both = dot(x_buffer[slot], weights[:, : 2 * cut])
+        d_hid = dot(gy_buffer[slot], weights[:, 2 * cut :])
+        gp = both[:, :cut]
+        up = both[:, cut:]
+        sig = jax.nn.sigmoid(gp)
+        silu = gp * sig
+        hid_ref[...] = (silu * up).astype(BF16)
+        dgu_ref[:, :cut] = (d_hid * up * sig * (1.0 + gp * (1.0 - sig))).astype(BF16)
+        dgu_ref[:, cut:] = (d_hid * silu).astype(BF16)
+
+    def out_map(s):
+        return (s % steps, s // steps)
+
+    return pl.pallas_call(
+        kernel,
+        out_shape=[
+            jax.ShapeDtypeStruct((seq, parts * cut), BF16),
+            jax.ShapeDtypeStruct((seq, 2 * parts * cut), BF16),
+        ],
+        grid=(parts * steps,),
+        in_specs=[pl.BlockSpec(memory_space=pl.ANY)] * (count + parts),
+        out_specs=[pl.BlockSpec((rows, cut), out_map), pl.BlockSpec((rows, 2 * cut), out_map)],
+        scratch_shapes=[
+            pltpu.VMEM((2, rows, dim), BF16),
+            pltpu.VMEM((2, rows, dim), BF16),
+            pltpu.VMEM((parts, dim, 3 * cut), BF16),
+            pltpu.SemaphoreType.DMA((2, 2)),
+            pltpu.SemaphoreType.DMA((parts,)),
+        ],
+        compiler_params=params_for(),
+        cost_estimate=cost(
+            flops=6 * seq * dim * cut * parts,
+            bytes_accessed=2 * parts * (2 * seq * dim + 3 * dim * cut + 3 * seq * cut),
+            transcendentals=seq * cut * parts,
+        ),
+        name="mlp_products",
+    )(*[piece for pieces in streams for piece in pieces], *sets)
 
 
 def partial_sums(lefts, rights, side, got=None):
+    lefts = [columns_of(left) for left in lefts]
     seq = lefts[0].shape[0]
     dim = rights[0].shape[0]
     rows = seq // 2
@@ -414,9 +486,10 @@
             send_y[...] = high
 
     in_specs = [
-        pl.BlockSpec((block, left.shape[1]), lambda i: (side * steps + i, 0)) for left in lefts
+        pl.BlockSpec((block, left.shape[1]), lambda i, left=left: (side * steps + i, left.index))
+        for left in lefts
     ] + [resident(right) for right in rights]
-    ins = list(lefts) + [right.array for right in rights]
+    ins = [left.array for left in lefts] + [right.array for right in rights]
     if got is not None:
         in_specs.append(by_rows(block, dim))
         ins.append(got)
@@ -449,6 +522,7 @@
 
 
 def whole_sums(lefts, rights, place):
+    lefts = [columns_of(left) for left in lefts]
     seq = lefts[0].shape[0]
     dim = rights[0].shape[0]
     chunks = place.shape[0]
@@ -470,7 +544,8 @@
             num_scalar_prefetch=1,
             grid=(chunks,),
             in_specs=[
-                pl.BlockSpec((block, left.shape[1]), lambda i, at: (at[i], 0)) for left in lefts
+                pl.BlockSpec((block, left.shape[1]), lambda i, at, left=left: (at[i], left.index))
+                for left in lefts
             ]
             + [resident(right) for right in rights],
             out_specs=pl.BlockSpec((block, dim), lambda i, at: (i, 0)),
@@ -482,25 +557,24 @@
             transcendentals=0,
         ),
         name="whole_sums",
-    )(place, *lefts, *[right.array for right in rights])
+    )(place, *[left.array for left in lefts], *[right.array for right in rights])
 
 
 def halves(array):
     if isinstance(array, (list, tuple)):
-        return [(half, 0) for half in array]
-    return [(array, 0), (array, 1)]
-
-
-def weight_grad(lefts, rights, seq, before=None, parts=1):
+        return [(columns_of(half), 0) for half in array]
+    return [(columns_of(array), 0), (columns_of(array), 1)]
+
+
+def weight_grad(lefts, rights, seq):
     seq //= 2
     lefts = [pair for left in lefts for pair in halves(left)]
     rights = [pair for right in rights for pair in halves(right)]
     height = lefts[0][0].shape[1]
     cols = rights[0][0].shape[1]
-    tall = min(512 if height < 1024 else 256, height)
+    tall = min(512 if height <= 1024 else 256, height)
     wide = min(1024, cols)
     count = len(lefts)
-    first = 0 if before is None else (parts - 1) * height // tall
 
     def kernel(*refs):
         total = None
@@ -509,15 +583,20 @@
             total = term if total is None else total + term
         refs[-1][...] = total.astype(BF16)
 
+    def left_spec(part, p):
+        first = part.index * (height // tall)
+        return pl.BlockSpec((seq, tall), lambda n, m: (p, first + m))
+
+    def right_spec(part, p):
+        first = part.index * (cols // wide)
+        return pl.BlockSpec((seq, wide), lambda n, m: (p, first + n))
+
     return pl.pallas_call(
         kernel,
-        out_shape=jax.ShapeDtypeStruct((parts * height, cols), BF16),
+        out_shape=jax.ShapeDtypeStruct((height, cols), BF16),
         grid=(cols // wide, height // tall),
-        in_specs=[pl.BlockSpec((seq, tall), lambda n, m, p=p: (p, m)) for _, p in lefts]
-        + [pl.BlockSpec((seq, wide), lambda n, m, p=p: (p, n)) for _, p in rights]
-        + [pl.BlockSpec(memory_space=pl.ANY)] * (before is not None),
-        out_specs=pl.BlockSpec((tall, wide), lambda n, m: (m + first, n)),
-        input_output_aliases={} if before is None else {2 * count: 0},
+        in_specs=[left_spec(*pair) for pair in lefts] + [right_spec(*pair) for pair in rights],
+        out_specs=pl.BlockSpec((tall, wide), lambda n, m: (m, n)),
         compiler_params=params_for(),
         cost_estimate=cost(
             flops=2 * seq * height * cols * count,
@@ -525,11 +604,7 @@
             transcendentals=0,
         ),
         name="weight_grad",
-    )(
-        *[a for a, _ in lefts],
-        *[a for a, _ in rights],
-        *([] if before is None else [before]),
-    )
+    )(*[part.array for part, _ in lefts], *[part.array for part, _ in rights])
 
 
 def head_stack(block, heads):
@@ -825,8 +900,7 @@
     attn_in, gy, mlp_in, branch = {}, {}, {}, {}
     qkv, att, lse, middle, inv_second = ({} for _ in range(5))
     grad_middle, gain_mlp, gain_attn, outputs, in_grads, d_qkv = ({} for _ in range(6))
-    hid = {r: [] for r in rows}
-    d_gu = {r: [] for r in rows}
+    hid, d_gu = {}, {}
 
     def know(r):
         facts[r] = row_facts(gate(doc_lengths[r]), seq)
@@ -853,13 +927,13 @@
         inv_second[r] = norm_scale(middle[r])
         mlp_in[r] = Gather(slots, (middle[r] * inv_second[r] * mlp_scale).astype(BF16))
 
-    def mlp(r, part):
-        one, two = mlp_products(
-            first_of(mlp_in[r].halves), gy[r].halves, full_gu[part], full_down[part]
-        )
-        ends(one)
-        hid[r].append(one)
-        d_gu[r].append(two)
+    def mlp(r):
+        hid[r], d_gu[r] = mlp_products(first_of(mlp_in[r].halves), gy[r].halves, ffn_sets)
+        ends(hid[r])
+
+    def parts_of(array):
+        width = array.shape[1] // len(spans)
+        return [Columns(array, width, part) for part in range(len(spans))]
 
     def after_mlp(r, total):
         total = gate(total).astype(F32)
@@ -908,22 +982,36 @@
         else:
             start()
 
+    def out_grad_sum():
+        grad = ends(weight_grad(*grad_factors(att, halves_of(branch)), seq))
+
+        def start():
+            size = grad.shape[1] // narrow
+
+            def block(number):
+                return lax.dynamic_slice_in_dim(gate(grad), (number % narrow) * size, size, 1)
+
+            total = block(here).astype(F32)
+            for step in range(1, narrow):
+                pairs = [(i, (i + step) % narrow) for i in range(narrow)]
+                total = total + lax.ppermute(block(here + step), "narrow", pairs).astype(F32)
+            grad_attn["out"] = total
+
+        return start
+
     def both(table):
         return [table[r] for r in rows]
 
     def halves_of(table):
         return {r: table[r].halves for r in rows}
 
-    def part_of(table, part):
-        return {r: table[r][part] for r in rows}
-
     sums, down, grad_gu, grad_down, grad_attn = {}, {}, [None, None], [None, None], {}
 
     def out_sum(r):
         sums[r] = spread([att[r]], [full_out])
 
     def mlp_sum(r):
-        whole = ends(whole_sums(first_of(d_gu[r]), full_gu, facts[r][1]))
+        whole = ends(whole_sums(first_of(parts_of(d_gu[r])), full_gu, facts[r][1]))
 
         def start():
             sums[r] = lax.psum_scatter(gate(whole), "wide", scatter_dimension=0, tiled=True)
@@ -934,24 +1022,13 @@
         sums[r] = spread([d_qkv[r]], [w_qkv])
 
     def down_sum(r):
-        down[r] = spread(hid[r], full_down)
+        down[r] = spread(parts_of(hid[r]), full_down)
 
     def gu_grad(part):
-        grad_of(halves_of(mlp_in), part_of(d_gu, part), grad_gu, part)
-
-    def down_grad(part):
-        factors = grad_factors(part_of(hid, part), halves_of(gy))
-        if part == 0:
-            grad_down[0] = ends(weight_grad(*factors, seq, None, 2))
-            return
-        grad = ends(weight_grad(*factors, seq, grad_down[0], 2))
-
-        def start():
-            grad_down[0] = lax.psum_scatter(
-                gate(grad), "narrow", scatter_dimension=1, tiled=True
-            )
-
-        slots.later(start)
+        grad_of(halves_of(mlp_in), {r: parts_of(d_gu[r])[part] for r in rows}, grad_gu, part)
+
+    def down_grad():
+        grad_of(hid, halves_of(gy), grad_down, 0, axis=1)
 
     one, two = 0, last
     attn_in[one] = Gather(slots, scaled_in[one])
@@ -1001,22 +1078,20 @@
     sums[two].near()
     ends(ffn_sets[1])
     turn()
-    mlp(one, 0)
+    mlp(one)
     sums[two].last()
     turn()
-    mlp(one, 1)
+    mlp_sum(one)
     after_attention(two, sums[two].total)
     turn()
-    mlp_sum(one)
+    down_sum(one)
+    down[one].core()
     mlp_in[two].far()
     turn()
-    down_sum(one)
+    down[one].even()
     mlp_in[two].core()
     turn()
-    mlp(two, 0)
-    down[one].core()
-    turn()
-    mlp(two, 1)
+    mlp(two)
     turn()
     mlp_sum(two)
     ends(sums[one])
@@ -1028,7 +1103,6 @@
     branch[one].far()
     turn()
     down_sum(two)
-    down[one].even()
     branch[one].core()
     turn()
     back_attention(one)
@@ -1040,35 +1114,34 @@
     down[two].even()
     after_mlp(two, sums[two])
     turn()
-    down_grad(0)
+    down_grad()
     sums[one].core()
     branch[two].far()
     down[one].last()
     turn()
     sums[one].even()
-    down_grad(1)
     branch[two].core()
-    down[two].near()
     ends(grad_gu[0])
     turn()
-    grad_of(att, halves_of(branch), grad_attn, "out", axis=1)
+    start_out = out_grad_sum()
     back_attention(two)
     sums[one].near()
-    down[two].last()
+    down[two].near()
     turn()
     back_sum(two)
     sums[one].last()
     ends(grad_gu[1])
     turn()
     sums[two].core()
+    grad_of(halves_of(attn_in), d_qkv, grad_attn, "qkv", False)
     turn()
     sums[two].even()
+    sums[two].near()
+    start_out()
     ends(grad_down[0])
     turn()
-    grad_of(halves_of(attn_in), d_qkv, grad_attn, "qkv", False)
-    sums[two].near()
-    turn()
     sums[two].last()
+    down[two].last(False)
     turn()
     for r in rows:
         outputs[r] = (middle[r] + down[r].total).astype(BF16)
@@ -1078,6 +1151,8 @@
     for axis in ("narrow", "wide"):
         count = lax.axis_size(axis)
         me = lax.axis_index(axis)
+        if axis == "wide":
+            gains = after(gains, grad_attn["qkv"])
         for bit in reversed(range(bits_of(count))):
             size = gains.shape[1] // 2
             mine = (me >> bit) & 1

time: 968 us -> 955 us (0.987)
  Pallas kernels: 480 us -> 452 us
  waiting for transfers between devices: 201 us -> 228 us
  other arithmetic: 102 us -> 91.5 us
    pallas_call x8 -> x4, Pallas kernels: 124 us -> 40.9 us  [streaming_call(): pl.pallas_call(kernel, out_shape=outs, grid=(steps,), in_specs=[pl.BlockS...]
    pallas_call x6 -> x7, Pallas kernels: 111 us -> 174 us  [the longest x5 105 us: weight_grad(): pl.pallas_call(kernel, out_shape=jax.ShapeDtypeStruct((height, cols), BF1...]
    ppermute x0 -> x3, waiting for transfers between devices: none -> 25.8 us  [start(): lax.ppermute(block(here + step), 'narrow', pairs).astype(F32)]
    reduce_scatter x4, waiting for transfers between devices: 19.3 us -> 0.01 us  [start(): lax.psum_scatter(gate(grad) if wait else grad, 'narrow', scatter_dimensio...]
    ppermute x70, waiting for transfers between devices: 147 us -> 164 us  [swap(): got = lax.ppermute(self.gate(block), axis, pairs)]
    unnamed x163 -> x155, local copies, waits for them, and re-layouts: 50.4 us -> 47.6 us
  transfers between devices with their start and end apart: 88 -> 90, of which waited for: 32 -> 34; matrix products, arithmetic and copies ran while one was open for 17% -> 16% of each run, Pallas kernels for 50% -> 48%
where the time goes in v3:
time: 955 us; the launch traced here: 944 us
  Pallas kernels  452 us (47%)
  waiting for transfers between devices  228 us (24%)
  other arithmetic  91.5 us (10%)
  local copies, waits for them, and re-layouts  80.7 us (8%)
  starting transfers between devices  77.5 us (8%)
  between operations  15.3 us (2%)
    ppermute x70, waiting for transfers between devices, swap(): got = lax.ppermute(self.gate(block), axis, pairs)  164 us
    pallas_call x5, Pallas kernels, weight_grad(): pl.pallas_call(kernel, out_shape=jax.ShapeDtypeStruct((height, cols), BF1...  105 us
    pallas_call x12, Pallas kernels, partial_sums(): pl.pallas_call(kernel, out_shape=out_shape, grid=(steps,), in_specs=in_sp...  93 us
    pallas_call x2, Pallas kernels, mlp_products(): pl.pallas_call(kernel, out_shape=[jax.ShapeDtypeStruct((seq, parts * cut)...  69.2 us
    ppermute x70, starting transfers between devices, swap(): got = lax.ppermute(self.gate(block), axis, pairs)  59.3 us
    pallas_call x2, Pallas kernels, attend_backward(): pl.pallas_call(functools.partial(backward_kernel, heads, blocks, size), o...  58.8 us
    pallas_call x2, Pallas kernels, whole_sums(): pl.pallas_call(kernel, out_shape=jax.ShapeDtypeStruct((seq, dim), BF16),...  49.5 us
    unnamed x155, local copies, waits for them, and re-layouts  47.6 us
  transfers between devices with their start and end apart: 90, of which 34 were waited for; matrix products, arithmetic and copies ran while one was open for 16% of the time, Pallas kernels for 48%

profile of v3, /device:TPU:0, one launch (start us, length us, event | category | flops | bytes accessed | tf_op | source)
XLA Modules:
  0.0 944.5 jit_solution(8211153614402169094)
XLA Ops:
  29.0 16.7 %collective-permute-done.3 = bf16[256,2048]{1,0:T(8,128)(2,1)S(1)} collective-permute-done((bf16[256,2048]{1,0:T(8,128)(2,1)S(1)}, bf16[256,2048]{1,0:T(8,128)(2,1)S(1)}, u32[]{:S(2)}, u32[]{:S(2)}) %collective-permute-start.3) | collective-permute-done | bytes 1048608 | tf_op jit(solution)/shard_map/ppermute | solution.py:98
  78.9 16.0 %collective-permute-done.8 = bf16[256,2048]{1,0:T(8,128)(2,1)S(1)} collective-permute-done((bf16[256,2048]{1,0:T(8,128)(2,1)}, bf16[256,2048]{1,0:T(8,128)(2,1)S(1)}, u32[]{:S(2)}, u32[]{:S(2)}) %collective-permute-start.8) | collective-permute-done | bytes 1048608 | tf_op jit(solution)/shard_map/ppermute | solution.py:98
  111.3 12.8 %project_qkv.2.qkv_ref = bf16[2048,768]{1,0:T(8,128)(2,1)} custom-call(bf16[1024,2048]{1,0:T(8,128)(2,1)} %constant_dynamic-update-slice_fusion.refs_0_, bf16[1024,2048]{1,0:T(8,128)(2,1)} %collective-permute-done.9.refs_1_, bf16[2048,1024]{1,0:T(8,128)(2,1)} %all-gather.4.cloned.1.call-done.refs_2_.refs_1_, f32[2048,128]{1,0:T(8,128)} %pad_maximum_fusion.9.refs_3_.cos_ref, ...), custom_call_target="tpu_custom_call" | custom-call | flops 128849016 | bytes 293601 | tf_op jit(solution)/shard_map/project_qkv/pallas_call | solution.py:256
  130.8 17.4 %attend_forward.2 = (bf16[2048,256]{1,0:T(8,128)(2,1)}, f32[8,4,256]{2,1,0:T(4,128)}) custom-call(s32[8]{0:T(128)} %and_select_fusion.low_ref, s32[8]{0:T(128)} %shift-left_or_fusion.place_ref, s32[8,1,256]{2,1,0:T(1,128)} %bitcast.96, bf16[2048,768]{1,0:T(8,128)(2,1)} %project_qkv.2.qkv_ref), custom_call_target="tpu_custom_call" | custom-call | flops 114532432 | bytes 83886 | tf_op jit(solution)/shard_map/attend_forward/pallas_call | solution.py:674
  167.5 12.7 %project_qkv.3.qkv_ref = bf16[2048,768]{1,0:T(8,128)(2,1)} custom-call(bf16[1024,2048]{1,0:T(8,128)(2,1)} %constant_dynamic-update-slice_fusion.5.refs_0_.refs_2_, bf16[1024,2048]{1,0:T(8,128)(2,1)} %collective-permute-done.12.refs_1_.refs_3_, bf16[2048,1024]{1,0:T(8,128)(2,1)} %all-gather.4.cloned.1.call-done.refs_2_.refs_1_, ...), custom_call_target="tpu_custom_call" | custom-call | flops 128849016 | bytes 293601 | tf_op jit(solution)/shard_map/project_qkv/pallas_call | solution.py:256
  190.6 17.0 %collective-permute-done.20 = bf16[256,2048]{1,0:T(8,128)(2,1)S(1)} collective-permute-done((bf16[256,2048]{1,0:T(8,128)(2,1)S(1)}, bf16[256,2048]{1,0:T(8,128)(2,1)S(1)}, u32[]{:S(2)}, u32[]{:S(2)}) %collective-permute-start.20) | collective-permute-done | bytes 1048608 | tf_op jit(solution)/shard_map/ppermute | solution.py:98
  214.5 17.9 %attend_forward.3 = (bf16[2048,256]{1,0:T(8,128)(2,1)}, f32[8,4,256]{2,1,0:T(4,128)}) custom-call(s32[8]{0:T(128)} %and_select_fusion.1.low_ref, s32[8]{0:T(128)} %shift-left_or_fusion.place_ref, s32[8,1,256]{2,1,0:T(1,128)} %bitcast.93, bf16[2048,768]{1,0:T(8,128)(2,1)} %project_qkv.3.qkv_ref), custom_call_target="tpu_custom_call" | custom-call | flops 114532432 | bytes 83886 | tf_op jit(solution)/shard_map/attend_forward/pallas_call | solution.py:674
  232.4 11.1 %all-gather.6.cloned.1.call-done.refs_4_.refs_2_ = bf16[2048,1536]{1,0:T(8,128)(2,1)} async-done(((bf16[512,1536]{1,0:T(8,128)(2,1)}), bf16[2048,1536]{1,0:T(8,128)(2,1)}) %all-gather.6.cloned.1.call-update) | async-done | bytes 6291472 | tf_op jit(solution)/shard_map/all_gather | solution.py:858
  278.2 23.5 %collective-permute-done.28 = bf16[256,2048]{1,0:T(8,128)(2,1)S(1)} collective-permute-done((bf16[256,2048]{1,0:T(8,128)(2,1)S(1)}, bf16[256,2048]{1,0:T(8,128)(2,1)S(1)}, u32[]{:S(2)}, u32[]{:S(2)}) %collective-permute-start.28) | collective-permute-done | bytes 1048608 | tf_op jit(solution)/shard_map/ppermute | solution.py:98
  321.8 24.2 %collective-permute-done.34 = bf16[256,2048]{1,0:T(8,128)(2,1)S(1)} collective-permute-done((bf16[256,2048]{1,0:T(8,128)(2,1)}, bf16[256,2048]{1,0:T(8,128)(2,1)S(1)}, u32[]{:S(2)}, u32[]{:S(2)}) %collective-permute-start.34) | collective-permute-done | bytes 1048608 | tf_op jit(solution)/shard_map/ppermute | solution.py:98
  362.2 34.5 %mlp_products.2 = (bf16[2048,1024]{1,0:T(8,128)(2,1)}, bf16[2048,2048]{1,0:T(8,128)(2,1)}) custom-call(bf16[1024,2048]{1,0:T(8,128)(2,1)} %constant_dynamic-update-slice_fusion.20.refs_0_, bf16[1024,2048]{1,0:T(8,128)(2,1)} %collective-permute-done.33.refs_1_, bf16[1024,2048]{1,0:T(8,128)(2,1)} %constant_dynamic-update-slice_fusion.10.refs_2_.refs_4_, ...), custom_call_target="tpu_custom_call" | custom-call | flops 515396064 | bytes 1174405 | tf_op jit(solution)/shard_map/mlp_products/pallas_call | solution.py:416
  403.3 24.7 %whole_sums.2 = bf16[2048,2048]{1,0:T(8,128)(2,1)} custom-call(s32[8]{0:T(128)} %shift-left_or_fusion.place_ref, bf16[2048,2048]{1,0:T(8,128)(2,1)} %get-tuple-element.207.refs_0_.refs_1_.refs_4_.refs_5_, bf16[2048,2048]{1,0:T(8,128)(2,1)} %get-tuple-element.207.refs_0_.refs_1_.refs_4_.refs_5_, ...), custom_call_target="tpu_custom_call" | custom-call | flops 343597376 | bytes 503316 | tf_op jit(solution)/shard_map/whole_sums/pallas_call | solution.py:540
  454.7 10.9 %partial_sums.17 = (bf16[256,2048]{1,0:T(8,128)(2,1)}, bf16[256,2048]{1,0:T(8,128)(2,1)}, bf16[256,2048]{1,0:T(8,128)(2,1)}, bf16[256,2048]{1,0:T(8,128)(2,1)}) custom-call(bf16[2048,1024]{1,0:T(8,128)(2,1)} %get-tuple-element.249.refs_0_.refs_1_, bf16[2048,1024]{1,0:T(8,128)(2,1)} %get-tuple-element.249.refs_0_.refs_1_, ...), custom_call_target="tpu_custom_call" | custom-call | flops 85899344 | bytes 293601 | tf_op jit(solution)/shard_map/partial_sums/pallas_call | solution.py:508
  465.6 34.7 %mlp_products.3 = (bf16[2048,1024]{1,0:T(8,128)(2,1)}, bf16[2048,2048]{1,0:T(8,128)(2,1)}) custom-call(bf16[1024,2048]{1,0:T(8,128)(2,1)} %constant_dynamic-update-slice_fusion.25.refs_0_.refs_2_, bf16[1024,2048]{1,0:T(8,128)(2,1)} %collective-permute-done.43.refs_1_.refs_3_, bf16[1024,2048]{1,0:T(8,128)(2,1)} %constant_dynamic-update-slice_fusion.15.refs_2_.refs_6_, ...), custom_call_target="tpu_custom_call" | custom-call | flops 515396064 | bytes 1174405 | tf_op jit(solution)/shard_map/mlp_products/pallas_call | solution.py:416
  500.4 24.8 %whole_sums.3 = bf16[2048,2048]{1,0:T(8,128)(2,1)} custom-call(s32[8]{0:T(128)} %shift-left_or_fusion.place_ref, bf16[2048,2048]{1,0:T(8,128)(2,1)} %get-tuple-element.221.refs_0_.refs_1_.refs_6_.refs_7_, bf16[2048,2048]{1,0:T(8,128)(2,1)} %get-tuple-element.221.refs_0_.refs_1_.refs_6_.refs_7_, ...), custom_call_target="tpu_custom_call" | custom-call | flops 343597376 | bytes 503316 | tf_op jit(solution)/shard_map/whole_sums/pallas_call | solution.py:540
  531.6 26.2 %weight_grad.5 = bf16[2048,1024]{1,0:T(8,128)(2,1)} custom-call(bf16[1024,2048]{1,0:T(8,128)(2,1)} %constant_dynamic-update-slice_fusion.20.refs_0_, bf16[1024,2048]{1,0:T(8,128)(2,1)} %collective-permute-done.33.refs_1_, bf16[1024,2048]{1,0:T(8,128)(2,1)} %constant_dynamic-update-slice_fusion.25.refs_0_.refs_2_, ...), custom_call_target="tpu_custom_call" | custom-call | flops 343597376 | bytes 503316 | tf_op jit(solution)/shard_map/weight_grad/pallas_call | solution.py:594
  570.0 24.6 %weight_grad.6 = bf16[2048,1024]{1,0:T(8,128)(2,1)} custom-call(bf16[1024,2048]{1,0:T(8,128)(2,1)} %constant_dynamic-update-slice_fusion.20.refs_0_, bf16[1024,2048]{1,0:T(8,128)(2,1)} %collective-permute-done.33.refs_1_, bf16[1024,2048]{1,0:T(8,128)(2,1)} %constant_dynamic-update-slice_fusion.25.refs_0_.refs_2_, ...), custom_call_target="tpu_custom_call" | custom-call | flops 343597376 | bytes 503316 | tf_op jit(solution)/shard_map/weight_grad/pallas_call | solution.py:594
  620.5 29.5 %attend_backward.2.refs_0_.refs_4_.refs_5_ = bf16[2048,768]{1,0:T(8,128)(2,1)} custom-call(s32[8]{0:T(128)} %and_select_fusion.low_ref, s32[8]{0:T(128)} %shift-left_or_fusion.place_ref, s32[8,1,256]{2,1,0:T(1,128)} %bitcast.97, bf16[2048,768]{1,0:T(8,128)(2,1)} %project_qkv.2.qkv_ref, bf16[2048,256]{1,0:T(8,128)(2,1)} %get-tuple-element.260.refs_0_.att_ref.refs_1_, ...), custom_call_target="tpu_custom_call" | custom-call | flops 286331072 | bytes 209715 | tf_op jit(solution)/shard_map/attend_backward/pallas_call | solution.py:781
  696.2 24.5 %weight_grad.7 = bf16[1024,2048]{1,0:T(8,128)(2,1)} custom-call(bf16[2048,1024]{1,0:T(8,128)(2,1)} %get-tuple-element.249.refs_0_.refs_1_, bf16[2048,1024]{1,0:T(8,128)(2,1)} %get-tuple-element.249.refs_0_.refs_1_, bf16[2048,1024]{1,0:T(8,128)(2,1)} %get-tuple-element.240.refs_0_.refs_1_.refs_2_.refs_3_, ...), custom_call_target="tpu_custom_call" | custom-call | flops 343597376 | bytes 671088 | tf_op jit(solution)/shard_map/weight_grad/pallas_call | solution.py:594
  745.6 10.4 %weight_grad.8 = bf16[256,2048]{1,0:T(8,128)(2,1)} custom-call(bf16[2048,256]{1,0:T(8,128)(2,1)} %get-tuple-element.260.refs_0_.att_ref.refs_1_, bf16[2048,256]{1,0:T(8,128)(2,1)} %get-tuple-element.260.refs_0_.att_ref.refs_1_, bf16[2048,256]{1,0:T(8,128)(2,1)} %get-tuple-element.194.refs_0_.att_ref.refs_2_.refs_3_, ...), custom_call_target="tpu_custom_call" | custom-call | flops 85899344 | bytes 419430 | tf_op jit(solution)/shard_map/weight_grad/pallas_call | solution.py:594
  756.0 29.3 %attend_backward.3.refs_0_.refs_6_.refs_7_ = bf16[2048,768]{1,0:T(8,128)(2,1)} custom-call(s32[8]{0:T(128)} %and_select_fusion.1.low_ref, s32[8]{0:T(128)} %shift-left_or_fusion.place_ref, s32[8,1,256]{2,1,0:T(1,128)} %bitcast.94, bf16[2048,768]{1,0:T(8,128)(2,1)} %project_qkv.3.qkv_ref, ...), custom_call_target="tpu_custom_call" | custom-call | flops 286331072 | bytes 209715 | tf_op jit(solution)/shard_map/attend_backward/pallas_call | solution.py:781
  816.4 19.3 %weight_grad.9 = bf16[2048,768]{1,0:T(8,128)(2,1)} custom-call(bf16[1024,2048]{1,0:T(8,128)(2,1)} %constant_dynamic-update-slice_fusion.refs_0_, bf16[1024,2048]{1,0:T(8,128)(2,1)} %collective-permute-done.9.refs_1_, bf16[1024,2048]{1,0:T(8,128)(2,1)} %constant_dynamic-update-slice_fusion.5.refs_0_.refs_2_, ...), custom_call_target="tpu_custom_call" | custom-call | flops 257698032 | bytes 461373 | tf_op jit(solution)/shard_map/weight_grad/pallas_call | solution.py:594
  858.8 11.8 %collective-permute-done.68 = bf16[256,2048]{1,0:T(8,128)(2,1)} collective-permute-done((bf16[256,2048]{1,0:T(8,128)(2,1)}, bf16[256,2048]{1,0:T(8,128)(2,1)}, u32[]{:S(2)}, u32[]{:S(2)}) %collective-permute-start.68) | collective-permute-done | bytes 1048608 | tf_op jit(solution)/shard_map/ppermute | solution.py:98
  880.2 25.8 %collective-permute-done.79 = bf16[256,512]{1,0:T(8,128)(2,1)} collective-permute-done((bf16[256,512]{1,0:T(8,128)(2,1)S(1)}, bf16[256,512]{1,0:T(8,128)(2,1)}, u32[]{:S(2)}, u32[]{:S(2)}) %collective-permute-start.79) | collective-permute-done | bytes 262176 | tf_op jit(solution)/shard_map/ppermute | solution.py:997
  (483 shorter events, 428.7 us)
Async XLA Ops:
  7.2 98.9 %all-gather.4.cloned.1.call-start = ((), (), s32[]{:S(2)}) async-start(), calls=%async_computation.6 | async-start | bytes 5242880 | tf_op jit(solution)/shard_map/all_gather | solution.py:858
  28.8 214.7 %all-gather.6.cloned.1.call-start = ((), (), s32[]{:S(2)}) async-start(), calls=%async_computation.7 | async-start | bytes 7864320 | tf_op jit(solution)/shard_map/all_gather | solution.py:858
  129.5 229.8 %all-gather.8.cloned.1.call-start = ((), (), s32[]{:S(2)}) async-start(), calls=%async_computation.8 | async-start | bytes 7864320 | tf_op jit(solution)/shard_map/all_gather | solution.py:858
  207.9 35.7 %collective-permute-start.21 = (bf16[256,2048]{1,0:T(8,128)(2,1)}, bf16[256,2048]{1,0:T(8,128)(2,1)}, u32[]{:S(2)}, u32[]{:S(2)}) collective-permute-start(bf16[256,2048]{1,0:T(8,128)(2,1)} %get-tuple-element.179), channel_id=1, source_target_pairs={{0,2},{1,3},{2,0},{3,1},{4,6},{5,7},{6,4},{7,5},{8,10},{9,11},{10,... | collective-permute-start | bytes 3145736 | tf_op jit(solution)/shard_map/ppermute | solution.py:98
  210.9 314.3 %reduce-scatter.7.cloned.1.call-start = ((), (), s32[]{:S(2)}) async-start(), calls=%async_computation.9 | async-start | bytes 9437184 | tf_op jit(solution)/shard_map/reduce_scatter | solution.py:1017
  320.2 39.1 %collective-permute-start.33 = (bf16[1024,2048]{1,0:T(8,128)(2,1)}, bf16[1024,2048]{1,0:T(8,128)(2,1)}, u32[]{:S(2)}, u32[]{:S(2)}) collective-permute-start(bf16[1024,2048]{1,0:T(8,128)(2,1)} %constant_dynamic-update-slice_fusion.20.refs_0_), channel_id=1, source_target_pairs={{0,1},{1,0},{2,3},{3,2},{4,5},{5,4},{6,7},{7,6},{8,9},{9,8},{10,11... | collective-permute-start | bytes 12582920 | tf_op jit(solution)/shard_map/ppermute | solution.py:98
  359.3 37.4 %collective-permute-start.36 = (bf16[128,2048]{1,0:T(8,128)(2,1)}, bf16[128,2048]{1,0:T(8,128)(2,1)S(1)}, u32[]{:S(2)}, u32[]{:S(2)}) collective-permute-start(bf16[128,2048]{1,0:T(8,128)(2,1)} %add_convert_fusion.11), channel_id=1, source_target_pairs={{0,4},{1,5},{2,6},{3,7},{4,0},{5,1},{6,2},{7,3},{8,12},{9,13},{10,... | collective-permute-start | bytes 1572872 | tf_op jit(solution)/shard_map/ppermute | solution.py:98
  360.8 36.0 %collective-permute-start.37 = (bf16[128,2048]{1,0:T(8,128)(2,1)}, bf16[128,2048]{1,0:T(8,128)(2,1)}, u32[]{:S(2)}, u32[]{:S(2)}) collective-permute-start(bf16[128,2048]{1,0:T(8,128)(2,1)} %add_convert_fusion.10), channel_id=1, source_target_pairs={{0,2},{1,3},{2,0},{3,1},{4,6},{5,7},{6,4},{7,5},{8,10},{9,11},{10,... | collective-permute-start | bytes 1572872 | tf_op jit(solution)/shard_map/ppermute | solution.py:98
  428.1 221.9 %reduce-scatter.9.cloned.1.call-start = ((), (), s32[]{:S(2)}) async-start(), calls=%async_computation.10 | async-start | bytes 9437184 | tf_op jit(solution)/shard_map/reduce_scatter | solution.py:1017
  525.2 208.7 %reduce-scatter.11.cloned.1.call-start = ((), (), s32[]{:S(2)}) async-start(), calls=%async_computation.11 | async-start | bytes 5242880 | tf_op jit(solution)/shard_map/reduce_scatter | solution.py:976
  567.6 232.8 %reduce-scatter.13.cloned.1.call-start = ((), (), s32[]{:S(2)}) async-start(), calls=%async_computation.12 | async-start | bytes 5242880 | tf_op jit(solution)/shard_map/reduce_scatter | solution.py:976
  608.2 41.8 %collective-permute-start.51 = (bf16[1024,2048]{1,0:T(8,128)(2,1)}, bf16[1024,2048]{1,0:T(8,128)(2,1)}, u32[]{:S(2)}, u32[]{:S(2)}) collective-permute-start(bf16[1024,2048]{1,0:T(8,128)(2,1)} %partial_sums.18), channel_id=1, source_target_pairs={{0,1},{1,0},{2,3},{3,2},{4,5},{5,4},{6,7},{7,6},{8,9},{9,8},{10,11... | collective-permute-start | bytes 12582920 | tf_op jit(solution)/shard_map/ppermute | solution.py:98
  608.7 41.3 %collective-permute-start.49 = (bf16[256,2048]{1,0:T(8,128)(2,1)}, bf16[256,2048]{1,0:T(8,128)(2,1)S(1)}, u32[]{:S(2)}, u32[]{:S(2)}) collective-permute-start(bf16[256,2048]{1,0:T(8,128)(2,1)} %get-tuple-element.232), channel_id=1, source_target_pairs={{0,2},{1,3},{2,0},{3,1},{4,6},{5,7},{6,4},{7,5},{8,10},{9,11},{10,... | collective-permute-start | bytes 3145736 | tf_op jit(solution)/shard_map/ppermute | solution.py:98
  610.8 39.1 %collective-permute-start.50 = (bf16[256,2048]{1,0:T(8,128)(2,1)}, bf16[256,2048]{1,0:T(8,128)(2,1)}, u32[]{:S(2)}, u32[]{:S(2)}) collective-permute-start(bf16[256,2048]{1,0:T(8,128)(2,1)} %get-tuple-element.236), channel_id=1, source_target_pairs={{0,4},{1,5},{2,6},{3,7},{4,0},{5,1},{6,2},{7,3},{8,12},{9,13},{10,... | collective-permute-start | bytes 3145736 | tf_op jit(solution)/shard_map/ppermute | solution.py:98
  612.7 259.9 %reduce-scatter.15.cloned.1.call-start = ((), (), s32[]{:S(2)}) async-start(), calls=%async_computation.13 | async-start | bytes 5242880 | tf_op jit(solution)/shard_map/reduce_scatter | solution.py:976
  681.7 42.8 %collective-permute-start.56 = (bf16[1024,2048]{1,0:T(8,128)(2,1)}, bf16[1024,2048]{1,0:T(8,128)(2,1)}, u32[]{:S(2)}, u32[]{:S(2)}) collective-permute-start(bf16[1024,2048]{1,0:T(8,128)(2,1)} %partial_sums.19), channel_id=1, source_target_pairs={{0,1},{1,0},{2,3},{3,2},{4,5},{5,4},{6,7},{7,6},{8,9},{9,8},{10,11... | collective-permute-start | bytes 12582920 | tf_op jit(solution)/shard_map/ppermute | solution.py:98
  724.6 204.0 %reduce-scatter.17.cloned.1.call-start = ((), (), s32[]{:S(2)}) async-start(), calls=%async_computation.14 | async-start | bytes 3932160 | tf_op jit(solution)/shard_map/reduce_scatter | solution.py:976
  733.9 51.4 %collective-permute-start.62 = (bf16[256,2048]{1,0:T(8,128)(2,1)}, bf16[256,2048]{1,0:T(8,128)(2,1)}, u32[]{:S(2)}, u32[]{:S(2)}) collective-permute-start(bf16[256,2048]{1,0:T(8,128)(2,1)} %get-tuple-element.264), channel_id=1, source_target_pairs={{0,4},{1,5},{2,6},{3,7},{4,0},{5,1},{6,2},{7,3},{8,12},{9,13},{10,... | collective-permute-start | bytes 3145736 | tf_op jit(solution)/shard_map/ppermute | solution.py:98
  735.7 51.7 %collective-permute-start.60 = (bf16[256,2048]{1,0:T(8,128)(2,1)}, bf16[256,2048]{1,0:T(8,128)(2,1)S(1)}, u32[]{:S(2)}, u32[]{:S(2)}) collective-permute-start(bf16[256,2048]{1,0:T(8,128)(2,1)} %get-tuple-element.257), channel_id=1, source_target_pairs={{0,2},{1,3},{2,0},{3,1},{4,6},{5,7},{6,4},{7,5},{8,10},{9,11},{10,... | collective-permute-start | bytes 3145736 | tf_op jit(solution)/shard_map/ppermute | solution.py:98
  736.6 50.8 %collective-permute-start.61 = (bf16[256,2048]{1,0:T(8,128)(2,1)}, bf16[256,2048]{1,0:T(8,128)(2,1)}, u32[]{:S(2)}, u32[]{:S(2)}) collective-permute-start(bf16[256,2048]{1,0:T(8,128)(2,1)} %get-tuple-element.262), channel_id=1, source_target_pairs={{0,2},{1,3},{2,0},{3,1},{4,6},{5,7},{6,4},{7,5},{8,10},{9,11},{10,... | collective-permute-start | bytes 3145736 | tf_op jit(solution)/shard_map/ppermute | solution.py:98
  737.8 49.7 %collective-permute-start.63 = (bf16[256,2048]{1,0:T(8,128)(2,1)}, bf16[256,2048]{1,0:T(8,128)(2,1)}, u32[]{:S(2)}, u32[]{:S(2)}) collective-permute-start(bf16[256,2048]{1,0:T(8,128)(2,1)} %get-tuple-element.266), channel_id=1, source_target_pairs={{0,4},{1,5},{2,6},{3,7},{4,0},{5,1},{6,2},{7,3},{8,12},{9,13},{10,... | collective-permute-start | bytes 3145736 | tf_op jit(solution)/shard_map/ppermute | solution.py:98
  854.9 51.1 %collective-permute-start.79 = (bf16[256,512]{1,0:T(8,128)(2,1)S(1)}, bf16[256,512]{1,0:T(8,128)(2,1)}, u32[]{:S(2)}, u32[]{:S(2)}) collective-permute-start(bf16[256,512]{1,0:T(8,128)(2,1)S(1)} %get-tuple-element.335), channel_id=1, source_target_pairs={{0,16},{8,24},{16,0},{24,8},{1,17},{9,25},{17,1},{25,9},{2,18},{10... | collective-permute-start | bytes 786440 | tf_op jit(solution)/shard_map/ppermute | solution.py:997
  874.3 36.5 %collective-permute-start.71 = (bf16[128,2048]{1,0:T(8,128)(2,1)S(1)}, bf16[128,2048]{1,0:T(8,128)(2,1)S(1)}, u32[]{:S(2)}, u32[]{:S(2)}) collective-permute-start(bf16[128,2048]{1,0:T(8,128)(2,1)S(1)} %add_convert_fusion.3), channel_id=1, source_target_pairs={{0,4},{1,5},{2,6},{3,7},{4,0},{5,1},{6,2},{7,3},{8,12},{9,13},{10,... | collective-permute-start | bytes 1572872 | tf_op jit(solution)/shard_map/ppermute | solution.py:98
  876.0 34.9 %collective-permute-start.72 = (bf16[128,2048]{1,0:T(8,128)(2,1)}, bf16[128,2048]{1,0:T(8,128)(2,1)S(1)}, u32[]{:S(2)}, u32[]{:S(2)}) collective-permute-start(bf16[128,2048]{1,0:T(8,128)(2,1)} %add_convert_fusion.2), channel_id=1, source_target_pairs={{0,2},{1,3},{2,0},{3,1},{4,6},{5,7},{6,4},{7,5},{8,10},{9,11},{10,... | collective-permute-start | bytes 1572872 | tf_op jit(solution)/shard_map/ppermute | solution.py:98
  (130 other events, 2271.2 us)
Sparse Core Ops, SparseCore 0:
  29.0 77.1 all-gather.3
  129.6 113.9 all-gather.5
  245.7 113.5 all-gather.7
  428.2 74.0 reduce-scatter.6
  525.3 82.5 reduce-scatter.8
  610.1 76.9 reduce-scatter.10
  689.5 77.2 reduce-scatter.12
  769.1 77.2 reduce-scatter.14
  848.8 75.7 reduce-scatter.16

commit v4 on v3

--- a/solution.py
+++ b/solution.py
@@ -991,11 +991,11 @@
             def block(number):
                 return lax.dynamic_slice_in_dim(gate(grad), (number % narrow) * size, size, 1)
 
-            total = block(here).astype(F32)
+            pieces = [block(here)]
             for step in range(1, narrow):
                 pairs = [(i, (i + step) % narrow) for i in range(narrow)]
-                total = total + lax.ppermute(block(here + step), "narrow", pairs).astype(F32)
-            grad_attn["out"] = total
+                pieces.append(lax.ppermute(block(here + step), "narrow", pairs))
+            grad_attn["out"] = pieces
 
         return start
 
@@ -1143,6 +1143,8 @@
     sums[two].last()
     down[two].last(False)
     turn()
+    pieces = [gate(piece).astype(F32) for piece in grad_attn["out"]]
+    grad_attn["out"] = sum(pieces[1:], pieces[0])
     for r in rows:
         outputs[r] = (middle[r] + down[r].total).astype(BF16)
         after_back(r, sums[r].total)

time: 955 us -> 963 us (level)
  Pallas kernels: 452 us -> 463 us
    ppermute x3, waiting for transfers between devices: 25.8 us -> 0.01 us  [start(): pieces.append(lax.ppermute(block(here + step), 'narrow', pairs))]
    ppermute x5, waiting for transfers between devices: 4.21 us -> 23.2 us  [per_device(): lax.ppermute(sent, axis, [(i, i ^ 1 << bit) for i in range(count)])]
    ppermute x70, waiting for transfers between devices: 164 us -> 173 us  [swap(): got = lax.ppermute(self.gate(block), axis, pairs)]
    unnamed x155 -> x157, local copies, waits for them, and re-layouts: 47.6 us -> 48.7 us
  transfers between devices with their start and end apart: 90 -> 90, of which waited for: 34 -> 34; matrix products, arithmetic and copies ran while one was open for 16% -> 17% of each run, Pallas kernels for 48% -> 49%
where the time goes in v4:
time: 963 us; the launch traced here: 952 us
  Pallas kernels  463 us (48%)
  waiting for transfers between devices  227 us (24%)
  other arithmetic  93.8 us (10%)
  local copies, waits for them, and re-layouts  84.7 us (9%)
  starting transfers between devices  68.6 us (7%)
  between operations  15.2 us (2%)
    ppermute x70, waiting for transfers between devices, swap(): got = lax.ppermute(self.gate(block), axis, pairs)  173 us
    pallas_call x5, Pallas kernels, weight_grad(): pl.pallas_call(kernel, out_shape=jax.ShapeDtypeStruct((height, cols), BF1...  105 us
    pallas_call x12, Pallas kernels, partial_sums(): pl.pallas_call(kernel, out_shape=out_shape, grid=(steps,), in_specs=in_sp...  93.7 us
    pallas_call x2, Pallas kernels, mlp_products(): pl.pallas_call(kernel, out_shape=[jax.ShapeDtypeStruct((seq, parts * cut)...  69.3 us
    pallas_call x2, Pallas kernels, attend_backward(): pl.pallas_call(functools.partial(backward_kernel, heads, blocks, size), o...  64.8 us
    ppermute x70, starting transfers between devices, swap(): got = lax.ppermute(self.gate(block), axis, pairs)  55.2 us
    pallas_call x2, Pallas kernels, whole_sums(): pl.pallas_call(kernel, out_shape=jax.ShapeDtypeStruct((seq, dim), BF16),...  49.5 us
    unnamed x157, local copies, waits for them, and re-layouts  48.7 us
  transfers between devices with their start and end apart: 90, of which 34 were waited for; matrix products, arithmetic and copies ran while one was open for 17% of the time, Pallas kernels for 49%

profile of v4, /device:TPU:0, one launch (start us, length us, event | category | flops | bytes accessed | tf_op | source)
XLA Modules:
  0.0 951.9 jit_solution(12651183832016818645)
XLA Ops:
  28.4 17.8 %collective-permute-done.3 = bf16[256,2048]{1,0:T(8,128)(2,1)S(1)} collective-permute-done((bf16[256,2048]{1,0:T(8,128)(2,1)}, bf16[256,2048]{1,0:T(8,128)(2,1)S(1)}, u32[]{:S(2)}, u32[]{:S(2)}) %collective-permute-start.3) | collective-permute-done | bytes 1048608 | tf_op jit(solution)/shard_map/ppermute | solution.py:98
  80.1 16.1 %collective-permute-done.8 = bf16[256,2048]{1,0:T(8,128)(2,1)S(1)} collective-permute-done((bf16[256,2048]{1,0:T(8,128)(2,1)}, bf16[256,2048]{1,0:T(8,128)(2,1)S(1)}, u32[]{:S(2)}, u32[]{:S(2)}) %collective-permute-start.8) | collective-permute-done | bytes 1048608 | tf_op jit(solution)/shard_map/ppermute | solution.py:98
  113.7 12.8 %project_qkv.2.qkv_ref = bf16[2048,768]{1,0:T(8,128)(2,1)} custom-call(bf16[1024,2048]{1,0:T(8,128)(2,1)} %constant_dynamic-update-slice_fusion.refs_0_, bf16[1024,2048]{1,0:T(8,128)(2,1)} %collective-permute-done.9.refs_1_, bf16[2048,1024]{1,0:T(8,128)(2,1)} %all-gather.4.cloned.1.call-done.refs_2_.refs_1_, f32[2048,128]{1,0:T(8,128)} %pad_maximum_fusion.9.refs_3_.cos_ref, ...), custom_call_target="tpu_custom_call" | custom-call | flops 128849016 | bytes 293601 | tf_op jit(solution)/shard_map/project_qkv/pallas_call | solution.py:256
  133.4 21.0 %attend_forward.2 = (bf16[2048,256]{1,0:T(8,128)(2,1)}, f32[8,4,256]{2,1,0:T(4,128)}) custom-call(s32[8]{0:T(128)} %and_select_fusion.low_ref, s32[8]{0:T(128)} %shift-left_or_fusion.place_ref, s32[8,1,256]{2,1,0:T(1,128)} %bitcast.96, bf16[2048,768]{1,0:T(8,128)(2,1)} %project_qkv.2.qkv_ref), custom_call_target="tpu_custom_call" | custom-call | flops 114532432 | bytes 83886 | tf_op jit(solution)/shard_map/attend_forward/pallas_call | solution.py:674
  170.2 12.7 %project_qkv.3.qkv_ref = bf16[2048,768]{1,0:T(8,128)(2,1)} custom-call(bf16[1024,2048]{1,0:T(8,128)(2,1)} %constant_dynamic-update-slice_fusion.5.refs_0_.refs_2_, bf16[1024,2048]{1,0:T(8,128)(2,1)} %collective-permute-done.12.refs_1_.refs_3_, bf16[2048,1024]{1,0:T(8,128)(2,1)} %all-gather.4.cloned.1.call-done.refs_2_.refs_1_, ...), custom_call_target="tpu_custom_call" | custom-call | flops 128849016 | bytes 293601 | tf_op jit(solution)/shard_map/project_qkv/pallas_call | solution.py:256
  194.4 17.0 %collective-permute-done.20 = bf16[256,2048]{1,0:T(8,128)(2,1)S(1)} collective-permute-done((bf16[256,2048]{1,0:T(8,128)(2,1)S(1)}, bf16[256,2048]{1,0:T(8,128)(2,1)S(1)}, u32[]{:S(2)}, u32[]{:S(2)}) %collective-permute-start.20) | collective-permute-done | bytes 1048608 | tf_op jit(solution)/shard_map/ppermute | solution.py:98
  218.3 18.6 %attend_forward.3 = (bf16[2048,256]{1,0:T(8,128)(2,1)}, f32[8,4,256]{2,1,0:T(4,128)}) custom-call(s32[8]{0:T(128)} %and_select_fusion.1.low_ref, s32[8]{0:T(128)} %shift-left_or_fusion.place_ref, s32[8,1,256]{2,1,0:T(1,128)} %bitcast.93, bf16[2048,768]{1,0:T(8,128)(2,1)} %project_qkv.3.qkv_ref), custom_call_target="tpu_custom_call" | custom-call | flops 114532432 | bytes 83886 | tf_op jit(solution)/shard_map/attend_forward/pallas_call | solution.py:674
  280.7 23.5 %collective-permute-done.28 = bf16[256,2048]{1,0:T(8,128)(2,1)S(1)} collective-permute-done((bf16[256,2048]{1,0:T(8,128)(2,1)S(1)}, bf16[256,2048]{1,0:T(8,128)(2,1)S(1)}, u32[]{:S(2)}, u32[]{:S(2)}) %collective-permute-start.28) | collective-permute-done | bytes 1048608 | tf_op jit(solution)/shard_map/ppermute | solution.py:98
  324.3 24.2 %collective-permute-done.34 = bf16[256,2048]{1,0:T(8,128)(2,1)S(1)} collective-permute-done((bf16[256,2048]{1,0:T(8,128)(2,1)}, bf16[256,2048]{1,0:T(8,128)(2,1)S(1)}, u32[]{:S(2)}, u32[]{:S(2)}) %collective-permute-start.34) | collective-permute-done | bytes 1048608 | tf_op jit(solution)/shard_map/ppermute | solution.py:98
  364.7 34.5 %mlp_products.2 = (bf16[2048,1024]{1,0:T(8,128)(2,1)}, bf16[2048,2048]{1,0:T(8,128)(2,1)}) custom-call(bf16[1024,2048]{1,0:T(8,128)(2,1)} %constant_dynamic-update-slice_fusion.20.refs_0_, bf16[1024,2048]{1,0:T(8,128)(2,1)} %collective-permute-done.33.refs_1_, bf16[1024,2048]{1,0:T(8,128)(2,1)} %constant_dynamic-update-slice_fusion.10.refs_2_.refs_4_, ...), custom_call_target="tpu_custom_call" | custom-call | flops 515396064 | bytes 1174405 | tf_op jit(solution)/shard_map/mlp_products/pallas_call | solution.py:416
  405.9 24.7 %whole_sums.2 = bf16[2048,2048]{1,0:T(8,128)(2,1)} custom-call(s32[8]{0:T(128)} %shift-left_or_fusion.place_ref, bf16[2048,2048]{1,0:T(8,128)(2,1)} %get-tuple-element.211.refs_0_.refs_1_.refs_4_.refs_5_, bf16[2048,2048]{1,0:T(8,128)(2,1)} %get-tuple-element.211.refs_0_.refs_1_.refs_4_.refs_5_, ...), custom_call_target="tpu_custom_call" | custom-call | flops 343597376 | bytes 503316 | tf_op jit(solution)/shard_map/whole_sums/pallas_call | solution.py:540
  457.2 10.9 %partial_sums.17 = (bf16[256,2048]{1,0:T(8,128)(2,1)}, bf16[256,2048]{1,0:T(8,128)(2,1)}, bf16[256,2048]{1,0:T(8,128)(2,1)}, bf16[256,2048]{1,0:T(8,128)(2,1)}) custom-call(bf16[2048,1024]{1,0:T(8,128)(2,1)} %get-tuple-element.253.refs_0_.refs_1_, bf16[2048,1024]{1,0:T(8,128)(2,1)} %get-tuple-element.253.refs_0_.refs_1_, ...), custom_call_target="tpu_custom_call" | custom-call | flops 85899344 | bytes 293601 | tf_op jit(solution)/shard_map/partial_sums/pallas_call | solution.py:508
  468.1 34.8 %mlp_products.3 = (bf16[2048,1024]{1,0:T(8,128)(2,1)}, bf16[2048,2048]{1,0:T(8,128)(2,1)}) custom-call(bf16[1024,2048]{1,0:T(8,128)(2,1)} %constant_dynamic-update-slice_fusion.25.refs_0_.refs_2_, bf16[1024,2048]{1,0:T(8,128)(2,1)} %collective-permute-done.43.refs_1_.refs_3_, bf16[1024,2048]{1,0:T(8,128)(2,1)} %constant_dynamic-update-slice_fusion.15.refs_2_.refs_6_, ...), custom_call_target="tpu_custom_call" | custom-call | flops 515396064 | bytes 1174405 | tf_op jit(solution)/shard_map/mlp_products/pallas_call | solution.py:416
  502.9 24.8 %whole_sums.3 = bf16[2048,2048]{1,0:T(8,128)(2,1)} custom-call(s32[8]{0:T(128)} %shift-left_or_fusion.place_ref, bf16[2048,2048]{1,0:T(8,128)(2,1)} %get-tuple-element.225.refs_0_.refs_1_.refs_6_.refs_7_, bf16[2048,2048]{1,0:T(8,128)(2,1)} %get-tuple-element.225.refs_0_.refs_1_.refs_6_.refs_7_, ...), custom_call_target="tpu_custom_call" | custom-call | flops 343597376 | bytes 503316 | tf_op jit(solution)/shard_map/whole_sums/pallas_call | solution.py:540
  534.1 26.4 %weight_grad.5 = bf16[2048,1024]{1,0:T(8,128)(2,1)} custom-call(bf16[1024,2048]{1,0:T(8,128)(2,1)} %constant_dynamic-update-slice_fusion.20.refs_0_, bf16[1024,2048]{1,0:T(8,128)(2,1)} %collective-permute-done.33.refs_1_, bf16[1024,2048]{1,0:T(8,128)(2,1)} %constant_dynamic-update-slice_fusion.25.refs_0_.refs_2_, ...), custom_call_target="tpu_custom_call" | custom-call | flops 343597376 | bytes 503316 | tf_op jit(solution)/shard_map/weight_grad/pallas_call | solution.py:594
  572.2 24.3 %weight_grad.6 = bf16[2048,1024]{1,0:T(8,128)(2,1)} custom-call(bf16[1024,2048]{1,0:T(8,128)(2,1)} %constant_dynamic-update-slice_fusion.20.refs_0_, bf16[1024,2048]{1,0:T(8,128)(2,1)} %collective-permute-done.33.refs_1_, bf16[1024,2048]{1,0:T(8,128)(2,1)} %constant_dynamic-update-slice_fusion.25.refs_0_.refs_2_, ...), custom_call_target="tpu_custom_call" | custom-call | flops 343597376 | bytes 503316 | tf_op jit(solution)/shard_map/weight_grad/pallas_call | solution.py:594
  622.4 34.4 %attend_backward.2.refs_0_.refs_4_.refs_5_ = bf16[2048,768]{1,0:T(8,128)(2,1)} custom-call(s32[8]{0:T(128)} %and_select_fusion.low_ref, s32[8]{0:T(128)} %shift-left_or_fusion.place_ref, s32[8,1,256]{2,1,0:T(1,128)} %bitcast.97, bf16[2048,768]{1,0:T(8,128)(2,1)} %project_qkv.2.qkv_ref, bf16[2048,256]{1,0:T(8,128)(2,1)} %get-tuple-element.264.refs_0_.att_ref.refs_1_, ...), custom_call_target="tpu_custom_call" | custom-call | flops 286331072 | bytes 209715 | tf_op jit(solution)/shard_map/attend_backward/pallas_call | solution.py:781
  671.4 10.2 %partial_sums.20 = (bf16[256,2048]{1,0:T(8,128)(2,1)}, bf16[256,2048]{1,0:T(8,128)(2,1)}, bf16[256,2048]{1,0:T(8,128)(2,1)}, bf16[256,2048]{1,0:T(8,128)(2,1)}) custom-call(bf16[2048,1024]{1,0:T(8,128)(2,1)} %get-tuple-element.244.refs_0_.refs_1_.refs_2_.refs_3_, bf16[2048,1024]{1,0:T(8,128)(2,1)} %get-tuple-element.244.refs_0_.refs_1_.refs_2_.refs_3_, ...), custom_call_target="tpu_custom_call" | custom-call | flops 85899344 | bytes 293601 | tf_op jit(solution)/shard_map/partial_sums/pallas_call | solution.py:508
  702.7 24.6 %weight_grad.7 = bf16[1024,2048]{1,0:T(8,128)(2,1)} custom-call(bf16[2048,1024]{1,0:T(8,128)(2,1)} %get-tuple-element.253.refs_0_.refs_1_, bf16[2048,1024]{1,0:T(8,128)(2,1)} %get-tuple-element.253.refs_0_.refs_1_, bf16[2048,1024]{1,0:T(8,128)(2,1)} %get-tuple-element.244.refs_0_.refs_1_.refs_2_.refs_3_, ...), custom_call_target="tpu_custom_call" | custom-call | flops 343597376 | bytes 671088 | tf_op jit(solution)/shard_map/weight_grad/pallas_call | solution.py:594
  752.1 10.2 %weight_grad.8 = bf16[256,2048]{1,0:T(8,128)(2,1)} custom-call(bf16[2048,256]{1,0:T(8,128)(2,1)} %get-tuple-element.264.refs_0_.att_ref.refs_1_, bf16[2048,256]{1,0:T(8,128)(2,1)} %get-tuple-element.264.refs_0_.att_ref.refs_1_, bf16[2048,256]{1,0:T(8,128)(2,1)} %get-tuple-element.198.refs_0_.att_ref.refs_2_.refs_3_, ...), custom_call_target="tpu_custom_call" | custom-call | flops 85899344 | bytes 419430 | tf_op jit(solution)/shard_map/weight_grad/pallas_call | solution.py:594
  762.4 30.4 %attend_backward.3.refs_0_.refs_6_.refs_7_ = bf16[2048,768]{1,0:T(8,128)(2,1)} custom-call(s32[8]{0:T(128)} %and_select_fusion.1.low_ref, s32[8]{0:T(128)} %shift-left_or_fusion.place_ref, s32[8,1,256]{2,1,0:T(1,128)} %bitcast.94, bf16[2048,768]{1,0:T(8,128)(2,1)} %project_qkv.3.qkv_ref, ...), custom_call_target="tpu_custom_call" | custom-call | flops 286331072 | bytes 209715 | tf_op jit(solution)/shard_map/attend_backward/pallas_call | solution.py:781
  821.1 19.3 %weight_grad.9 = bf16[2048,768]{1,0:T(8,128)(2,1)} custom-call(bf16[1024,2048]{1,0:T(8,128)(2,1)} %constant_dynamic-update-slice_fusion.refs_0_, bf16[1024,2048]{1,0:T(8,128)(2,1)} %collective-permute-done.9.refs_1_, bf16[1024,2048]{1,0:T(8,128)(2,1)} %constant_dynamic-update-slice_fusion.5.refs_0_.refs_2_, ...), custom_call_target="tpu_custom_call" | custom-call | flops 257698032 | bytes 461373 | tf_op jit(solution)/shard_map/weight_grad/pallas_call | solution.py:594
  857.2 18.4 %collective-permute-done.68 = bf16[256,2048]{1,0:T(8,128)(2,1)} collective-permute-done((bf16[256,2048]{1,0:T(8,128)(2,1)}, bf16[256,2048]{1,0:T(8,128)(2,1)}, u32[]{:S(2)}, u32[]{:S(2)}) %collective-permute-start.68) | collective-permute-done | bytes 1048608 | tf_op jit(solution)/shard_map/ppermute | solution.py:98
  910.0 22.2 %collective-permute-done.73 = f32[2,1024]{1,0:T(2,128)S(1)} collective-permute-done((f32[2,1024]{1,0:T(2,128)S(1)}, f32[2,1024]{1,0:T(2,128)S(1)}, u32[]{:S(2)}, u32[]{:S(2)}) %collective-permute-start.73) | collective-permute-done | bytes 8224 | tf_op jit(solution)/shard_map/ppermute | solution.py:1163
  (485 shorter events, 422.7 us)
Async XLA Ops:
  7.2 98.4 %all-gather.4.cloned.1.call-start = ((), (), s32[]{:S(2)}) async-start(), calls=%async_computation.6 | async-start | bytes 5242880 | tf_op jit(solution)/shard_map/all_gather | solution.py:858
  28.3 217.8 %all-gather.6.cloned.1.call-start = ((), (), s32[]{:S(2)}) async-start(), calls=%async_computation.7 | async-start | bytes 7864320 | tf_op jit(solution)/shard_map/all_gather | solution.py:858
  132.0 229.8 %all-gather.8.cloned.1.call-start = ((), (), s32[]{:S(2)}) async-start(), calls=%async_computation.8 | async-start | bytes 7864320 | tf_op jit(solution)/shard_map/all_gather | solution.py:858
  214.6 313.1 %reduce-scatter.7.cloned.1.call-start = ((), (), s32[]{:S(2)}) async-start(), calls=%async_computation.9 | async-start | bytes 9437184 | tf_op jit(solution)/shard_map/reduce_scatter | solution.py:1017
  322.7 39.1 %collective-permute-start.33 = (bf16[1024,2048]{1,0:T(8,128)(2,1)}, bf16[1024,2048]{1,0:T(8,128)(2,1)}, u32[]{:S(2)}, u32[]{:S(2)}) collective-permute-start(bf16[1024,2048]{1,0:T(8,128)(2,1)} %constant_dynamic-update-slice_fusion.20.refs_0_), channel_id=1, source_target_pairs={{0,1},{1,0},{2,3},{3,2},{4,5},{5,4},{6,7},{7,6},{8,9},{9,8},{10,11... | collective-permute-start | bytes 12582920 | tf_op jit(solution)/shard_map/ppermute | solution.py:98
  361.8 37.5 %collective-permute-start.36 = (bf16[128,2048]{1,0:T(8,128)(2,1)}, bf16[128,2048]{1,0:T(8,128)(2,1)S(1)}, u32[]{:S(2)}, u32[]{:S(2)}) collective-permute-start(bf16[128,2048]{1,0:T(8,128)(2,1)} %add_convert_fusion.11), channel_id=1, source_target_pairs={{0,4},{1,5},{2,6},{3,7},{4,0},{5,1},{6,2},{7,3},{8,12},{9,13},{10,... | collective-permute-start | bytes 1572872 | tf_op jit(solution)/shard_map/ppermute | solution.py:98
  363.2 36.0 %collective-permute-start.37 = (bf16[128,2048]{1,0:T(8,128)(2,1)}, bf16[128,2048]{1,0:T(8,128)(2,1)}, u32[]{:S(2)}, u32[]{:S(2)}) collective-permute-start(bf16[128,2048]{1,0:T(8,128)(2,1)} %add_convert_fusion.10), channel_id=1, source_target_pairs={{0,2},{1,3},{2,0},{3,1},{4,6},{5,7},{6,4},{7,5},{8,10},{9,11},{10,... | collective-permute-start | bytes 1572872 | tf_op jit(solution)/shard_map/ppermute | solution.py:98
  430.6 226.2 %reduce-scatter.9.cloned.1.call-start = ((), (), s32[]{:S(2)}) async-start(), calls=%async_computation.10 | async-start | bytes 9437184 | tf_op jit(solution)/shard_map/reduce_scatter | solution.py:1017
  527.7 212.7 %reduce-scatter.11.cloned.1.call-start = ((), (), s32[]{:S(2)}) async-start(), calls=%async_computation.11 | async-start | bytes 5242880 | tf_op jit(solution)/shard_map/reduce_scatter | solution.py:976
  601.4 205.1 %reduce-scatter.13.cloned.1.call-start = ((), (), s32[]{:S(2)}) async-start(), calls=%async_computation.12 | async-start | bytes 5242880 | tf_op jit(solution)/shard_map/reduce_scatter | solution.py:976
  610.3 46.4 %collective-permute-start.51 = (bf16[1024,2048]{1,0:T(8,128)(2,1)}, bf16[1024,2048]{1,0:T(8,128)(2,1)}, u32[]{:S(2)}, u32[]{:S(2)}) collective-permute-start(bf16[1024,2048]{1,0:T(8,128)(2,1)} %partial_sums.18), channel_id=1, source_target_pairs={{0,1},{1,0},{2,3},{3,2},{4,5},{5,4},{6,7},{7,6},{8,9},{9,8},{10,11... | collective-permute-start | bytes 12582920 | tf_op jit(solution)/shard_map/ppermute | solution.py:98
  610.8 46.0 %collective-permute-start.49 = (bf16[256,2048]{1,0:T(8,128)(2,1)}, bf16[256,2048]{1,0:T(8,128)(2,1)}, u32[]{:S(2)}, u32[]{:S(2)}) collective-permute-start(bf16[256,2048]{1,0:T(8,128)(2,1)} %get-tuple-element.236), channel_id=1, source_target_pairs={{0,2},{1,3},{2,0},{3,1},{4,6},{5,7},{6,4},{7,5},{8,10},{9,11},{10,... | collective-permute-start | bytes 3145736 | tf_op jit(solution)/shard_map/ppermute | solution.py:98
  613.0 43.7 %collective-permute-start.50 = (bf16[256,2048]{1,0:T(8,128)(2,1)S(1)}, bf16[256,2048]{1,0:T(8,128)(2,1)}, u32[]{:S(2)}, u32[]{:S(2)}) collective-permute-start(bf16[256,2048]{1,0:T(8,128)(2,1)S(1)} %copy-done.64), channel_id=1, source_target_pairs={{0,4},{1,5},{2,6},{3,7},{4,0},{5,1},{6,2},{7,3},{8,12},{9,13},{10,... | collective-permute-start | bytes 3145736 | tf_op jit(solution)/shard_map/ppermute | solution.py:98
  663.7 216.8 %reduce-scatter.15.cloned.1.call-start = ((), (), s32[]{:S(2)}) async-start(), calls=%async_computation.13 | async-start | bytes 5242880 | tf_op jit(solution)/shard_map/reduce_scatter | solution.py:976
  687.9 43.2 %collective-permute-start.56 = (bf16[1024,2048]{1,0:T(8,128)(2,1)}, bf16[1024,2048]{1,0:T(8,128)(2,1)}, u32[]{:S(2)}, u32[]{:S(2)}) collective-permute-start(bf16[1024,2048]{1,0:T(8,128)(2,1)} %partial_sums.19), channel_id=1, source_target_pairs={{0,1},{1,0},{2,3},{3,2},{4,5},{5,4},{6,7},{7,6},{8,9},{9,8},{10,11... | collective-permute-start | bytes 12582920 | tf_op jit(solution)/shard_map/ppermute | solution.py:98
  696.0 35.1 %collective-permute-start.54 = (bf16[128,2048]{1,0:T(8,128)(2,1)}, bf16[128,2048]{1,0:T(8,128)(2,1)}, u32[]{:S(2)}, u32[]{:S(2)}) collective-permute-start(bf16[128,2048]{1,0:T(8,128)(2,1)} %add_convert_fusion.9), channel_id=1, source_target_pairs={{0,4},{1,5},{2,6},{3,7},{4,0},{5,1},{6,2},{7,3},{8,12},{9,13},{10,... | collective-permute-start | bytes 1572872 | tf_op jit(solution)/shard_map/ppermute | solution.py:98
  731.2 204.9 %reduce-scatter.17.cloned.1.call-start = ((), (), s32[]{:S(2)}) async-start(), calls=%async_computation.14 | async-start | bytes 3932160 | tf_op jit(solution)/shard_map/reduce_scatter | solution.py:976
  740.4 52.4 %collective-permute-start.62 = (bf16[256,2048]{1,0:T(8,128)(2,1)}, bf16[256,2048]{1,0:T(8,128)(2,1)}, u32[]{:S(2)}, u32[]{:S(2)}) collective-permute-start(bf16[256,2048]{1,0:T(8,128)(2,1)} %get-tuple-element.268), channel_id=1, source_target_pairs={{0,4},{1,5},{2,6},{3,7},{4,0},{5,1},{6,2},{7,3},{8,12},{9,13},{10,... | collective-permute-start | bytes 3145736 | tf_op jit(solution)/shard_map/ppermute | solution.py:98
  741.5 53.5 %collective-permute-start.60 = (bf16[256,2048]{1,0:T(8,128)(2,1)}, bf16[256,2048]{1,0:T(8,128)(2,1)S(1)}, u32[]{:S(2)}, u32[]{:S(2)}) collective-permute-start(bf16[256,2048]{1,0:T(8,128)(2,1)} %get-tuple-element.261), channel_id=1, source_target_pairs={{0,2},{1,3},{2,0},{3,1},{4,6},{5,7},{6,4},{7,5},{8,10},{9,11},{10,... | collective-permute-start | bytes 3145736 | tf_op jit(solution)/shard_map/ppermute | solution.py:98
  741.9 53.0 %collective-permute-start.61 = (bf16[256,2048]{1,0:T(8,128)(2,1)}, bf16[256,2048]{1,0:T(8,128)(2,1)}, u32[]{:S(2)}, u32[]{:S(2)}) collective-permute-start(bf16[256,2048]{1,0:T(8,128)(2,1)} %get-tuple-element.266), channel_id=1, source_target_pairs={{0,2},{1,3},{2,0},{3,1},{4,6},{5,7},{6,4},{7,5},{8,10},{9,11},{10,... | collective-permute-start | bytes 3145736 | tf_op jit(solution)/shard_map/ppermute | solution.py:98
  743.5 51.4 %collective-permute-start.63 = (bf16[256,2048]{1,0:T(8,128)(2,1)}, bf16[256,2048]{1,0:T(8,128)(2,1)}, u32[]{:S(2)}, u32[]{:S(2)}) collective-permute-start(bf16[256,2048]{1,0:T(8,128)(2,1)} %get-tuple-element.270), channel_id=1, source_target_pairs={{0,4},{1,5},{2,6},{3,7},{4,0},{5,1},{6,2},{7,3},{8,12},{9,13},{10,... | collective-permute-start | bytes 3145736 | tf_op jit(solution)/shard_map/ppermute | solution.py:98
  886.0 53.0 %collective-permute-start.80 = (bf16[256,512]{1,0:T(8,128)(2,1)}, bf16[256,512]{1,0:T(8,128)(2,1)}, u32[]{:S(2)}, u32[]{:S(2)}) collective-permute-start(bf16[256,512]{1,0:T(8,128)(2,1)} %get-tuple-element.342), channel_id=1, source_target_pairs={{0,24},{8,0},{16,8},{24,16},{1,25},{9,1},{17,9},{25,17},{2,26},{10... | collective-permute-start | bytes 786440 | tf_op jit(solution)/shard_map/ppermute | solution.py:997
  886.0 53.0 %collective-permute-start.79 = (bf16[256,512]{1,0:T(8,128)(2,1)}, bf16[256,512]{1,0:T(8,128)(2,1)}, u32[]{:S(2)}, u32[]{:S(2)}) collective-permute-start(bf16[256,512]{1,0:T(8,128)(2,1)} %get-tuple-element.343), channel_id=1, source_target_pairs={{0,16},{8,24},{16,0},{24,8},{1,17},{9,25},{17,1},{25,9},{2,18},{10... | collective-permute-start | bytes 786440 | tf_op jit(solution)/shard_map/ppermute | solution.py:997
  886.0 53.0 %collective-permute-start.78 = (bf16[256,512]{1,0:T(8,128)(2,1)}, bf16[256,512]{1,0:T(8,128)(2,1)}, u32[]{:S(2)}, u32[]{:S(2)}) collective-permute-start(bf16[256,512]{1,0:T(8,128)(2,1)} %get-tuple-element.344), channel_id=1, source_target_pairs={{0,8},{8,16},{16,24},{24,0},{1,9},{9,17},{17,25},{25,1},{2,10},{10... | collective-permute-start | bytes 786440 | tf_op jit(solution)/shard_map/ppermute | solution.py:997
  (131 other events, 2210.1 us)
Sparse Core Ops, SparseCore 0:
  28.4 77.1 all-gather.3
  132.1 113.8 all-gather.5
  248.2 113.5 all-gather.7
  430.7 74.1 reduce-scatter.6
  527.9 82.6 reduce-scatter.8
  612.7 77.7 reduce-scatter.10
  692.9 77.2 reduce-scatter.12
  772.5 77.2 reduce-scatter.14
  855.6 74.6 reduce-scatter.16
